TPU v7x, 32 devices: a whole 2x2x4 slice. The times are simulated.
32 devices in a mesh: rep: 4 (over y, core), shard: 8 (over z, x).
Axes of the slice: x: 2, y: 2, z: 4, core: 2. Of those that a mesh axis runs over, the one named last changes fastest.
Arguments:
- block_input: bfloat16 [4096, 2048], P(('rep', 'shard')), may hold values from -6 to 6
- cotangent: bfloat16 [4096, 2048], P(('rep', 'shard')), may hold values from -6 to 6
- attn_gain: bfloat16 [2048], P('shard'), may hold values from 0.5 to 1.5
- query_weight: bfloat16 [2048, 2048], P('shard'), may hold values from -0.125 to 0.125
- key_weight: bfloat16 [2048, 256], P('shard'), may hold values from -0.125 to 0.125
- value_weight: bfloat16 [2048, 256], P('shard'), may hold values from -0.125 to 0.125
- out_weight: bfloat16 [2048, 2048], P('shard'), may hold values from -1 to 1
- mlp_gain: bfloat16 [2048], P('shard'), may hold values from 0.5 to 1.5
- gate_weight: bfloat16 [2048, 5632], P('shard'), may hold values from -0.125 to 0.125
- up_weight: bfloat16 [2048, 5632], P('shard'), may hold values from -0.125 to 0.125
- down_weight: bfloat16 [5632, 2048], P('shard'), may hold values from -0.078125 to 0.078125
Outputs:
- block_output: bfloat16 [4096, 2048], P(('rep', 'shard'))
- input_grad: float32 [4096, 2048], P(('rep', 'shard'))
- query_grad: float32 [2048, 2048], P('shard')
- key_grad: float32 [2048, 256], P('shard')
- value_grad: float32 [2048, 256], P('shard')
- out_grad: float32 [2048, 2048], P('shard')
- gate_grad: float32 [2048, 5632], P('shard')
- up_grad: float32 [2048, 5632], P('shard')
- down_grad: float32 [5632, 2048], P('shard')
- attn_gain_grad: float32 [2048], P('shard')
- mlp_gain_grad: float32 [2048], P('shard')
All inputs are finite; a program needn't handle non-finite values.
Results may differ from a plain program's by a relative error of at most 0.02.
Values may be sent and summed in bfloat16 or wider, within the bound.
A program may use at most 448 MiB of HBM per device.

v0:
```python
import math

import jax
import jax.numpy as jnp
from jax import lax
from jax.sharding import PartitionSpec as P

H = 32
KV = 4
HD = 64


epsilon = 1e-05


def rotary_tables(length, head_size):
    positions = jnp.arange(length, dtype=jnp.float32)[:, None]
    spacing = jnp.arange(head_size // 2, dtype=jnp.float32) * (-2.0 * math.log(10000.0) / head_size)
    angles = positions * jnp.exp(spacing)[None, :]
    cos_table = jnp.cos(angles)
    sin_table = jnp.sin(angles)
    return (
        jnp.concatenate([cos_table, cos_table], axis=-1),
        jnp.concatenate([sin_table, sin_table], axis=-1),
    )


def rotate_half(values):
    middle = values.shape[-1] // 2
    return jnp.concatenate([-values[..., middle:], values[..., :middle]], axis=-1)


def rotate_back(values):
    middle = values.shape[-1] // 2
    return jnp.concatenate([values[..., middle:], -values[..., :middle]], axis=-1)


def apply_rotary(values, cos_table, sin_table):
    return values * cos_table[:, None, :] + rotate_half(values) * sin_table[:, None, :]


def rotary_back(grads, cos_table, sin_table):
    return grads * cos_table[:, None, :] + rotate_back(grads * sin_table[:, None, :])


def norm_back(grad_normed, inputs, scale):
    return scale * grad_normed - inputs * (scale * scale * scale) * jnp.mean(
        grad_normed * inputs, axis=-1, keepdims=True
    )


def matmul(left, right):
    return jnp.dot(left, right, preferred_element_type=jnp.float32)


def contract_last(left, right):
    return lax.dot_general(
        left, right, (((1,), (1,)), ((), ())), preferred_element_type=jnp.float32
    )


def contract_first(left, right):
    return lax.dot_general(
        left, right, (((0,), (0,)), ((), ())), preferred_element_type=jnp.float32
    )


def input_fold(normed, pieces):
    gain_piece = pieces[0]
    block = (normed * gain_piece.astype(jnp.float32)[None, :]).astype(jnp.bfloat16)
    first = (gain_piece, block)
    rest = tuple((matmul(block, piece) for piece in pieces[1:]))
    return first + rest


def add_rows(left, piece):
    return matmul(left, piece)


def place_columns(rights, pieces):
    term = contract_last(rights[0], pieces[0])
    for right, piece in zip(rights[1:], pieces[1:]):
        term = term + contract_last(right, piece)
    return term


def place_single(right, piece):
    return place_columns((right,), (piece,))


def down_term(product, cotangent):
    return contract_first(product, cotangent)


def per_device(
    block_input,
    cotangent,
    attn_gain,
    query_weight,
    key_weight,
    value_weight,
    out_weight,
    mlp_gain,
    gate_weight,
    up_weight,
    down_weight,
):
    length = block_input.shape[0]
    groups = H // KV
    scale_factor = HD ** (-0.5)
    x_float = block_input.astype(jnp.float32)
    rms_one = lax.rsqrt(jnp.mean(x_float * x_float, axis=-1, keepdims=True) + epsilon)
    normed_one = x_float * rms_one
    attn_parts = input_fold(
        normed_one,
        (
            lax.all_gather(attn_gain, "shard", axis=0, tiled=True),
            lax.all_gather(query_weight, "shard", axis=0, tiled=True),
            lax.all_gather(key_weight, "shard", axis=0, tiled=True),
            lax.all_gather(value_weight, "shard", axis=0, tiled=True),
        ),
    )
    gain_one, hidden_one, query_raw, key_raw, value_raw = attn_parts
    cos_table, sin_table = rotary_tables(length, HD)
    query_rot = apply_rotary(query_raw.reshape(length, H, HD), cos_table, sin_table)
    query_rot = query_rot.astype(jnp.bfloat16).reshape(length, KV, groups, HD)
    key_rot = apply_rotary(key_raw.reshape(length, KV, HD), cos_table, sin_table).astype(
        jnp.bfloat16
    )
    value_rows = value_raw.reshape(length, KV, HD).astype(jnp.bfloat16)
    causal = jnp.arange(length)[:, None] >= jnp.arange(length)[None, :]
    scores = (
        jnp.einsum("ikgd,jkd->kgij", query_rot, key_rot, preferred_element_type=jnp.float32)
        * scale_factor
    )
    log_total = jnp.log(jnp.sum(jnp.where(causal, jnp.exp(scores), 0.0), axis=-1))
    weights_bf = jnp.where(causal, jnp.exp(scores - log_total[..., None]), 0.0).astype(jnp.bfloat16)
    attended = jnp.einsum(
        "kgij,jkd->ikgd", weights_bf, value_rows, preferred_element_type=jnp.float32
    )
    attended = attended.reshape(length, H * HD).astype(jnp.bfloat16)
    mixed_sum = x_float + add_rows(
        attended, lax.all_gather(out_weight, "shard", axis=0, tiled=True)
    )
    rms_two = lax.rsqrt(jnp.mean(mixed_sum * mixed_sum, axis=-1, keepdims=True) + epsilon)
    normed_two = mixed_sum * rms_two
    mlp_parts = input_fold(
        normed_two,
        (
            lax.all_gather(mlp_gain, "shard", axis=0, tiled=True),
            lax.all_gather(gate_weight, "shard", axis=0, tiled=True),
            lax.all_gather(up_weight, "shard", axis=0, tiled=True),
        ),
    )
    gain_two, hidden_two, gate_raw, up_raw = mlp_parts
    sigmoid = jax.nn.sigmoid(gate_raw)
    activated = gate_raw * sigmoid
    product = (activated * up_raw).astype(jnp.bfloat16)
    down_raw = add_rows(product, lax.all_gather(down_weight, "shard", axis=0, tiled=True))
    block_output = (mixed_sum + down_raw).astype(jnp.bfloat16)
    grad_product = place_single(cotangent, lax.all_gather(down_weight, "shard", axis=0, tiled=True))
    down_rows_grad = lax.psum_scatter(
        down_term(product, cotangent).astype(jnp.bfloat16), "shard", scatter_dimension=0, tiled=True
    )
    grad_gate = (grad_product * up_raw * sigmoid * (1.0 + gate_raw * (1.0 - sigmoid))).astype(
        jnp.bfloat16
    )
    grad_up = (grad_product * activated).astype(jnp.bfloat16)
    grad_hidden_two = place_columns(
        (grad_gate, grad_up),
        (
            lax.all_gather(gate_weight, "shard", axis=0, tiled=True),
            lax.all_gather(up_weight, "shard", axis=0, tiled=True),
        ),
    )
    gate_local = contract_first(hidden_two, grad_gate)
    up_local = contract_first(hidden_two, grad_up)
    mlp_gain_local = jnp.sum(grad_hidden_two * normed_two, axis=0)
    gate_rows_grad, up_rows_grad, mlp_gain_rows = (
        lax.psum_scatter(
            gate_local.astype(jnp.bfloat16), "shard", scatter_dimension=0, tiled=True
        ).astype(jnp.float32),
        lax.psum_scatter(
            up_local.astype(jnp.bfloat16), "shard", scatter_dimension=0, tiled=True
        ).astype(jnp.float32),
        lax.psum_scatter(
            mlp_gain_local.astype(jnp.bfloat16), "shard", scatter_dimension=0, tiled=True
        ).astype(jnp.float32),
    )
    grad_mixed = cotangent.astype(jnp.float32) + norm_back(
        grad_hidden_two * gain_two.astype(jnp.float32), mixed_sum, rms_two
    )
    grad_mixed_bf = grad_mixed.astype(jnp.bfloat16)
    grad_attended = place_single(
        grad_mixed_bf, lax.all_gather(out_weight, "shard", axis=0, tiled=True)
    )
    grad_attended = grad_attended.astype(jnp.bfloat16).reshape(length, KV, groups, HD)
    weights = jnp.where(causal, jnp.exp(scores - log_total[..., None]), 0.0)
    grad_weights = jnp.einsum(
        "ikgd,jkd->kgij", grad_attended, value_rows, preferred_element_type=jnp.float32
    )
    row_total = jnp.sum(weights * grad_weights, axis=-1, keepdims=True)
    grad_scores = (weights * (grad_weights - row_total) * scale_factor).astype(jnp.bfloat16)
    grad_query_rot = jnp.einsum(
        "kgij,jkd->ikgd", grad_scores, key_rot, preferred_element_type=jnp.float32
    ).reshape(length, H, HD)
    grad_key_rot = jnp.einsum(
        "kgij,ikgd->jkd", grad_scores, query_rot, preferred_element_type=jnp.float32
    )
    grad_value = jnp.einsum(
        "kgij,ikgd->jkd", weights_bf, grad_attended, preferred_element_type=jnp.float32
    )
    grad_query = (
        rotary_back(grad_query_rot, cos_table, sin_table)
        .astype(jnp.bfloat16)
        .reshape(length, H * HD)
    )
    grad_key = (
        rotary_back(grad_key_rot, cos_table, sin_table)
        .astype(jnp.bfloat16)
        .reshape(length, KV * HD)
    )
    grad_value_bf = grad_value.astype(jnp.bfloat16).reshape(length, KV * HD)
    grad_hidden_one = place_columns(
        (grad_query, grad_key, grad_value_bf),
        (
            lax.all_gather(query_weight, "shard", axis=0, tiled=True),
            lax.all_gather(key_weight, "shard", axis=0, tiled=True),
            lax.all_gather(value_weight, "shard", axis=0, tiled=True),
        ),
    )
    query_local = contract_first(hidden_one, grad_query)
    key_local = contract_first(hidden_one, grad_key)
    value_local = contract_first(hidden_one, grad_value_bf)
    out_local = contract_first(attended, grad_mixed_bf)
    attn_gain_local = jnp.sum(grad_hidden_one * normed_one, axis=0)
    query_rows_grad, key_rows_grad, value_rows_grad, out_rows_grad, attn_gain_rows = (
        lax.psum_scatter(
            query_local.astype(jnp.bfloat16), "shard", scatter_dimension=0, tiled=True
        ).astype(jnp.float32),
        lax.psum_scatter(
            key_local.astype(jnp.bfloat16), "shard", scatter_dimension=0, tiled=True
        ).astype(jnp.float32),
        lax.psum_scatter(
            value_local.astype(jnp.bfloat16), "shard", scatter_dimension=0, tiled=True
        ).astype(jnp.float32),
        lax.psum_scatter(
            out_local.astype(jnp.bfloat16), "shard", scatter_dimension=0, tiled=True
        ).astype(jnp.float32),
        lax.psum_scatter(
            attn_gain_local.astype(jnp.bfloat16), "shard", scatter_dimension=0, tiled=True
        ).astype(jnp.float32),
    )
    input_grad = grad_mixed + norm_back(
        grad_hidden_one * gain_one.astype(jnp.float32), x_float, rms_one
    )
    summed = (
        lax.psum(query_rows_grad.astype(jnp.bfloat16), "rep").astype(jnp.float32),
        lax.psum(key_rows_grad.astype(jnp.bfloat16), "rep").astype(jnp.float32),
        lax.psum(value_rows_grad.astype(jnp.bfloat16), "rep").astype(jnp.float32),
        lax.psum(out_rows_grad.astype(jnp.bfloat16), "rep").astype(jnp.float32),
        lax.psum(gate_rows_grad.astype(jnp.bfloat16), "rep").astype(jnp.float32),
        lax.psum(up_rows_grad.astype(jnp.bfloat16), "rep").astype(jnp.float32),
        lax.psum(down_rows_grad, "rep").astype(jnp.float32),
        lax.psum(attn_gain_rows.astype(jnp.bfloat16), "rep").astype(jnp.float32),
        lax.psum(mlp_gain_rows.astype(jnp.bfloat16), "rep").astype(jnp.float32),
    )
    return (block_output, input_grad) + tuple(summed)


def solution(mesh):
    in_specs = (
        P(("rep", "shard"), None),
        P(("rep", "shard"), None),
        P("shard"),
        P("shard", None),
        P("shard", None),
        P("shard", None),
        P("shard", None),
        P("shard"),
        P("shard", None),
        P("shard", None),
        P("shard", None),
    )
    out_specs = (
        P(("rep", "shard"), None),
        P(("rep", "shard"), None),
        P("shard", None),
        P("shard", None),
        P("shard", None),
        P("shard", None),
        P("shard", None),
        P("shard", None),
        P("shard", None),
        P("shard"),
        P("shard"),
    )
    return jax.shard_map(
        per_device, mesh=mesh, in_specs=in_specs, out_specs=out_specs, check_vma=False
    )
```

profile of v0, /device:TPU:1, one launch (start us, length us, event | category | flops | bytes accessed | tf_op | source)
XLA Modules:
  0.0 3509.5 jit_solution(452623784468544038)
XLA Ops:
  8.0 0.7 all-gather.12.cloned.1.call-update
  8.7 0.7 all-gather.14.cloned.1.call-update
  11.2 0.7 all-gather.22.cloned.1.call-update
  12.0 17.9 all-gather
  29.9 12.8 all-gather.1
  43.8 6.9 all-gather.10.cloned.1.call-done
  50.7 1.6 convolution_convert_fusion.9
  52.4 39.6 %all-gather.12.cloned.1.call-done = bf16[2048,256]{1,0:T(8,128)(2,1)} async-done(((bf16[256,256]{1,0:T(8,128)(2,1)}), bf16[2048,256]{1,0:T(8,128)(2,1)}) %all-gather.12.cloned.1.call-update) | async-done | bytes 1048592 | tf_op jit(solution)/shard_map/all_gather | solution.py:119
  91.9 1.8 fusion.72
  93.8 124.5 %all-gather.14.cloned.1.call-done = bf16[2048,2048]{1,0:T(8,128)(2,1)} async-done(((bf16[256,2048]{1,0:T(8,128)(2,1)}), bf16[2048,2048]{1,0:T(8,128)(2,1)}) %all-gather.14.cloned.1.call-update) | async-done | bytes 8388624 | tf_op jit(solution)/shard_map/all_gather | solution.py:118
  218.3 6.8 fusion.70
  225.5 1.8 fusion.77
  227.3 3.6 convolution_convert_fusion.8
  230.8 112.1 %all-gather.16.cloned.1.call-done = bf16[2048,2048]{1,0:T(8,128)(2,1)} async-done(((bf16[256,2048]{1,0:T(8,128)(2,1)}), bf16[2048,2048]{1,0:T(8,128)(2,1)}) %all-gather.16.cloned.1.call-update) | async-done | bytes 8388624 | tf_op jit(solution)/shard_map/all_gather | solution.py:143
  343.0 4.7 multiply_reduce_fusion.2
  347.7 2.4 fusion.5
  350.3 433.8 %all-gather.18.cloned.1.call-done = bf16[2048,5632]{1,0:T(8,128)(2,1)} async-done(((bf16[256,5632]{1,0:T(8,128)(2,1)}), bf16[2048,5632]{1,0:T(8,128)(2,1)}) %all-gather.18.cloned.1.call-update) | async-done | bytes 23068688 | tf_op jit(solution)/shard_map/all_gather | solution.py:151
  784.1 12.3 fusion.78
  796.5 430.1 %all-gather.20.cloned.1.call-done = bf16[2048,5632]{1,0:T(8,128)(2,1)} async-done(((bf16[256,5632]{1,0:T(8,128)(2,1)}), bf16[2048,5632]{1,0:T(8,128)(2,1)}) %all-gather.20.cloned.1.call-update) | async-done | bytes 23068688 | tf_op jit(solution)/shard_map/all_gather | solution.py:152
  1226.6 12.7 fusion.79
  1239.3 429.9 %all-gather.22.cloned.1.call-done = bf16[5632,2048]{1,0:T(8,128)(2,1)} async-done(((bf16[704,2048]{1,0:T(8,128)(2,1)}), bf16[5632,2048]{1,0:T(8,128)(2,1)}) %all-gather.22.cloned.1.call-update) | async-done | bytes 23068688 | tf_op jit(solution)/shard_map/all_gather | solution.py:159
  1669.2 14.8 multiply_convert_fusion
  1684.0 12.2 fusion.80
  1696.3 13.1 multiply_reduce_fusion
  1709.4 1.7 subtract_add_fusion
  1711.1 7.1 convolution_convert_fusion.7
  1718.2 2.0 copy.50
  1720.2 2.8 fusion.81
  1723.1 4.9 broadcast_multiply_fusion
  1728.0 0.9 fusion.49
  1728.9 1.5 convolution_convert_fusion.6
  1730.5 3.3 fusion.16
  1733.8 1.5 convolution_convert_fusion.5
  1735.6 5.2 fusion.32
  1740.8 1.3 bitcast_multiply_fusion.1
  1742.3 1.0 copy-done.6
  1743.5 0.8 copy-done.4
  1744.3 5.8 convolution_convert_fusion.4
  1750.1 6.6 convolution_convert_fusion.3
  1756.8 12.2 convolution_convert_fusion.2
  1769.1 12.2 convolution_convert_fusion.1
  1781.6 0.8 copy-done.11
  1782.3 12.3 convolution_convert_fusion
  1794.7 65.5 %reduce-scatter.12.cloned.1.call-done = bf16[256,256]{1,0:T(8,128)(2,1)} async-done(((bf16[2048,256]{1,0:T(8,128)(2,1)}), bf16[256,256]{1,0:T(8,128)(2,1)}) %reduce-scatter.12.cloned.1.call-update) | async-done | bytes 131088 | tf_op jit(solution)/shard_map/reduce_scatter | solution.py:244
  1860.2 151.4 %reduce-scatter.8.cloned.1.call-done = bf16[256,2048]{1,0:T(8,128)(2,1)} async-done(((bf16[2048,2048]{1,0:T(8,128)(2,1)}), bf16[256,2048]{1,0:T(8,128)(2,1)}) %reduce-scatter.8.cloned.1.call-update) | async-done | bytes 1048592 | tf_op jit(solution)/shard_map/reduce_scatter | solution.py:238
  2011.6 150.2 %reduce-scatter.14.cloned.1.call-done = bf16[256,2048]{1,0:T(8,128)(2,1)} async-done(((bf16[2048,2048]{1,0:T(8,128)(2,1)}), bf16[256,2048]{1,0:T(8,128)(2,1)}) %reduce-scatter.14.cloned.1.call-update) | async-done | bytes 1048592 | tf_op jit(solution)/shard_map/reduce_scatter | solution.py:247
  2161.8 376.0 %reduce-scatter.16.cloned.1.call-done = bf16[256,5632]{1,0:T(8,128)(2,1)} async-done(((bf16[2048,5632]{1,0:T(8,128)(2,1)}), bf16[256,5632]{1,0:T(8,128)(2,1)}) %reduce-scatter.16.cloned.1.call-update) | async-done | bytes 2883600 | tf_op jit(solution)/shard_map/reduce_scatter | solution.py:180
  2537.8 376.0 %reduce-scatter.18.cloned.1.call-done = bf16[256,5632]{1,0:T(8,128)(2,1)} async-done(((bf16[2048,5632]{1,0:T(8,128)(2,1)}), bf16[256,5632]{1,0:T(8,128)(2,1)}) %reduce-scatter.18.cloned.1.call-update) | async-done | bytes 2883600 | tf_op jit(solution)/shard_map/reduce_scatter | solution.py:183
  2913.8 375.8 %reduce-scatter.20.cloned.1.call-done = bf16[704,2048]{1,0:T(8,128)(2,1)} async-done(((bf16[5632,2048]{1,0:T(8,128)(2,1)}), bf16[704,2048]{1,0:T(8,128)(2,1)}) %reduce-scatter.20.cloned.1.call-update) | async-done | bytes 2883600 | tf_op jit(solution)/shard_map/reduce_scatter | solution.py:162
  3291.5 6.4 fusion.82
  3298.4 0.9 copy-done.13
  3299.3 1.5 fusion.18
  3300.9 16.1 all-reduce.2
  3317.1 9.4 all-reduce.3
  3327.7 2.7 fusion.22
  3330.4 12.3 fusion.3
  3342.6 144.4 %all-reduce.7.cloned.1.call-done = (bf16[256,2048]{1,0:T(8,128)(2,1)}, bf16[256,256]{1,0:T(8,128)(2,1)}, bf16[256,256]{1,0:T(8,128)(2,1)}, bf16[256,2048]{1,0:T(...) async-done(((bf16[256,2048]{1,0:T(8,128)(2,1)}, bf16[256,256]{1,0:T(8,128)(2,1)}, bf16[256,256]{1,0:T(8,128)(2,1)}, ...) | async-done | bytes 11010064 | tf_op jit(solution)/shard_map/psum | solution.py:258
  3487.0 2.9 convert_element_type.175
  3489.9 0.7 convert_element_type.177
  3490.6 0.7 convert_element_type.179
  3491.3 1.6 convert_element_type.181
  3492.9 3.2 convert_element_type.183
  3496.1 3.2 convert_element_type.185
  3499.3 3.3 convert_element_type.187
  (99 shorter events, 8.4 us)
Async XLA Ops:
  7.2 43.5 %all-gather.10.cloned.1.call-start = ((), (), s32[]{:S(2)}) async-start(), calls=%async_computation.7 | async-start | bytes 1179648 | tf_op jit(solution)/shard_map/all_gather | solution.py:120
  7.9 84.0 %all-gather.12.cloned.1.call-start = ((), (), s32[]{:S(2)}) async-start(), calls=%async_computation.8 | async-start | bytes 1179648 | tf_op jit(solution)/shard_map/all_gather | solution.py:119
  8.7 209.6 %all-gather.14.cloned.1.call-start = ((), (), s32[]{:S(2)}) async-start(), calls=%async_computation.9 | async-start | bytes 9437184 | tf_op jit(solution)/shard_map/all_gather | solution.py:118
  9.4 333.6 %all-gather.16.cloned.1.call-start = ((), (), s32[]{:S(2)}) async-start(), calls=%async_computation.10 | async-start | bytes 9437184 | tf_op jit(solution)/shard_map/all_gather | solution.py:143
  10.0 774.2 %all-gather.18.cloned.1.call-start = ((), (), s32[]{:S(2)}) async-start(), calls=%async_computation.11 | async-start | bytes 25952256 | tf_op jit(solution)/shard_map/all_gather | solution.py:151
  10.6 1216.0 %all-gather.20.cloned.1.call-start = ((), (), s32[]{:S(2)}) async-start(), calls=%async_computation.12 | async-start | bytes 25952256 | tf_op jit(solution)/shard_map/all_gather | solution.py:152
  11.1 0.8 copy-start.20
  11.1 18.7 copy-start.21
  11.2 31.8 copy-start
  11.2 1658.0 %all-gather.22.cloned.1.call-start = ((), (), s32[]{:S(2)}) async-start(), calls=%async_computation.13 | async-start | bytes 25952256 | tf_op jit(solution)/shard_map/all_gather | solution.py:159
  11.9 1782.8 %reduce-scatter.10.cloned.1.call-start = ((), (), s32[]{:S(2)}) async-start(), calls=%async_computation.15 | async-start | bytes 1179648 | tf_op jit(solution)/shard_map/reduce_scatter | solution.py:241
  42.8 304.9 %copy-start.18 = (pred[128,128]{0,1:T(8,128)(4,1)}, pred[128,128]{0,1:T(8,128)(4,1)S(1)}, u32[]{:S(2)}) copy-start(pred[128,128]{0,1:T(8,128)(4,1)S(1)} %iota_compare_fusion) | copy-start | bytes 49156
  225.4 122.3 %copy-start.12 = (bf16[128,4,8,64]{0,3,2,1:T(8,128)(2,1)}, bf16[128,4,8,64]{0,3,2,1:T(8,128)(2,1)S(1)}, u32[]{:S(2)}) copy-start(bf16[128,4,8,64]{0,3,2,1:T(8,128)(2,1)S(1)} %fusion.25) | copy-start | bytes 1572868
  230.8 116.9 %copy-start.3 = (bf16[4,64,8,128]{3,1,2,0:T(8,128)(2,1)}, bf16[4,64,8,128]{3,1,2,0:T(8,128)(2,1)S(1)}, u32[]{:S(2)}) copy-start(bf16[4,64,8,128]{3,1,2,0:T(8,128)(2,1)S(1)} %convolution_convert_fusion.8) | copy-start | bytes 1572868
  796.5 872.7 %copy-start.10 = (bf16[128,2048]{1,0:T(8,128)(2,1)S(1)}, bf16[128,2048]{1,0:T(8,128)(2,1)}, u32[]{:S(2)}) copy-start(bf16[128,2048]{1,0:T(8,128)(2,1)} %param.12) | copy-start | bytes 1572868
  1684.0 12.3 copy-start.1
  1730.5 129.8 %reduce-scatter.12.cloned.1.call-start = ((), (), s32[]{:S(2)}) async-start(), calls=%async_computation.16 | async-start | bytes 1179648 | tf_op jit(solution)/shard_map/reduce_scatter | solution.py:244
  1735.4 276.2 %reduce-scatter.8.cloned.1.call-start = ((), (), s32[]{:S(2)}) async-start(), calls=%async_computation.14 | async-start | bytes 9437184 | tf_op jit(solution)/shard_map/reduce_scatter | solution.py:238
  1742.1 1.2 copy-start.6
  1743.5 0.8 copy-start.4
  1750.1 411.7 %reduce-scatter.14.cloned.1.call-start = ((), (), s32[]{:S(2)}) async-start(), calls=%async_computation.17 | async-start | bytes 9437184 | tf_op jit(solution)/shard_map/reduce_scatter | solution.py:247
  1756.8 781.0 %reduce-scatter.16.cloned.1.call-start = ((), (), s32[]{:S(2)}) async-start(), calls=%async_computation.18 | async-start | bytes 25952256 | tf_op jit(solution)/shard_map/reduce_scatter | solution.py:180
  1769.0 1144.7 %reduce-scatter.18.cloned.1.call-start = ((), (), s32[]{:S(2)}) async-start(), calls=%async_computation.19 | async-start | bytes 25952256 | tf_op jit(solution)/shard_map/reduce_scatter | solution.py:183
  1781.3 1.0 copy-start.11
  1781.3 1508.3 %reduce-scatter.20.cloned.1.call-start = ((), (), s32[]{:S(2)}) async-start(), calls=%async_computation.20 | async-start | bytes 25952256 | tf_op jit(solution)/shard_map/reduce_scatter | solution.py:162
  1794.6 1692.4 %all-reduce.7.cloned.1.call-start = ((), (), s32[]{:S(2)}) async-start(), calls=%async_computation.21 | async-start | bytes 22020096 | tf_op jit(solution)/shard_map/psum | solution.py:258
  3289.6 0.7 copy-start.22
  3289.6 1.9 copy-start.5
  3291.5 6.4 copy-start.14
  3297.9 1.4 copy-start.13
  3299.3 28.4 copy-start.19
  3326.5 3.8 copy-start.2
  3487.0 2.9 copy-start.17
  3487.0 3.6 copy-start.16
  3487.0 4.3 copy-start.15
  3489.9 3.0 copy-start.9
  3492.9 3.2 copy-start.8
  3496.1 3.2 copy-start.7
Sparse Core Ops, SparseCore 0:
  10.1 40.5 all-gather.9
  52.8 39.0 all-gather.11
  94.1 124.1 all-gather.13
  220.3 122.6 all-gather.15
  344.3 439.7 all-gather.17
  785.5 441.0 all-gather.19
  1228.1 441.0 all-gather.21
  1730.6 62.4 reduce-scatter.9
  1797.1 63.0 reduce-scatter.11
  1863.7 147.8 reduce-scatter.7
  2015.2 146.5 reduce-scatter.13
  2165.6 372.2 reduce-scatter.15
  2541.7 372.0 reduce-scatter.17
  2917.5 372.0 reduce-scatter.19
  3292.7 194.2 all-reduce.6
where the time goes:
time: 3520 us; the launch traced here: 3510 us
  waiting for transfers between devices  3220 us (91%)
  matrix products  184 us (5%)
  blocking collectives  56.2 us (2%)
    all_gather x1, waiting for transfers between devices, per_device(): lax.all_gather(gate_weight, 'shard', axis=0, tiled=True)  434 us
    all_gather x1, waiting for transfers between devices, per_device(): lax.all_gather(up_weight, 'shard', axis=0, tiled=True)  430 us
    all_gather x1, waiting for transfers between devices, per_device(): lax.all_gather(down_weight, 'shard', axis=0, tiled=True)  430 us
    reduce_scatter x1, waiting for transfers between devices, per_device(): lax.psum_scatter(gate_local.astype(jnp.bfloat16), 'shard', scatter_dimens...  376 us
    reduce_scatter x1, waiting for transfers between devices, per_device(): lax.psum_scatter(up_local.astype(jnp.bfloat16), 'shard', scatter_dimensio...  376 us
    reduce_scatter x1, waiting for transfers between devices, per_device(): lax.psum_scatter(down_term(product, cotangent).astype(jnp.bfloat16), 'sha...  376 us
    reduce_scatter x1, waiting for transfers between devices, per_device(): lax.psum_scatter(query_local.astype(jnp.bfloat16), 'shard', scatter_dimen...  151 us
    reduce_scatter x1, waiting for transfers between devices, per_device(): lax.psum_scatter(out_local.astype(jnp.bfloat16), 'shard', scatter_dimensi...  150 us
  transfers between devices with their start and end apart: 15, of which 14 were waited for; matrix products, arithmetic and copies ran while one was open for 4% of the time, Pallas kernels for 0%

commit v1 on v0

v1 whole, which is shorter than its diff:
```python
import math

import jax
import jax.numpy as jnp
from jax import lax
from jax.sharding import Mesh, PartitionSpec as P

KV = 4
HD = 64
X = 2
epsilon = 1e-05

TP = ("rep", "x")


def rotary_tables(length, head_size):
    positions = jnp.arange(length, dtype=jnp.float32)[:, None]
    spacing = jnp.arange(head_size // 2, dtype=jnp.float32) * (-2.0 * math.log(10000.0) / head_size)
    angles = positions * jnp.exp(spacing)[None, :]
    cos_table = jnp.cos(angles)
    sin_table = jnp.sin(angles)
    return (
        jnp.concatenate([cos_table, cos_table], axis=-1),
        jnp.concatenate([sin_table, sin_table], axis=-1),
    )


def rotate_half(values):
    middle = values.shape[-1] // 2
    return jnp.concatenate([-values[..., middle:], values[..., :middle]], axis=-1)


def rotate_back(values):
    middle = values.shape[-1] // 2
    return jnp.concatenate([values[..., middle:], -values[..., :middle]], axis=-1)


def norm_back(grad_normed, inputs, scale):
    return scale * grad_normed - inputs * (scale * scale * scale) * jnp.mean(
        grad_normed * inputs, axis=-1, keepdims=True
    )


def matmul(left, right):
    return jnp.dot(left, right, preferred_element_type=jnp.float32)


def contract_last(left, right):
    return lax.dot_general(
        left, right, (((1,), (1,)), ((), ())), preferred_element_type=jnp.float32
    )


def contract_first(left, right):
    return lax.dot_general(
        left, right, (((0,), (0,)), ((), ())), preferred_element_type=jnp.float32
    )


def gather_tokens(rows):
    return lax.all_gather(rows, TP, axis=0, tiled=True)


def scatter_tokens(partial):
    return lax.psum_scatter(
        partial.astype(jnp.bfloat16), TP, scatter_dimension=0, tiled=True
    ).astype(jnp.float32)


def swap_x(pieces):
    x = lax.axis_index("x")
    away = jnp.where(x == 0, pieces[1], pieces[0])
    own = jnp.where(x == 0, pieces[0], pieces[1])
    came = lax.ppermute(away, "x", [(0, 1), (1, 0)])
    return jnp.stack([jnp.where(x == 0, own, came), jnp.where(x == 0, came, own)])


def per_device(
    block_input,
    cotangent,
    attn_gain,
    query_weight,
    key_weight,
    value_weight,
    out_weight,
    mlp_gain,
    gate_weight,
    up_weight,
    down_weight,
):
    length, width = block_input.shape
    reps, zs = lax.axis_size("rep"), lax.axis_size("z")
    group = reps * X
    r = lax.axis_index("rep")
    z = lax.axis_index("z")
    x = lax.axis_index("x")
    rows = query_weight.shape[0]
    heads_wide = query_weight.shape[1] // group
    per_kv = zs // KV
    hidden_piece = down_weight.shape[0] // reps
    hidden_wide = zs * hidden_piece
    heads = heads_wide // HD
    scale_factor = HD ** (-0.5)

    def own_rep(values, axis):
        return lax.dynamic_index_in_dim(values, r, axis, keepdims=False)

    def query_columns(weight):
        pieces = own_rep(weight.reshape(rows, KV, per_kv, X, -1), 1)
        return jnp.moveaxis(pieces, 2, 0).reshape(X, rows, heads_wide)

    def hidden_columns(weight):
        pieces = own_rep(weight.reshape(rows, zs, X, reps, hidden_piece), 3)
        return jnp.moveaxis(pieces, 2, 0).reshape(X, rows, hidden_wide)

    def key_columns(weight):
        piece = own_rep(weight.reshape(rows, KV, HD), 1)
        return jnp.broadcast_to(piece[None], (X, rows, HD))

    attn_pack = jnp.concatenate(
        [query_columns(query_weight), key_columns(key_weight), key_columns(value_weight)], axis=2
    )
    mlp_pack = jnp.concatenate([hidden_columns(gate_weight), hidden_columns(up_weight)], axis=2)

    gains = lax.all_gather(jnp.stack([attn_gain, mlp_gain]), ("z", "x"), axis=1, tiled=True)
    gains = gains.astype(jnp.float32)
    gain_one, gain_two = gains[0], gains[1]
    attn_w = lax.all_gather(swap_x(attn_pack), "z", axis=0).reshape(width, -1)
    out_all = lax.all_gather(out_weight, "z", axis=0)
    out_w = own_rep(out_all.reshape(KV, per_kv * rows, width), 0)
    mlp_w = lax.all_gather(swap_x(mlp_pack), "z", axis=0).reshape(width, -1)
    down_w = lax.all_gather(
        own_rep(down_weight.reshape(reps, hidden_piece, width), 0), "z", axis=0
    ).reshape(hidden_wide, width)

    x_float = block_input.astype(jnp.float32)
    rms_one = lax.rsqrt(jnp.mean(x_float * x_float, axis=-1, keepdims=True) + epsilon)
    normed_one = x_float * rms_one
    hidden_one = gather_tokens((normed_one * gain_one[None, :]).astype(jnp.bfloat16))
    cot_all = gather_tokens(cotangent)
    raw = matmul(hidden_one, attn_w).reshape(group, length, -1)
    cos_table, sin_table = rotary_tables(length, HD)

    def rotary(values):
        return (
            values * cos_table[:, None, :] + rotate_half(values) * sin_table[:, None, :]
        ).astype(jnp.bfloat16)

    def rotary_back(grads):
        return (
            grads * cos_table[:, None, :] + rotate_back(grads * sin_table[:, None, :])
        ).astype(jnp.bfloat16)

    query_rot = rotary(raw[..., :heads_wide].reshape(group, length, heads, HD))
    key_rot = rotary(raw[..., None, heads_wide : heads_wide + HD])[:, :, 0]
    value_rows = raw[..., heads_wide + HD :].astype(jnp.bfloat16)
    causal = jnp.arange(length)[:, None] >= jnp.arange(length)[None, :]

    def product_of(spec, left, right):
        return jnp.einsum(spec, left, right, preferred_element_type=jnp.float32)

    scores = product_of("bigd,bjd->bgij", query_rot, key_rot) * scale_factor
    log_total = jnp.log(jnp.sum(jnp.where(causal, jnp.exp(scores), 0.0), axis=-1))
    weights = jnp.where(causal, jnp.exp(scores - log_total[..., None]), 0.0)
    weights_bf = weights.astype(jnp.bfloat16)
    attended = product_of("bgij,bjd->bigd", weights_bf, value_rows)
    attended = attended.astype(jnp.bfloat16).reshape(group * length, heads_wide)
    mixed_sum = x_float + scatter_tokens(matmul(attended, out_w))

    rms_two = lax.rsqrt(jnp.mean(mixed_sum * mixed_sum, axis=-1, keepdims=True) + epsilon)
    normed_two = mixed_sum * rms_two
    hidden_two = gather_tokens((normed_two * gain_two[None, :]).astype(jnp.bfloat16))
    gate_up = matmul(hidden_two, mlp_w)
    gate_raw, up_raw = gate_up[:, :hidden_wide], gate_up[:, hidden_wide:]
    sigmoid = jax.nn.sigmoid(gate_raw)
    activated = gate_raw * sigmoid
    product = (activated * up_raw).astype(jnp.bfloat16)
    grad_product = contract_last(cot_all, down_w)
    grad_gate = grad_product * up_raw * sigmoid * (1.0 + gate_raw * (1.0 - sigmoid))
    grad_up = grad_product * activated
    grad_both = jnp.concatenate([grad_gate, grad_up], axis=1).astype(jnp.bfloat16)
    grad_hidden_two = scatter_tokens(contract_last(grad_both, mlp_w))
    block_output = (mixed_sum + scatter_tokens(matmul(product, down_w))).astype(jnp.bfloat16)
    down_local = contract_first(product, cot_all).astype(jnp.bfloat16)
    mlp_local = contract_first(hidden_two, grad_both).astype(jnp.bfloat16)

    grad_mixed = cotangent.astype(jnp.float32) + norm_back(
        grad_hidden_two * gain_two[None, :], mixed_sum, rms_two
    )

    grad_mixed_bf = gather_tokens(grad_mixed.astype(jnp.bfloat16))
    grad_attended = contract_last(grad_mixed_bf, out_w).astype(jnp.bfloat16)
    out_local = contract_first(attended, grad_mixed_bf).astype(jnp.bfloat16)
    grad_attended = grad_attended.reshape(group, length, heads, HD)
    grad_weights = product_of("bigd,bjd->bgij", grad_attended, value_rows)
    row_total = jnp.sum(weights * grad_weights, axis=-1, keepdims=True)
    grad_scores = (weights * (grad_weights - row_total) * scale_factor).astype(jnp.bfloat16)
    grad_query = rotary_back(product_of("bgij,bjd->bigd", grad_scores, key_rot))
    grad_key = rotary_back(product_of("bgij,bigd->bjd", grad_scores, query_rot)[:, :, None])
    grad_value = product_of("bgij,bigd->bjd", weights_bf, grad_attended).astype(jnp.bfloat16)
    grad_attn = jnp.concatenate(
        [
            grad_query.reshape(group * length, heads_wide),
            grad_key.reshape(group * length, HD),
            grad_value.reshape(group * length, HD),
        ],
        axis=1,
    )
    grad_hidden_one = scatter_tokens(contract_last(grad_attn, attn_w))
    attn_local = contract_first(hidden_one, grad_attn).astype(jnp.bfloat16)
    input_grad = grad_mixed + norm_back(
        grad_hidden_one * gain_one[None, :], x_float, rms_one
    )

    def scatter_z(partial):
        return lax.psum_scatter(partial, "z", scatter_dimension=0, tiled=True)

    def to_owner(partial):
        pieces = swap_x(scatter_z(partial).reshape(X, rows, -1))
        return lax.all_gather(pieces, "rep", axis=0).astype(jnp.float32)

    down_grad = lax.all_gather(scatter_z(down_local), "rep", axis=0, tiled=True).astype(jnp.float32)
    mlp_grad = to_owner(mlp_local).reshape(reps, X, rows, 2, zs, hidden_piece)
    mlp_grad = mlp_grad.transpose(3, 2, 4, 1, 0, 5).reshape(2, rows, -1)
    out_padded = jnp.where(
        (jnp.arange(KV) == r)[:, None, None],
        out_local.reshape(1, per_kv * rows, width),
        jnp.zeros((), jnp.bfloat16),
    )
    out_grad = lax.psum(scatter_z(out_padded.reshape(zs * rows, width)), "rep").astype(jnp.float32)
    attn_grad = to_owner(attn_local)
    query_grad = attn_grad[..., :heads_wide].reshape(KV, X, rows, per_kv, -1)
    query_grad = query_grad.transpose(2, 0, 3, 1, 4).reshape(rows, -1)
    key_value = jnp.sum(attn_grad[..., heads_wide:], axis=1)
    key_grad = key_value[..., :HD].transpose(1, 0, 2).reshape(rows, -1)
    value_grad = key_value[..., HD:].transpose(1, 0, 2).reshape(rows, -1)
    gain_grads = lax.psum(
        jnp.stack(
            [
                jnp.sum(grad_hidden_one * normed_one, axis=0),
                jnp.sum(grad_hidden_two * normed_two, axis=0),
            ]
        ),
        ("rep", "z", "x"),
    )
    gain_grads = lax.dynamic_slice_in_dim(gain_grads, (z * X + x) * rows, rows, axis=1)
    return (
        block_output,
        input_grad,
        query_grad,
        key_grad,
        value_grad,
        out_grad,
        mlp_grad[0],
        mlp_grad[1],
        down_grad,
        gain_grads[0],
        gain_grads[1],
    )


def solution(mesh):
    reps, shards = mesh.shape["rep"], mesh.shape["shard"]
    cube = Mesh(mesh.devices.reshape(reps, shards // X, X), ("rep", "z", "x"))
    tokens = P(("rep", "z", "x"), None)
    matrix = P(("z", "x"), None)
    vector = P(("z", "x"))
    in_specs = (tokens, tokens, vector) + (matrix,) * 4 + (vector,) + (matrix,) * 3
    out_specs = (tokens, tokens) + (matrix,) * 7 + (vector,) * 2
    return jax.shard_map(
        per_device, mesh=cube, in_specs=in_specs, out_specs=out_specs, check_vma=False
    )
```

time: 3520 us -> 1150 us (0.33)
  waiting for transfers between devices: 3220 us -> 807 us
  local copies, waits for them, and re-layouts: 7.09 us -> 94.8 us
  matrix products: 184 us -> 100 us
    reduce_scatter x7 -> x8, waiting for transfers between devices: 1490 us -> 310 us  [the longest x4 193 us: scatter_z(): return lax.psum_scatter(partial, 'z', scatter_dimension=0, tiled=True)]
    all_gather x7 -> x11, waiting for transfers between devices: 1580 us -> 434 us  [the longest x4 145 us: gather_tokens(): return lax.all_gather(rows, TP, axis=0, tiled=True)]
    psum x1, waiting for transfers between devices: 144 us -> 10.1 us  [per_device(): lax.psum(scatter_z(out_padded.reshape(zs * rows, width)), 'rep')]
    ppermute x0 -> x4, waiting for transfers between devices: none -> 51.8 us  [swap_x(): came = lax.ppermute(away, 'x', [(0, 1), (1, 0)])]
  transfers between devices with their start and end apart: 15 -> 24, of which waited for: 14 -> 24; matrix products, arithmetic and copies ran while one was open for 4% -> 18% of each run, Pallas kernels for 0% -> 0%
where the time goes in v1:
time: 1150 us; the launch traced here: 1140 us
  waiting for transfers between devices  807 us (70%)
  matrix products  100 us (9%)
  local copies, waits for them, and re-layouts  94.8 us (8%)
  blocking collectives  57 us (5%)
  other arithmetic  55.7 us (5%)
  between operations  15.4 us (1%)
    reduce_scatter x4, waiting for transfers between devices, scatter_z(): return lax.psum_scatter(partial, 'z', scatter_dimension=0, tiled=True)  193 us
    all_gather x4, waiting for transfers between devices, gather_tokens(): return lax.all_gather(rows, TP, axis=0, tiled=True)  145 us
    reduce_scatter x4, waiting for transfers between devices, scatter_tokens(): lax.psum_scatter(partial.astype(jnp.bfloat16), TP, scatter_dimension=0, t...  117 us
    all_gather x1, waiting for transfers between devices, per_device(): mlp_w = lax.all_gather(swap_x(mlp_pack), 'z', axis=0).reshape(width, -1)  102 us
    all_gather x1, waiting for transfers between devices, per_device(): out_all = lax.all_gather(out_weight, 'z', axis=0)  60.1 us
    all_gather x2, waiting for transfers between devices, to_owner(): return lax.all_gather(pieces, 'rep', axis=0).astype(jnp.float32)  59.3 us
    ppermute x4, waiting for transfers between devices, swap_x(): came = lax.ppermute(away, 'x', [(0, 1), (1, 0)])  51.8 us
    all_gather x1, waiting for transfers between devices, per_device(): lax.all_gather(own_rep(down_weight.reshape(reps, hidden_piece, width), 0)...  49 us
  transfers between devices with their start and end apart: 24, of which 24 were waited for; matrix products, arithmetic and copies ran while one was open for 18% of the time, Pallas kernels for 0%

profile of v1, /device:TPU:1, one launch (start us, length us, event | category | flops | bytes accessed | tf_op | source)
XLA Modules:
  0.0 1138.1 jit_solution(16875060193501791917)
XLA Ops:
  9.7 2.6 reshape.197
  15.8 4.6 collective-permute-done
  21.4 17.2 %all_gather.52 = bf16[2,2048]{1,0:T(2,128)(2,1)S(1)} all-gather(bf16[2,256]{1,0:T(2,128)(2,1)S(1)} %pad_maximum_fusion.15), channel_id=1, replica_groups=mesh['rep'=4,'z'=4,'x'=2] {'z','x'}, dimensions={1}, use_global_device_ids=true | all-gather | bytes 9216 | tf_op jit(solution)/shard_map/all_gather | solution.py:125
  44.0 15.6 %all-gather.29.cloned.1.call-done = bf16[8,256,384]{2,1,0:T(8,128)(2,1)} async-done(((bf16[2,256,384]{2,1,0:T(8,128)(2,1)}), bf16[8,256,384]{2,1,0:T(8,128)(2,1)}) %all-gather.29.cloned.1.call-update) | async-done | bytes 1572880 | tf_op jit(solution)/shard_map/all_gather | solution.py:128
  59.6 39.3 %all-gather.17.cloned.1.call-done = bf16[1024,2048]{1,0:T(8,128)(2,1)} async-done(((bf16[128,2048]{1,0:T(8,128)(2,1)}), bf16[1024,2048]{1,0:T(8,128)(2,1)}) %all-gather.17.cloned.1.call-update) | async-done | bytes 4194320 | tf_op jit(solution)/shard_map/all_gather | solution.py:61
  98.9 5.0 fusion.88
  106.1 2.6 copy.129
  113.4 3.7 fusion.8
  117.1 2.3 fusion.21
  120.6 60.1 %all-gather.31.cloned.1.call-done = bf16[1024,2048]{1,0:T(8,128)(2,1)} async-done(((bf16[256,2048]{1,0:T(8,128)(2,1)}), bf16[1024,2048]{1,0:T(8,128)(2,1)}) %all-gather.31.cloned.1.call-update) | async-done | bytes 4194320 | tf_op jit(solution)/shard_map/all_gather | solution.py:129
  180.7 4.7 convolution_convert_fusion.4
  185.5 4.5 copy.138
  190.0 4.6 copy.136
  194.6 2.4 dynamic-slice_bitcast_fusion
  198.0 2.3 copy.141
  202.3 2.3 copy.140
  207.8 27.1 %collective-permute-done.1 = bf16[256,1408]{1,0:T(8,128)(2,1)S(1)} collective-permute-done((bf16[256,1408]{1,0:T(8,128)(2,1)S(1)}, bf16[256,1408]{1,0:T(8,128)(2,1)S(1)}, u32[]{:S(2)}, u32[]{:S(2)}) %collective-permute-start.1) | collective-permute-done | bytes 720928 | tf_op jit(solution)/shard_map/ppermute | solution.py:74
  236.8 9.8 reduce-scatter.9.cloned.1.call-done
  253.3 102.2 %all-gather.33.cloned.1.call-done = bf16[8,256,1408]{2,1,0:T(8,128)(2,1)} async-done(((bf16[2,256,1408]{2,1,0:T(8,128)(2,1)}), bf16[8,256,1408]{2,1,0:T(8,128)(2,1)}) %all-gather.33.cloned.1.call-update) | async-done | bytes 5767184 | tf_op jit(solution)/shard_map/all_gather | solution.py:131
  355.5 37.5 %all-gather.19.cloned.1.call-done = bf16[1024,2048]{1,0:T(8,128)(2,1)} async-done(((bf16[128,2048]{1,0:T(8,128)(2,1)}), bf16[1024,2048]{1,0:T(8,128)(2,1)}) %all-gather.19.cloned.1.call-update) | async-done | bytes 4194320 | tf_op jit(solution)/shard_map/all_gather | solution.py:61
  393.0 11.7 %fusion.89 = f32[1024,1408]{1,0:T(8,128)} fusion(bf16[1024,2048]{1,0:T(8,128)(2,1)} %all-gather.19.cloned.1.call-done, bf16[2048,1408]{1,0:T(8,128)(2,1)} %bitcast.267), kind=kOutput, calls=%fused_computation.187 | convolution fusion | flops 5905580032 | bytes 15728640 | tf_op jit(solution)/shard_map/dot_general | solution.py:45
  404.7 49.0 %all-gather.21.cloned.1.call-done = bf16[4,176,2048]{2,1,0:T(8,128)(2,1)} async-done(((bf16[1,176,2048]{2,1,0:T(8,128)(2,1)}), bf16[4,176,2048]{2,1,0:T(8,128)(2,1)}) %all-gather.21.cloned.1.call-update) | async-done | bytes 2883600 | tf_op jit(solution)/shard_map/all_gather | solution.py:132
  453.7 37.8 %all-gather.23.cloned.1.call-done = bf16[1024,2048]{1,0:T(8,128)(2,1)} async-done(((bf16[128,2048]{1,0:T(8,128)(2,1)}), bf16[1024,2048]{1,0:T(8,128)(2,1)}) %all-gather.23.cloned.1.call-update) | async-done | bytes 4194320 | tf_op jit(solution)/shard_map/all_gather | solution.py:61
  491.5 9.1 fusion.4
  502.3 8.2 convolution_convert_fusion.2
  510.6 50.7 %reduce-scatter.13.cloned.1.call-done = bf16[128,2048]{1,0:T(8,128)(2,1)} async-done(((bf16[1024,2048]{1,0:T(8,128)(2,1)}), bf16[128,2048]{1,0:T(8,128)(2,1)}) %reduce-scatter.13.cloned.1.call-update) | async-done | bytes 524304 | tf_op jit(solution)/shard_map/reduce_scatter | solution.py:65
  563.4 2.3 fusion.83
  565.9 7.0 convolution_convert_fusion.5
  573.0 30.0 %all-gather.25.cloned.1.call-done = bf16[1024,2048]{1,0:T(8,128)(2,1)} async-done(((bf16[128,2048]{1,0:T(8,128)(2,1)}), bf16[1024,2048]{1,0:T(8,128)(2,1)}) %all-gather.25.cloned.1.call-update) | async-done | bytes 4194320 | tf_op jit(solution)/shard_map/all_gather | solution.py:61
  603.0 4.6 convolution_convert_fusion.9
  607.6 2.9 reshape.238
  614.9 2.8 fusion.66
  617.7 3.9 convolution_bitcast_fusion.1
  625.7 4.3 broadcast_multiply_fusion
  633.9 3.6 convolution_convert_fusion.6
  637.8 11.3 convolution_convert_fusion
  649.1 12.3 %reduce-scatter.23.cloned.1.call-done = bf16[176,2048]{1,0:T(8,128)(2,1)} async-done(((bf16[704,2048]{1,0:T(8,128)(2,1)}), bf16[176,2048]{1,0:T(8,128)(2,1)}) %reduce-scatter.23.cloned.1.call-update) | async-done | bytes 720912 | tf_op jit(solution)/shard_map/reduce_scatter | solution.py:216
  661.5 37.9 %reduce-scatter.17.cloned.1.call-done = bf16[512,384]{1,0:T(8,128)(2,1)} async-done(((bf16[2048,384]{1,0:T(8,128)(2,1)}), bf16[512,384]{1,0:T(8,128)(2,1)}) %reduce-scatter.17.cloned.1.call-update) | async-done | bytes 393232 | tf_op jit(solution)/shard_map/reduce_scatter | solution.py:216
  701.7 4.2 collective-permute-done.2
  707.8 6.2 convolution_convert_fusion.1
  715.5 6.7 convolution_convert_fusion.3
  722.3 81.5 %reduce-scatter.21.cloned.1.call-done = bf16[512,1408]{1,0:T(8,128)(2,1)} async-done(((bf16[2048,1408]{1,0:T(8,128)(2,1)}), bf16[512,1408]{1,0:T(8,128)(2,1)}) %reduce-scatter.21.cloned.1.call-update) | async-done | bytes 1441808 | tf_op jit(solution)/shard_map/reduce_scatter | solution.py:216
  806.5 15.9 %collective-permute-done.3 = bf16[256,1408]{1,0:T(8,128)(2,1)S(1)} collective-permute-done((bf16[256,1408]{1,0:T(8,128)(2,1)S(1)}, bf16[256,1408]{1,0:T(8,128)(2,1)S(1)}, u32[]{:S(2)}, u32[]{:S(2)}) %collective-permute-start.3) | collective-permute-done | bytes 720928 | tf_op jit(solution)/shard_map/ppermute | solution.py:74
  824.0 3.4 convolution_convert_fusion.7
  827.4 2.3 bitcast_select_fusion
  830.1 3.1 all-gather.27.cloned.1.call-done
  833.2 5.1 convert_element_type.136
  838.3 16.5 %all-gather.35.cloned.1.call-done = bf16[8,256,384]{2,1,0:T(8,128)(2,1)} async-done(((bf16[2,256,384]{2,1,0:T(8,128)(2,1)}), bf16[8,256,384]{2,1,0:T(8,128)(2,1)}) %all-gather.35.cloned.1.call-update) | async-done | bytes 1572880 | tf_op jit(solution)/shard_map/all_gather | solution.py:220
  860.0 2.7 reshape.216
  866.3 42.9 %reduce-scatter.15.cloned.1.call-done = bf16[128,2048]{1,0:T(8,128)(2,1)} async-done(((bf16[1024,2048]{1,0:T(8,128)(2,1)}), bf16[128,2048]{1,0:T(8,128)(2,1)}) %reduce-scatter.15.cloned.1.call-update) | async-done | bytes 524304 | tf_op jit(solution)/shard_map/reduce_scatter | solution.py:65
  910.9 39.7 %psum.15 = f32[2,2048]{1,0:T(2,128)S(1)} all-reduce(f32[2,2048]{1,0:T(2,128)S(1)} %pad_maximum_fusion.14), channel_id=1, replica_groups=mesh['rep'=4,'z'=4,'x'=2] {'rep','z','x'}, use_global_device_ids=true, to_apply=%region_18.19 | all-reduce | flops 4096 | bytes 32768 | tf_op jit(solution)/shard_map/psum | solution.py:237
  951.3 13.4 %reduce-scatter.11.cloned.1.call-done = bf16[128,2048]{1,0:T(8,128)(2,1)} async-done(((bf16[1024,2048]{1,0:T(8,128)(2,1)}), bf16[128,2048]{1,0:T(8,128)(2,1)}) %reduce-scatter.11.cloned.1.call-update) | async-done | bytes 524304 | tf_op jit(solution)/shard_map/reduce_scatter | solution.py:65
  964.7 3.2 fusion.26
  967.9 42.8 %all-gather.37.cloned.1.call-done = bf16[8,256,1408]{2,1,0:T(8,128)(2,1)} async-done(((bf16[2,256,1408]{2,1,0:T(8,128)(2,1)}), bf16[8,256,1408]{2,1,0:T(8,128)(2,1)}) %all-gather.37.cloned.1.call-update) | async-done | bytes 5767184 | tf_op jit(solution)/shard_map/all_gather | solution.py:220
  1010.6 8.2 copy.159
  1018.9 8.8 convert_bitcast_fusion
  1027.6 61.4 %reduce-scatter.19.cloned.1.call-done = bf16[256,2048]{1,0:T(8,128)(2,1)} async-done(((bf16[1024,2048]{1,0:T(8,128)(2,1)}), bf16[256,2048]{1,0:T(8,128)(2,1)}) %reduce-scatter.19.cloned.1.call-update) | async-done | bytes 1048592 | tf_op jit(solution)/shard_map/reduce_scatter | solution.py:216
  1089.1 7.7 fusion.84
  1096.7 2.9 copy.160
  1099.6 6.2 copy.164
  1105.8 5.7 copy.161
  1111.6 6.4 copy.165
  1117.9 10.1 all-reduce.2.cloned.1.call-done
  1128.0 2.8 convert_element_type.133
  (209 shorter events, 73.0 us)
Async XLA Ops:
  7.2 243.9 %copy-start = (bf16[704,2048]{1,0:T(8,128)(2,1)S(1)}, bf16[704,2048]{1,0:T(8,128)(2,1)}, u32[]{:S(2)}) copy-start(bf16[704,2048]{1,0:T(8,128)(2,1)} %param.21) | copy-start | bytes 8650756
  7.2 52.4 %all-gather.29.cloned.1.call-start = ((), (), s32[]{:S(2)}) async-start(), calls=%async_computation.23 | async-start | bytes 1966080 | tf_op jit(solution)/shard_map/all_gather | solution.py:128
  13.5 7.8 copy-start.38
  13.5 7.9 copy-start.39
  13.5 25.1 %copy-start.2 = (bf16[128,2048]{1,0:T(8,128)(2,1)S(1)}, bf16[128,2048]{1,0:T(8,128)(2,1)}, u32[]{:S(2)}) copy-start(bf16[128,2048]{1,0:T(8,128)(2,1)} %param.11) | copy-start | bytes 1572868
  13.7 6.7 collective-permute-start
  21.3 77.6 %all-gather.17.cloned.1.call-start = ((), (), s32[]{:S(2)}) async-start(), calls=%async_computation.8 | async-start | bytes 4718592 | tf_op jit(solution)/shard_map/all_gather | solution.py:61
  40.8 139.9 %all-gather.31.cloned.1.call-start = ((), (), s32[]{:S(2)}) async-start(), calls=%async_computation.24 | async-start | bytes 5242880 | tf_op jit(solution)/shard_map/all_gather | solution.py:129
  41.6 205.0 %reduce-scatter.9.cloned.1.call-start = ((), (), s32[]{:S(2)}) async-start(), calls=%async_computation.9 | async-start | bytes 4718592 | tf_op jit(solution)/shard_map/reduce_scatter | solution.py:65
  103.9 1.1 copy-start.9
  109.8 2.5 copy-start.5
  110.1 2.3 copy-start.19
  110.1 2.3 copy-start.21
  185.4 170.1 %all-gather.33.cloned.1.call-start = ((), (), s32[]{:S(2)}) async-start(), calls=%async_computation.25 | async-start | bytes 7208960 | tf_op jit(solution)/shard_map/all_gather | solution.py:131
  204.5 30.3 %copy-start.7 = (bf16[2,256,704]{2,1,0:T(8,128)(2,1)S(1)}, bf16[2,256,704]{2,1,0:T(8,128)(2,1)}, u32[]{:S(2)}) copy-start(bf16[2,256,704]{2,1,0:T(8,128)(2,1)} %copy.141) | copy-start | bytes 2162692
  204.5 30.3 %copy-start.8 = (bf16[2,256,704]{2,1,0:T(8,128)(2,1)S(1)}, bf16[2,256,704]{2,1,0:T(8,128)(2,1)}, u32[]{:S(2)}) copy-start(bf16[2,256,704]{2,1,0:T(8,128)(2,1)} %copy.140) | copy-start | bytes 2162692
  206.5 28.3 %collective-permute-start.1 = (bf16[256,1408]{1,0:T(8,128)(2,1)S(1)}, bf16[256,1408]{1,0:T(8,128)(2,1)S(1)}, u32[]{:S(2)}, u32[]{:S(2)}) collective-permute-start(bf16[256,1408]{1,0:T(8,128)(2,1)S(1)} %get-tuple-element.48), channel_id=1, source_target_pairs={{0,1},{1,0},{2,3},{3,2},{4,5},{5,4},{6,7},{7,6},{8,9},{9,8},{10,11... | collective-permute-start | bytes 2162696 | tf_op jit(solution)/shard_map/ppermute | solution.py:74
  236.7 156.3 %all-gather.19.cloned.1.call-start = ((), (), s32[]{:S(2)}) async-start(), calls=%async_computation.10 | async-start | bytes 4718592 | tf_op jit(solution)/shard_map/all_gather | solution.py:61
  251.0 202.7 %all-gather.21.cloned.1.call-start = ((), (), s32[]{:S(2)}) async-start(), calls=%async_computation.11 | async-start | bytes 3604480 | tf_op jit(solution)/shard_map/all_gather | solution.py:132
  252.0 239.5 %all-gather.23.cloned.1.call-start = ((), (), s32[]{:S(2)}) async-start(), calls=%async_computation.13 | async-start | bytes 4718592 | tf_op jit(solution)/shard_map/all_gather | solution.py:61
  252.8 308.5 %reduce-scatter.13.cloned.1.call-start = ((), (), s32[]{:S(2)}) async-start(), calls=%async_computation.14 | async-start | bytes 4718592 | tf_op jit(solution)/shard_map/reduce_scatter | solution.py:65
  491.5 10.8 copy-start.36
  500.6 1.1 copy-start.42
  500.6 1.7 copy-start.43
  500.7 65.3 %copy-start.40 = (bf16[1024,704]{1,0:T(8,128)(2,1)}, bf16[1024,704]{1,0:T(8,128)(2,1)S(1)}, u32[]{:S(2)}) copy-start(bf16[1024,704]{1,0:T(8,128)(2,1)S(1)} %get-tuple-element.54) | copy-start | bytes 4325380
  510.5 50.8 %copy-start.3 = (bf16[128,2048]{1,0:T(8,128)(2,1)S(1)}, bf16[128,2048]{1,0:T(8,128)(2,1)}, u32[]{:S(2)}) copy-start(bf16[128,2048]{1,0:T(8,128)(2,1)} %reduce-scatter.9.cloned.1.call-done) | copy-start | bytes 1572868
  510.5 50.8 %copy-start.27 = (f32[128]{0:T(128)S(1)}, f32[128]{0:T(128)}, u32[]{:S(2)}) copy-start(f32[128]{0:T(128)} %copy-done.26) | copy-start | bytes 1540
  510.6 52.8 %copy-start.11 = (bf16[128,2048]{1,0:T(8,128)(2,1)S(1)}, bf16[128,2048]{1,0:T(8,128)(2,1)}, u32[]{:S(2)}) copy-start(bf16[128,2048]{1,0:T(8,128)(2,1)} %param.12) | copy-start | bytes 1572868
  510.6 52.8 %copy-start.31 = (f32[128]{0:T(128)S(1)}, f32[128]{0:T(128)}, u32[]{:S(2)}) copy-start(f32[128]{0:T(128)} %get-tuple-element.81) | copy-start | bytes 1540
  510.6 92.4 %all-gather.25.cloned.1.call-start = ((), (), s32[]{:S(2)}) async-start(), calls=%async_computation.15 | async-start | bytes 4718592 | tf_op jit(solution)/shard_map/all_gather | solution.py:61
  563.4 9.5 copy-start.33
  565.7 95.7 %reduce-scatter.23.cloned.1.call-start = ((), (), s32[]{:S(2)}) async-start(), calls=%async_computation.21 | async-start | bytes 3604480 | tf_op jit(solution)/shard_map/reduce_scatter | solution.py:216
  572.9 126.4 %reduce-scatter.17.cloned.1.call-start = ((), (), s32[]{:S(2)}) async-start(), calls=%async_computation.17 | async-start | bytes 1966080 | tf_op jit(solution)/shard_map/reduce_scatter | solution.py:216
  607.6 5.1 copy-start.6
  612.6 2.3 copy-start.14
  621.6 1.4 copy-start.17
  622.8 2.9 copy-start.18
  622.8 2.9 copy-start.22
  625.7 5.7 copy-start.20
  630.0 1.5 copy-start.15
  631.5 2.4 copy-start.37
  637.5 166.2 %reduce-scatter.21.cloned.1.call-start = ((), (), s32[]{:S(2)}) async-start(), calls=%async_computation.20 | async-start | bytes 7208960 | tf_op jit(solution)/shard_map/reduce_scatter | solution.py:216
  649.1 184.1 %all-gather.27.cloned.1.call-start = ((), (), s32[]{:S(2)}) async-start(), calls=%async_computation.22 | async-start | bytes 3604480 | tf_op jit(solution)/shard_map/all_gather | solution.py:222
  661.4 193.4 %all-gather.35.cloned.1.call-start = ((), (), s32[]{:S(2)}) async-start(), calls=%async_computation.26 | async-start | bytes 1966080 | tf_op jit(solution)/shard_map/all_gather | solution.py:220
  700.4 5.5 collective-permute-start.2
  707.8 201.5 %reduce-scatter.15.cloned.1.call-start = ((), (), s32[]{:S(2)}) async-start(), calls=%async_computation.16 | async-start | bytes 4718592 | tf_op jit(solution)/shard_map/reduce_scatter | solution.py:65
  714.0 1.4 copy-start.41
  714.1 250.6 %reduce-scatter.11.cloned.1.call-start = ((), (), s32[]{:S(2)}) async-start(), calls=%async_computation.12 | async-start | bytes 4718592 | tf_op jit(solution)/shard_map/reduce_scatter | solution.py:65
  722.2 288.4 %all-gather.37.cloned.1.call-start = ((), (), s32[]{:S(2)}) async-start(), calls=%async_computation.27 | async-start | bytes 7208960 | tf_op jit(solution)/shard_map/all_gather | solution.py:220
  803.7 18.7 %copy-start.10 = (bf16[512,1408]{1,0:T(8,128)(2,1)S(1)}, bf16[512,1408]{1,0:T(8,128)(2,1)}, u32[]{:S(2)}) copy-start(bf16[512,1408]{1,0:T(8,128)(2,1)} %reduce-scatter.21.cloned.1.call-done) | copy-start | bytes 4325380
  805.3 17.1 %collective-permute-start.3 = (bf16[256,1408]{1,0:T(8,128)(2,1)S(1)}, bf16[256,1408]{1,0:T(8,128)(2,1)S(1)}, u32[]{:S(2)}, u32[]{:S(2)}) collective-permute-start(bf16[256,1408]{1,0:T(8,128)(2,1)S(1)} %broadcast_select_fusion.1), channel_id=1, source_target_pairs={{0,1},{1,0},{2,3},{3,2},{4,5},{5,4},{6,7},{7,6},{8,9},{9,8},{10,11... | collective-permute-start | bytes 2162696 | tf_op jit(solution)/shard_map/ppermute | solution.py:74
  822.6 1.4 copy-start.16
  823.8 265.2 %reduce-scatter.19.cloned.1.call-start = ((), (), s32[]{:S(2)}) async-start(), calls=%async_computation.18 | async-start | bytes 5242880 | tf_op jit(solution)/shard_map/reduce_scatter | solution.py:216
  829.8 298.3 %all-reduce.2.cloned.1.call-start = ((), (), s32[]{:S(2)}) async-start(), calls=%async_computation.19 | async-start | bytes 2097152 | tf_op jit(solution)/shard_map/psum | solution.py:230
  856.4 1.7 copy-start.4
  864.0 45.3 %copy-start.30 = (f32[128]{0:T(128)S(1)}, f32[128]{0:T(128)}, u32[]{:S(2)}) copy-start(f32[128]{0:T(128)} %copy-done.29) | copy-start | bytes 1540
  864.2 46.7 %copy-start.25 = (f32[2048]{0:T(1024)S(1)}, f32[2048]{0:T(1024)}, u32[]{:S(2)}) copy-start(f32[2048]{0:T(1024)} %get-tuple-element.44) | copy-start | bytes 24580
  864.2 100.5 %copy-start.12 = (bf16[128,2048]{1,0:T(8,128)(2,1)S(1)}, bf16[128,2048]{1,0:T(8,128)(2,1)}, u32[]{:S(2)}) copy-start(bf16[128,2048]{1,0:T(8,128)(2,1)} %param.12) | copy-start | bytes 1572868
  864.2 100.4 %copy-start.13 = (bf16[128,2048]{1,0:T(8,128)(2,1)S(1)}, bf16[128,2048]{1,0:T(8,128)(2,1)}, u32[]{:S(2)}) copy-start(bf16[128,2048]{1,0:T(8,128)(2,1)} %reduce-scatter.13.cloned.1.call-done) | copy-start | bytes 1572868
  864.2 100.4 %copy-start.28 = (f32[128]{0:T(128)S(1)}, f32[128]{0:T(128)}, u32[]{:S(2)}) copy-start(f32[128]{0:T(128)} %copy-done.26) | copy-start | bytes 1540
  864.2 100.4 %copy-start.32 = (f32[128]{0:T(128)S(1)}, f32[128]{0:T(128)}, u32[]{:S(2)}) copy-start(f32[128]{0:T(128)} %get-tuple-element.81) | copy-start | bytes 1540
  864.2 100.4 %copy-start.34 = (f32[128]{0:T(128)S(1)}, f32[128]{0:T(128)}, u32[]{:S(2)}) copy-start(f32[128]{0:T(128)} %copy-done.33) | copy-start | bytes 1540
  864.3 100.4 %copy-start.35 = (f32[128]{0:T(128)S(1)}, f32[128]{0:T(128)}, u32[]{:S(2)}) copy-start(f32[128]{0:T(128)} %get-tuple-element.79) | copy-start | bytes 1540
  1111.6 19.3 %copy-start.1 = (bf16[704,2048]{1,0:T(8,128)(2,1)S(1)}, bf16[704,2048]{1,0:T(8,128)(2,1)}, u32[]{:S(2)}) copy-start(bf16[704,2048]{1,0:T(8,128)(2,1)} %param.21) | copy-start | bytes 8650756
  (4 other events, 2.9 us)
Sparse Core Ops, SparseCore 0:
  21.4 38.1 all-gather.28
  62.1 36.7 all-gather.16
  100.5 80.1 all-gather.30
  185.5 60.9 reduce-scatter.8
  248.5 106.9 all-gather.32
  357.8 35.1 all-gather.18
  395.1 58.5 all-gather.20
  455.6 35.8 all-gather.22
  510.7 50.5 reduce-scatter.12
  565.8 37.1 all-gather.24
  605.9 55.4 reduce-scatter.22
  664.1 35.1 reduce-scatter.16
  702.2 101.4 reduce-scatter.20
  805.1 27.9 all-gather.26
  835.2 19.6 all-gather.34
  858.6 50.5 reduce-scatter.14
  913.0 51.5 reduce-scatter.10
  966.6 43.9 all-gather.36
  1012.9 76.0 reduce-scatter.18
  1091.2 36.7 all-reduce.1

commit v2 on v1

--- a/solution.py
+++ b/solution.py
@@ -7,10 +7,11 @@
 
 KV = 4
 HD = 64
-X = 2
+PAIR = 2
 epsilon = 1e-05
 
-TP = ("rep", "x")
+TP = ("rep", "zl")
+HOLDERS = ("zh", "x")
 
 
 def rotary_tables(length, head_size):
@@ -67,12 +68,44 @@
     ).astype(jnp.float32)
 
 
-def swap_x(pieces):
-    x = lax.axis_index("x")
-    away = jnp.where(x == 0, pieces[1], pieces[0])
-    own = jnp.where(x == 0, pieces[0], pieces[1])
-    came = lax.ppermute(away, "x", [(0, 1), (1, 0)])
-    return jnp.stack([jnp.where(x == 0, own, came), jnp.where(x == 0, came, own)])
+SWAP = [(0, 1), (1, 0)]
+
+
+def swap(pieces, axis):
+    first = lax.axis_index(axis) == 0
+    came = lax.ppermute(jnp.where(first, pieces[1], pieces[0]), axis, SWAP)
+    own = jnp.where(first, pieces[0], pieces[1])
+    return jnp.stack([jnp.where(first, own, came), jnp.where(first, came, own)])
+
+
+def exchange(piece, axis):
+    first = lax.axis_index(axis) == 0
+    came = lax.ppermute(piece, axis, SWAP)
+    return jnp.stack([jnp.where(first, piece, came), jnp.where(first, came, piece)])
+
+
+def gather_holders(piece):
+    if lax.axis_size("zh") == PAIR and lax.axis_size("x") == PAIR:
+        both = exchange(exchange(piece, "zh"), "x")
+        return jnp.moveaxis(both, 0, 1).reshape((PAIR * PAIR,) + piece.shape)
+    return lax.all_gather(piece, HOLDERS, axis=0)
+
+
+def add(left, right):
+    return (left.astype(jnp.float32) + right.astype(jnp.float32)).astype(jnp.bfloat16)
+
+
+def halve(pieces, axis):
+    first = lax.axis_index(axis) == 0
+    came = lax.ppermute(jnp.where(first, pieces[1], pieces[0]), axis, SWAP)
+    return add(jnp.where(first, pieces[0], pieces[1]), came)
+
+
+def scatter_holders(partial):
+    if lax.axis_size("zh") == PAIR and lax.axis_size("x") == PAIR:
+        pieces = jnp.moveaxis(partial.reshape((PAIR, PAIR) + partial.shape[1:]), 1, 0)
+        return halve(halve(pieces, "x"), "zh")
+    return lax.psum_scatter(partial, HOLDERS, scatter_dimension=0, tiled=False)
 
 
 def per_device(
@@ -89,49 +122,70 @@
     down_weight,
 ):
     length, width = block_input.shape
-    reps, zs = lax.axis_size("rep"), lax.axis_size("z")
-    group = reps * X
-    r = lax.axis_index("rep")
-    z = lax.axis_index("z")
-    x = lax.axis_index("x")
+    reps, xs = lax.axis_size("rep"), lax.axis_size("x")
+    high = lax.axis_size("zh")
+    holders = high * xs
+    group = reps * PAIR
+    r, zl, x = lax.axis_index("rep"), lax.axis_index("zl"), lax.axis_index("x")
+    shard = (lax.axis_index("zh") * PAIR + zl) * xs + x
     rows = query_weight.shape[0]
     heads_wide = query_weight.shape[1] // group
-    per_kv = zs // KV
+    per_rep = holders // reps
     hidden_piece = down_weight.shape[0] // reps
-    hidden_wide = zs * hidden_piece
+    hidden_wide = holders * hidden_piece
     heads = heads_wide // HD
     scale_factor = HD ** (-0.5)
 
     def own_rep(values, axis):
         return lax.dynamic_index_in_dim(values, r, axis, keepdims=False)
 
+    def by_holder(values, axis):
+        shape = values.shape
+        cut = values.reshape(shape[:axis] + (high, PAIR, xs, -1) + shape[axis + 1 :])
+        cut = jnp.moveaxis(cut, axis + 1, 0)
+        return cut.reshape((PAIR,) + shape[:axis] + (holders, -1) + shape[axis + 1 :])
+
     def query_columns(weight):
-        pieces = own_rep(weight.reshape(rows, KV, per_kv, X, -1), 1)
-        return jnp.moveaxis(pieces, 2, 0).reshape(X, rows, heads_wide)
+        pieces = by_holder(weight, 1).reshape(PAIR, rows, reps, heads_wide)
+        return own_rep(pieces, 2)
 
     def hidden_columns(weight):
-        pieces = own_rep(weight.reshape(rows, zs, X, reps, hidden_piece), 3)
-        return jnp.moveaxis(pieces, 2, 0).reshape(X, rows, hidden_wide)
+        pieces = by_holder(weight, 1).reshape(PAIR, rows, holders, reps, hidden_piece)
+        return own_rep(pieces, 3).reshape(PAIR, rows, hidden_wide)
+
+    key_heads = [
+        (((r * per_rep // xs) * PAIR + low) * xs * heads_wide // (per_rep * HD)) * KV
+        // (query_weight.shape[1] // HD)
+        for low in range(PAIR)
+    ]
 
     def key_columns(weight):
-        piece = own_rep(weight.reshape(rows, KV, HD), 1)
-        return jnp.broadcast_to(piece[None], (X, rows, HD))
+        pieces = weight.reshape(rows, KV, HD)
+        return jnp.stack(
+            [lax.dynamic_index_in_dim(pieces, k, 1, keepdims=False) for k in key_heads]
+        )
 
     attn_pack = jnp.concatenate(
         [query_columns(query_weight), key_columns(key_weight), key_columns(value_weight)], axis=2
     )
     mlp_pack = jnp.concatenate([hidden_columns(gate_weight), hidden_columns(up_weight)], axis=2)
 
-    gains = lax.all_gather(jnp.stack([attn_gain, mlp_gain]), ("z", "x"), axis=1, tiled=True)
+    gains = lax.all_gather(
+        jnp.stack([attn_gain, mlp_gain]), ("zh", "zl", "x"), axis=1, tiled=True
+    )
     gains = gains.astype(jnp.float32)
     gain_one, gain_two = gains[0], gains[1]
-    attn_w = lax.all_gather(swap_x(attn_pack), "z", axis=0).reshape(width, -1)
-    out_all = lax.all_gather(out_weight, "z", axis=0)
-    out_w = own_rep(out_all.reshape(KV, per_kv * rows, width), 0)
-    mlp_w = lax.all_gather(swap_x(mlp_pack), "z", axis=0).reshape(width, -1)
-    down_w = lax.all_gather(
-        own_rep(down_weight.reshape(reps, hidden_piece, width), 0), "z", axis=0
-    ).reshape(hidden_wide, width)
+
+    def all_rows(pack):
+        whole = gather_holders(swap(pack, "zl"))
+        whole = whole.reshape((high, xs, PAIR) + whole.shape[2:])
+        return jnp.swapaxes(whole, 1, 2).reshape(width, -1)
+
+    attn_w = all_rows(attn_pack)
+    out_w = own_rep(gather_holders(out_weight).reshape(reps, per_rep * rows, width), 0)
+    down_w = gather_holders(own_rep(down_weight.reshape(reps, hidden_piece, width), 0))
+    down_w = down_w.reshape(hidden_wide, width)
+    mlp_w = all_rows(mlp_pack)
 
     x_float = block_input.astype(jnp.float32)
     rms_one = lax.rsqrt(jnp.mean(x_float * x_float, axis=-1, keepdims=True) + epsilon)
@@ -212,28 +266,44 @@
         grad_hidden_one * gain_one[None, :], x_float, rms_one
     )
 
-    def scatter_z(partial):
-        return lax.psum_scatter(partial, "z", scatter_dimension=0, tiled=True)
-
     def to_owner(partial):
-        pieces = swap_x(scatter_z(partial).reshape(X, rows, -1))
+        pieces = partial.reshape(high, PAIR, xs, rows, -1)
+        pieces = jnp.swapaxes(pieces, 1, 2).reshape(holders, PAIR, rows, -1)
+        pieces = swap(scatter_holders(pieces), "zl")
         return lax.all_gather(pieces, "rep", axis=0).astype(jnp.float32)
 
-    down_grad = lax.all_gather(scatter_z(down_local), "rep", axis=0, tiled=True).astype(jnp.float32)
-    mlp_grad = to_owner(mlp_local).reshape(reps, X, rows, 2, zs, hidden_piece)
-    mlp_grad = mlp_grad.transpose(3, 2, 4, 1, 0, 5).reshape(2, rows, -1)
+    def from_holder(values):
+        cut = values.reshape(PAIR, rows, high, xs, -1)
+        return cut.transpose(1, 2, 0, 3, 4).reshape(rows, -1)
+
+    down_grad = scatter_holders(down_local.reshape(holders, hidden_piece, width))
+    down_grad = lax.all_gather(down_grad, "rep", axis=0, tiled=True).astype(jnp.float32)
+    mlp_grad = to_owner(mlp_local).reshape(reps, PAIR, rows, 2, holders, hidden_piece)
+    mlp_grad = mlp_grad.transpose(3, 1, 2, 4, 0, 5)
+    gate_grad, up_grad = from_holder(mlp_grad[0]), from_holder(mlp_grad[1])
     out_padded = jnp.where(
-        (jnp.arange(KV) == r)[:, None, None],
-        out_local.reshape(1, per_kv * rows, width),
+        (jnp.arange(reps) == r)[:, None, None],
+        out_local.reshape(1, per_rep * rows, width),
         jnp.zeros((), jnp.bfloat16),
     )
-    out_grad = lax.psum(scatter_z(out_padded.reshape(zs * rows, width)), "rep").astype(jnp.float32)
+    out_padded = scatter_holders(out_padded.reshape(holders, rows, width))
+    out_grad = lax.psum(out_padded, "rep").astype(jnp.float32)
     attn_grad = to_owner(attn_local)
-    query_grad = attn_grad[..., :heads_wide].reshape(KV, X, rows, per_kv, -1)
-    query_grad = query_grad.transpose(2, 0, 3, 1, 4).reshape(rows, -1)
-    key_value = jnp.sum(attn_grad[..., heads_wide:], axis=1)
-    key_grad = key_value[..., :HD].transpose(1, 0, 2).reshape(rows, -1)
-    value_grad = key_value[..., HD:].transpose(1, 0, 2).reshape(rows, -1)
+    query_grad = attn_grad[..., :heads_wide].transpose(1, 2, 0, 3)
+    query_grad = from_holder(query_grad.reshape(PAIR, rows, holders, -1))
+    key_value = attn_grad[..., heads_wide:]
+
+    def key_back(values):
+        total = jnp.zeros((KV, rows, HD), jnp.float32)
+        for rep in range(reps):
+            for low in range(PAIR):
+                head = (rep * per_rep // xs) * PAIR + low
+                head = head * xs * heads_wide // (per_rep * HD)
+                head = head * KV // (query_weight.shape[1] // HD)
+                total = total.at[head].add(values[rep, low])
+        return total.transpose(1, 0, 2).reshape(rows, -1)
+
+    key_grad, value_grad = key_back(key_value[..., :HD]), key_back(key_value[..., HD:])
     gain_grads = lax.psum(
         jnp.stack(
             [
@@ -241,9 +311,9 @@
                 jnp.sum(grad_hidden_two * normed_two, axis=0),
             ]
         ),
-        ("rep", "z", "x"),
-    )
-    gain_grads = lax.dynamic_slice_in_dim(gain_grads, (z * X + x) * rows, rows, axis=1)
+        ("rep", "zh", "zl", "x"),
+    )
+    gain_grads = lax.dynamic_slice_in_dim(gain_grads, shard * rows, rows, axis=1)
     return (
         block_output,
         input_grad,
@@ -251,8 +321,8 @@
         key_grad,
         value_grad,
         out_grad,
-        mlp_grad[0],
-        mlp_grad[1],
+        gate_grad,
+        up_grad,
         down_grad,
         gain_grads[0],
         gain_grads[1],
@@ -261,10 +331,12 @@
 
 def solution(mesh):
     reps, shards = mesh.shape["rep"], mesh.shape["shard"]
-    cube = Mesh(mesh.devices.reshape(reps, shards // X, X), ("rep", "z", "x"))
-    tokens = P(("rep", "z", "x"), None)
-    matrix = P(("z", "x"), None)
-    vector = P(("z", "x"))
+    xs = 1
+    while 2 * (2 * xs) ** 2 <= shards:
+        xs *= 2
+    names = ("rep", "zh", "zl", "x")
+    cube = Mesh(mesh.devices.reshape(reps, shards // (PAIR * xs), PAIR, xs), names)
+    tokens, matrix, vector = P(names, None), P(names[1:], None), P(names[1:])
     in_specs = (tokens, tokens, vector) + (matrix,) * 4 + (vector,) + (matrix,) * 3
     out_specs = (tokens, tokens) + (matrix,) * 7 + (vector,) * 2
     return jax.shard_map(

time: 1150 us -> 1210 us (1.052)
  other arithmetic: 55.7 us -> 85.4 us
  starting transfers between devices: 7.77 us -> 26.2 us
    ppermute x4 -> x20, waiting for transfers between devices: 51.8 us -> 535 us  [the longest x8 239 us: exchange(): came = lax.ppermute(piece, axis, SWAP)]
    all_gather x5 -> x1, waiting for transfers between devices: 230 us -> 0.02 us  [per_device(): lax.all_gather(down_grad, 'rep', axis=0, tiled=True).astype(jnp.float32)]
    reduce_scatter x4 -> x0, waiting for transfers between devices: 193 us -> none  [scatter_z(): return lax.psum_scatter(partial, 'z', scatter_dimension=0, tiled=True)]
    reduce_scatter x4, waiting for transfers between devices: 117 us -> 282 us  [scatter_tokens(): lax.psum_scatter(partial.astype(jnp.bfloat16), TP, scatter_dimension=0, t...]
    all_gather x4, waiting for transfers between devices: 145 us -> 0.02 us  [gather_tokens(): return lax.all_gather(rows, TP, axis=0, tiled=True)]
    all_gather x2, waiting for transfers between devices: 59.3 us -> 0.01 us  [to_owner(): return lax.all_gather(pieces, 'rep', axis=0).astype(jnp.float32)]
    ppermute x4 -> x20, starting transfers between devices: 5.85 us -> 24.7 us  [the longest x8 14.5 us: halve(): came = lax.ppermute(jnp.where(first, pieces[1], pieces[0]), axis, SWAP)]
    another operation x8 -> x26, other arithmetic: 5.93 us -> 19 us  [the longest x14 14.1 us: exchange(): jnp.stack([jnp.where(first, piece, came), jnp.where(first, came, piece)])]
  transfers between devices with their start and end apart: 24 -> 32, of which waited for: 24 -> 20; matrix products, arithmetic and copies ran while one was open for 18% -> 18% of each run, Pallas kernels for 0% -> 0%
where the time goes in v2:
time: 1210 us; the launch traced here: 1200 us
  waiting for transfers between devices  818 us (68%)
  local copies, waits for them, and re-layouts  103 us (9%)
  matrix products  90.6 us (7%)
  other arithmetic  85.4 us (7%)
  blocking collectives  59.6 us (5%)
  starting transfers between devices  26.2 us (2%)
  between operations  15.9 us (1%)
    reduce_scatter x4, waiting for transfers between devices, scatter_tokens(): lax.psum_scatter(partial.astype(jnp.bfloat16), TP, scatter_dimension=0, t...  282 us
    ppermute x8, waiting for transfers between devices, exchange(): came = lax.ppermute(piece, axis, SWAP)  239 us
    ppermute x8, waiting for transfers between devices, halve(): came = lax.ppermute(jnp.where(first, pieces[1], pieces[0]), axis, SWAP)  226 us
    ppermute x4, waiting for transfers between devices, swap(): came = lax.ppermute(jnp.where(first, pieces[1], pieces[0]), axis, SWAP)  70.4 us
    psum x1, blocking collectives, per_device(): lax.psum(jnp.stack([jnp.sum(grad_hidden_one * normed_one, axis=0), jnp.su...  41.7 us
    unnamed x116, local copies, waits for them, and re-layouts  29.6 us
    dot_general x4, matrix products, matmul(): return jnp.dot(left, right, preferred_element_type=jnp.float32)  27.8 us
    dot_general x4, matrix products, contract_last(): lax.dot_general(left, right, (((1,), (1,)), ((), ())), preferred_element_...  25.8 us
  transfers between devices with their start and end apart: 32, of which 20 were waited for; matrix products, arithmetic and copies ran while one was open for 18% of the time, Pallas kernels for 0%

profile of v2, /device:TPU:1, one launch (start us, length us, event | category | flops | bytes accessed | tf_op | source)
XLA Modules:
  0.0 1198.3 jit_solution(9677408877149972076)
XLA Ops:
  10.5 17.9 %all_gather.30 = bf16[2,2048]{1,0:T(2,128)(2,1)S(1)} all-gather(bf16[2,256]{1,0:T(2,128)(2,1)S(1)} %pad_maximum_fusion.23), channel_id=1, replica_groups=mesh['rep'=4,'zh'=2,'zl'=2,'x'=2] {'zh','zl','x'}, dimensions={1}, use_global_device_ids=true | all-gather | bytes 9216 | tf_op jit(solution)/shard_map/all_gather | solution.py:173
  32.6 28.2 %collective-permute-done = bf16[256,384]{1,0:T(8,128)(2,1)S(1)} collective-permute-done((bf16[256,384]{1,0:T(8,128)(2,1)S(1)}, bf16[256,384]{1,0:T(8,128)(2,1)S(1)}, u32[]{:S(2)}, u32[]{:S(2)}) %collective-permute-start) | collective-permute-done | bytes 196640 | tf_op jit(solution)/shard_map/ppermute | solution.py:76
  60.8 16.7 %collective-permute-done.3 = bf16[256,2048]{1,0:T(8,128)(2,1)} collective-permute-done((bf16[256,2048]{1,0:T(8,128)(2,1)}, bf16[256,2048]{1,0:T(8,128)(2,1)}, u32[]{:S(2)}, u32[]{:S(2)}) %collective-permute-start.3) | collective-permute-done | bytes 1048608 | tf_op jit(solution)/shard_map/ppermute | solution.py:83
  80.8 19.1 %collective-permute-done.1 = bf16[2,256,384]{2,1,0:T(8,128)(2,1)S(1)} collective-permute-done((bf16[2,256,384]{2,1,0:T(8,128)(2,1)S(1)}, bf16[2,256,384]{2,1,0:T(8,128)(2,1)S(1)}, u32[]{:S(2)}, u32[]{:S(2)}) %collective-permute-start.1) | collective-permute-done | bytes 393248 | tf_op jit(solution)/shard_map/ppermute | solution.py:83
  104.0 40.5 %collective-permute-done.2 = bf16[2,2,256,384]{3,2,1,0:T(8,128)(2,1)} collective-permute-done((bf16[2,2,256,384]{3,2,1,0:T(8,128)(2,1)}, bf16[2,2,256,384]{3,2,1,0:T(8,128)(2,1)}, u32[]{:S(2)}, u32[]{:S(2)}) %collective-permute-start.2) | collective-permute-done | bytes 786464 | tf_op jit(solution)/shard_map/ppermute | solution.py:83
  149.3 2.4 pad_maximum_fusion
  151.6 5.0 fusion.126
  166.1 4.7 convolution_convert_fusion.4
  170.9 85.8 %reduce-scatter.5.cloned.1.call-done = bf16[128,2048]{1,0:T(8,128)(2,1)} async-done(((bf16[1024,2048]{1,0:T(8,128)(2,1)}), bf16[128,2048]{1,0:T(8,128)(2,1)}) %reduce-scatter.5.cloned.1.call-update) | async-done | bytes 524304 | tf_op jit(solution)/shard_map/reduce_scatter | solution.py:66
  261.2 3.1 copy.160
  266.1 3.2 copy.162
  272.3 24.3 %collective-permute-done.5 = bf16[256,1408]{0,1:T(8,128)(2,1)S(1)} collective-permute-done((bf16[256,1408]{0,1:T(8,128)(2,1)S(1)}, bf16[256,1408]{0,1:T(8,128)(2,1)S(1)}, u32[]{:S(2)}, u32[]{:S(2)}) %collective-permute-start.5) | collective-permute-done | bytes 720928 | tf_op jit(solution)/shard_map/ppermute | solution.py:76
  297.1 2.2 collective-permute-start.6
  301.9 74.9 %collective-permute-done.6 = bf16[2,256,1408]{1,2,0:T(8,128)(2,1)} collective-permute-done((bf16[2,256,1408]{1,2,0:T(8,128)(2,1)S(1)}, bf16[2,256,1408]{1,2,0:T(8,128)(2,1)}, u32[]{:S(2)}, u32[]{:S(2)}) %collective-permute-start.6) | collective-permute-done | bytes 1441824 | tf_op jit(solution)/shard_map/ppermute | solution.py:83
  379.8 12.3 %collective-permute-done.8 = bf16[176,2048]{1,0:T(8,128)(2,1)} collective-permute-done((bf16[176,2048]{1,0:T(8,128)(2,1)}, bf16[176,2048]{1,0:T(8,128)(2,1)}, u32[]{:S(2)}, u32[]{:S(2)}) %collective-permute-start.8) | collective-permute-done | bytes 720928 | tf_op jit(solution)/shard_map/ppermute | solution.py:83
  395.0 75.1 %collective-permute-done.9 = bf16[2,176,2048]{2,1,0:T(8,128)(2,1)S(1)} collective-permute-done((bf16[2,176,2048]{2,1,0:T(8,128)(2,1)S(1)}, bf16[2,176,2048]{2,1,0:T(8,128)(2,1)S(1)}, u32[]{:S(2)}, u32[]{:S(2)}) %collective-permute-start.9) | collective-permute-done | bytes 1441824 | tf_op jit(solution)/shard_map/ppermute | solution.py:83
  471.1 3.0 maximum_bitcast_fusion
  474.1 8.3 copy.164
  482.4 11.7 fusion.127
  494.1 9.5 fusion.6
  505.3 8.2 convolution_convert_fusion.2
  513.6 92.6 %reduce-scatter.9.cloned.1.call-done = bf16[128,2048]{1,0:T(8,128)(2,1)} async-done(((bf16[1024,2048]{1,0:T(8,128)(2,1)}), bf16[128,2048]{1,0:T(8,128)(2,1)}) %reduce-scatter.9.cloned.1.call-update) | async-done | bytes 524304 | tf_op jit(solution)/shard_map/reduce_scatter | solution.py:66
  607.7 2.3 fusion.121
  610.5 5.4 convolution_convert_fusion.5
  619.8 8.8 convolution_convert_fusion
  628.6 8.4 copy.183
  637.0 4.6 select_bitcast_fusion
  642.8 7.6 collective-permute-done.18
  654.7 30.1 %collective-permute-done.19 = bf16[176,2048]{1,0:T(8,128)(2,1)S(1)} collective-permute-done((bf16[176,2048]{1,0:T(8,128)(2,1)S(1)}, bf16[176,2048]{1,0:T(8,128)(2,1)S(1)}, u32[]{:S(2)}, u32[]{:S(2)}) %collective-permute-start.19) | collective-permute-done | bytes 720928 | tf_op jit(solution)/shard_map/ppermute | solution.py:100
  686.2 26.0 %collective-permute-done.15 = bf16[2,2,256,1408]{2,3,1,0:T(8,128)(2,1)} collective-permute-done((bf16[2,2,256,1408]{2,3,1,0:T(8,128)(2,1)}, bf16[2,2,256,1408]{2,3,1,0:T(8,128)(2,1)}, u32[]{:S(2)}, u32[]{:S(2)}) %collective-permute-start.15) | collective-permute-done | bytes 2883616 | tf_op jit(solution)/shard_map/ppermute | solution.py:100
  712.2 4.7 fusion.2
  719.2 61.3 %collective-permute-done.16 = bf16[2,256,1408]{1,2,0:T(8,128)(2,1)S(1)} collective-permute-done((bf16[2,256,1408]{1,2,0:T(8,128)(2,1)S(1)}, bf16[2,256,1408]{1,2,0:T(8,128)(2,1)S(1)}, u32[]{:S(2)}, u32[]{:S(2)}) %collective-permute-start.16) | collective-permute-done | bytes 1441824 | tf_op jit(solution)/shard_map/ppermute | solution.py:100
  781.1 2.2 collective-permute-start.17
  783.3 15.0 %collective-permute-done.17 = bf16[256,1408]{0,1:T(8,128)(2,1)S(1)} collective-permute-done((bf16[256,1408]{0,1:T(8,128)(2,1)S(1)}, bf16[256,1408]{0,1:T(8,128)(2,1)S(1)}, u32[]{:S(2)}, u32[]{:S(2)}) %collective-permute-start.17) | collective-permute-done | bytes 720928 | tf_op jit(solution)/shard_map/ppermute | solution.py:76
  800.4 3.8 convolution_convert_fusion.9
  805.3 3.6 convolution_convert_fusion.7
  813.3 3.0 fusion.78
  816.3 3.8 convolution_bitcast_fusion.1
  821.2 4.3 broadcast_multiply_fusion
  829.5 4.6 convolution_convert_fusion.6
  834.8 39.0 %collective-permute-done.10 = bf16[2,2,256,384]{3,2,1,0:T(8,128)(2,1)S(1)} collective-permute-done((bf16[2,2,256,384]{3,2,1,0:T(8,128)(2,1)S(1)}, bf16[2,2,256,384]{3,2,1,0:T(8,128)(2,1)S(1)}, u32[]{:S(2)}, u32[]{:S(2)}) %collective-permute-start.10) | collective-permute-done | bytes 786464 | tf_op jit(solution)/shard_map/ppermute | solution.py:100
  874.2 2.9 fusion.3
  877.2 6.0 collective-permute-start.14
  883.3 62.1 %collective-permute-done.11 = bf16[2,256,384]{2,1,0:T(8,128)(2,1)S(1)} collective-permute-done((bf16[2,256,384]{2,1,0:T(8,128)(2,1)S(1)}, bf16[2,256,384]{2,1,0:T(8,128)(2,1)S(1)}, u32[]{:S(2)}, u32[]{:S(2)}) %collective-permute-start.11) | collective-permute-done | bytes 393248 | tf_op jit(solution)/shard_map/ppermute | solution.py:100
  948.0 2.9 collective-permute-done.12
  952.1 4.4 convolution_convert_fusion.1
  958.3 6.4 convolution_convert_fusion.3
  964.8 5.1 convert_element_type.264
  969.9 8.3 copy.185
  978.2 8.4 convert_bitcast_fusion
  986.6 7.7 fusion.122
  994.7 3.2 copy.189
  997.9 6.2 copy.194
  1004.1 3.2 copy.186
  1007.3 3.2 copy.187
  1010.5 6.2 copy.193
  1016.7 2.8 convert_element_type.245
  1019.5 3.1 copy.181
  1025.4 2.4 copy.182
  1027.8 3.9 reshape.738
  1039.9 57.0 %reduce-scatter.11.cloned.1.call-done = bf16[128,2048]{1,0:T(8,128)(2,1)} async-done(((bf16[1024,2048]{1,0:T(8,128)(2,1)}), bf16[128,2048]{1,0:T(8,128)(2,1)}) %reduce-scatter.11.cloned.1.call-update) | async-done | bytes 524304 | tf_op jit(solution)/shard_map/reduce_scatter | solution.py:66
  1098.5 41.7 %psum.15 = f32[2,2048]{1,0:T(2,128)S(1)} all-reduce(f32[2,2048]{1,0:T(2,128)S(1)} %pad_maximum_fusion.22), channel_id=1, replica_groups=mesh['rep'=4,'zh'=2,'zl'=2,'x'=2] {'rep','zh','zl','x'}, use_global_device_ids=true, to_apply=%region_13.14 | all-reduce | flops 4096 | bytes 32768 | tf_op jit(solution)/shard_map/psum | solution.py:307
  1140.9 46.9 %reduce-scatter.7.cloned.1.call-done = bf16[128,2048]{1,0:T(8,128)(2,1)} async-done(((bf16[1024,2048]{1,0:T(8,128)(2,1)}), bf16[128,2048]{1,0:T(8,128)(2,1)}) %reduce-scatter.7.cloned.1.call-update) | async-done | bytes 524304 | tf_op jit(solution)/shard_map/reduce_scatter | solution.py:66
  1187.9 3.2 fusion.33
  (277 shorter events, 97.9 us)
Async XLA Ops:
  7.2 23.5 %copy-start.32 = (bf16[256,256]{1,0:T(8,128)(2,1)S(1)}, bf16[256,256]{1,0:T(8,128)(2,1)}, u32[]{:S(2)}) copy-start(bf16[256,256]{1,0:T(8,128)(2,1)} %param.47) | copy-start | bytes 393220
  7.2 23.6 %copy-start.33 = (bf16[256,256]{1,0:T(8,128)(2,1)S(1)}, bf16[256,256]{1,0:T(8,128)(2,1)}, u32[]{:S(2)}) copy-start(bf16[256,256]{1,0:T(8,128)(2,1)} %param.48) | copy-start | bytes 393220
  7.2 24.1 %copy-start.23 = (bf16[256,2048]{1,0:T(8,128)(2,1)S(1)}, bf16[256,2048]{1,0:T(8,128)(2,1)}, u32[]{:S(2)}) copy-start(bf16[256,2048]{1,0:T(8,128)(2,1)} %param.46) | copy-start | bytes 3145732
  7.2 144.4 %all-gather.10.cloned.1.call-start = ((), (), s32[]{:S(2)}) async-start(), calls=%async_computation.4 | async-start | bytes 4718592 | tf_op jit(solution)/shard_map/all_gather | solution.py:62
  9.2 21.5 %copy-start.40 = (f32[128]{0:T(128)}, f32[128]{0:T(128)S(1)}, u32[]{:S(2)}) copy-start(f32[128]{0:T(128)S(1)} %get-tuple-element.304) | copy-start | bytes 1540
  30.4 226.2 %reduce-scatter.5.cloned.1.call-start = ((), (), s32[]{:S(2)}) async-start(), calls=%async_computation.5 | async-start | bytes 4718592 | tf_op jit(solution)/shard_map/reduce_scatter | solution.py:66
  30.5 47.0 %collective-permute-start.3 = (bf16[256,2048]{1,0:T(8,128)(2,1)}, bf16[256,2048]{1,0:T(8,128)(2,1)}, u32[]{:S(2)}, u32[]{:S(2)}) collective-permute-start(bf16[256,2048]{1,0:T(8,128)(2,1)} %param.49), channel_id=1, source_target_pairs={{0,4},{4,0},{1,5},{5,1},{2,6},{6,2},{3,7},{7,3},{8,12},{12,8},{9,1... | collective-permute-start | bytes 3145736 | tf_op jit(solution)/shard_map/ppermute | solution.py:83
  32.5 28.3 %collective-permute-start = (bf16[256,384]{1,0:T(8,128)(2,1)S(1)}, bf16[256,384]{1,0:T(8,128)(2,1)S(1)}, u32[]{:S(2)}, u32[]{:S(2)}) collective-permute-start(bf16[256,384]{1,0:T(8,128)(2,1)S(1)} %select_bitcast_fusion.27), channel_id=1, source_target_pairs={{0,2},{2,0},{1,3},{3,1},{4,6},{6,4},{5,7},{7,5},{8,10},{10,8},{9,1... | collective-permute-start | bytes 589832 | tf_op jit(solution)/shard_map/ppermute | solution.py:76
  80.7 66.7 %collective-permute-start.4 = (bf16[2,256,2048]{2,1,0:T(8,128)(2,1)}, bf16[2,256,2048]{2,1,0:T(8,128)(2,1)}, u32[]{:S(2)}, u32[]{:S(2)}) collective-permute-start(bf16[2,256,2048]{2,1,0:T(8,128)(2,1)} %pad_maximum_fusion.4), channel_id=1, source_target_pairs={{0,1},{1,0},{2,3},{3,2},{4,5},{5,4},{6,7},{7,6},{8,9},{9,8},{10,11... | collective-permute-start | bytes 6291464 | tf_op jit(solution)/shard_map/ppermute | solution.py:83
  80.8 19.1 %collective-permute-start.1 = (bf16[2,256,384]{2,1,0:T(8,128)(2,1)S(1)}, bf16[2,256,384]{2,1,0:T(8,128)(2,1)S(1)}, u32[]{:S(2)}, u32[]{:S(2)}) collective-permute-start(bf16[2,256,384]{2,1,0:T(8,128)(2,1)S(1)} %pad_maximum_fusion.14), channel_id=1, source_target_pairs={{0,4},{4,0},{1,5},{5,1},{2,6},{6,2},{3,7},{7,3},{8,12},{12,8},{9,1... | collective-permute-start | bytes 1179656 | tf_op jit(solution)/shard_map/ppermute | solution.py:83
  101.0 43.6 %collective-permute-start.2 = (bf16[2,2,256,384]{3,2,1,0:T(8,128)(2,1)}, bf16[2,2,256,384]{3,2,1,0:T(8,128)(2,1)}, u32[]{:S(2)}, u32[]{:S(2)}) collective-permute-start(bf16[2,2,256,384]{3,2,1,0:T(8,128)(2,1)} %pad_maximum_fusion.10), channel_id=1, source_target_pairs={{0,1},{1,0},{2,3},{3,2},{4,5},{5,4},{6,7},{7,6},{8,9},{9,8},{10,11... | collective-permute-start | bytes 2359304 | tf_op jit(solution)/shard_map/ppermute | solution.py:83
  156.6 4.2 copy-start.7
  166.1 4.7 copy-start.17
  170.8 85.8 %copy-start.2 = (bf16[128,2048]{1,0:T(8,128)(2,1)S(1)}, bf16[128,2048]{1,0:T(8,128)(2,1)}, u32[]{:S(2)}) copy-start(bf16[128,2048]{1,0:T(8,128)(2,1)} %param.43) | copy-start | bytes 1572868
  170.8 311.6 %all-gather.12.cloned.1.call-start = ((), (), s32[]{:S(2)}) async-start(), calls=%async_computation.6 | async-start | bytes 4718592 | tf_op jit(solution)/shard_map/all_gather | solution.py:62
  261.2 233.0 %all-gather.14.cloned.1.call-start = ((), (), s32[]{:S(2)}) async-start(), calls=%async_computation.8 | async-start | bytes 4718592 | tf_op jit(solution)/shard_map/all_gather | solution.py:62
  271.0 25.6 %collective-permute-start.5 = (bf16[256,1408]{0,1:T(8,128)(2,1)S(1)}, bf16[256,1408]{0,1:T(8,128)(2,1)S(1)}, u32[]{:S(2)}, u32[]{:S(2)}) collective-permute-start(bf16[256,1408]{0,1:T(8,128)(2,1)S(1)} %select_bitcast_fusion.22), channel_id=1, source_target_pairs={{0,2},{2,0},{1,3},{3,1},{4,6},{6,4},{5,7},{7,5},{8,10},{10,8},{9,1... | collective-permute-start | bytes 2162696 | tf_op jit(solution)/shard_map/ppermute | solution.py:76
  297.1 79.6 %collective-permute-start.6 = (bf16[2,256,1408]{1,2,0:T(8,128)(2,1)S(1)}, bf16[2,256,1408]{1,2,0:T(8,128)(2,1)}, u32[]{:S(2)}, u32[]{:S(2)}) collective-permute-start(bf16[2,256,1408]{1,2,0:T(8,128)(2,1)S(1)} %pad_maximum_fusion.7), channel_id=1, source_target_pairs={{0,4},{4,0},{1,5},{5,1},{2,6},{6,2},{3,7},{7,3},{8,12},{12,8},{9,1... | collective-permute-start | bytes 4325384 | tf_op jit(solution)/shard_map/ppermute | solution.py:83
  301.4 90.8 %collective-permute-start.8 = (bf16[176,2048]{1,0:T(8,128)(2,1)}, bf16[176,2048]{1,0:T(8,128)(2,1)}, u32[]{:S(2)}, u32[]{:S(2)}) collective-permute-start(bf16[176,2048]{1,0:T(8,128)(2,1)} %dynamic-slice_bitcast_fusion), channel_id=1, source_target_pairs={{0,4},{4,0},{1,5},{5,1},{2,6},{6,2},{3,7},{7,3},{8,12},{12,8},{9,1... | collective-permute-start | bytes 2162696 | tf_op jit(solution)/shard_map/ppermute | solution.py:83
  301.6 304.6 %reduce-scatter.9.cloned.1.call-start = ((), (), s32[]{:S(2)}) async-start(), calls=%async_computation.9 | async-start | bytes 4718592 | tf_op jit(solution)/shard_map/reduce_scatter | solution.py:66
  378.6 92.1 %collective-permute-start.7 = (bf16[2,2,256,1408]{2,3,1,0:T(8,128)(2,1)S(1)}, bf16[2,2,256,1408]{2,3,1,0:T(8,128)(2,1)S(1)}, u32[]{:S(2)}, u32[]{:S(2)}) collective-permute-start(bf16[2,2,256,1408]{2,3,1,0:T(8,128)(2,1)S(1)} %pad_maximum_fusion.1), channel_id=1, source_target_pairs={{0,1},{1,0},{2,3},{3,2},{4,5},{5,4},{6,7},{7,6},{8,9},{9,8},{10,11... | collective-permute-start | bytes 8650760 | tf_op jit(solution)/shard_map/ppermute | solution.py:83
  393.8 76.4 %collective-permute-start.9 = (bf16[2,176,2048]{2,1,0:T(8,128)(2,1)S(1)}, bf16[2,176,2048]{2,1,0:T(8,128)(2,1)S(1)}, u32[]{:S(2)}, u32[]{:S(2)}) collective-permute-start(bf16[2,176,2048]{2,1,0:T(8,128)(2,1)S(1)} %pad_maximum_fusion.8), channel_id=1, source_target_pairs={{0,1},{1,0},{2,3},{3,2},{4,5},{5,4},{6,7},{7,6},{8,9},{9,8},{10,11... | collective-permute-start | bytes 4325384 | tf_op jit(solution)/shard_map/ppermute | solution.py:83
  470.6 23.5 %copy-start.15 = (bf16[2,2,176,2048]{3,2,0,1:T(8,128)(2,1)}, bf16[2,2,176,2048]{3,2,0,1:T(8,128)(2,1)S(1)}, u32[]{:S(2)}) copy-start(bf16[2,2,176,2048]{3,2,0,1:T(8,128)(2,1)S(1)} %pad_maximum_fusion.2) | copy-start | bytes 8650756
  494.1 11.1 copy-start.8
  513.5 92.7 %copy-start.3 = (bf16[128,2048]{1,0:T(8,128)(2,1)S(1)}, bf16[128,2048]{1,0:T(8,128)(2,1)}, u32[]{:S(2)}) copy-start(bf16[128,2048]{1,0:T(8,128)(2,1)} %reduce-scatter.5.cloned.1.call-done) | copy-start | bytes 1572868
  513.5 92.7 %copy-start.38 = (f32[128]{0:T(128)S(1)}, f32[128]{0:T(128)}, u32[]{:S(2)}) copy-start(f32[128]{0:T(128)} %copy-done.37) | copy-start | bytes 1540
  513.5 94.2 %copy-start.9 = (bf16[128,2048]{1,0:T(8,128)(2,1)S(1)}, bf16[128,2048]{1,0:T(8,128)(2,1)}, u32[]{:S(2)}) copy-start(bf16[128,2048]{1,0:T(8,128)(2,1)} %param.44) | copy-start | bytes 1572868
  513.5 94.2 %copy-start.42 = (f32[128]{0:T(128)S(1)}, f32[128]{0:T(128)}, u32[]{:S(2)}) copy-start(f32[128]{0:T(128)} %get-tuple-element.305) | copy-start | bytes 1540
  513.6 97.0 %copy-start.48 = (bf16[1024,704]{1,0:T(8,128)(2,1)S(1)}, bf16[1024,704]{1,0:T(8,128)(2,1)}, u32[]{:S(2)}) copy-start(bf16[1024,704]{1,0:T(8,128)(2,1)} %get-tuple-element.244) | copy-start | bytes 4325380
  513.6 286.9 %all-gather.16.cloned.1.call-start = ((), (), s32[]{:S(2)}) async-start(), calls=%async_computation.10 | async-start | bytes 4718592 | tf_op jit(solution)/shard_map/all_gather | solution.py:62
  607.7 8.2 copy-start.44
  610.1 354.7 %all-gather.18.cloned.1.call-start = ((), (), s32[]{:S(2)}) async-start(), calls=%async_computation.13 | async-start | bytes 3604480 | tf_op jit(solution)/shard_map/all_gather | solution.py:280
  615.9 2.9 copy-start.50
  615.9 2.9 copy-start.52
  616.3 3.5 copy-start.47
  617.6 32.7 %collective-permute-start.18 = (bf16[2,176,2048]{2,1,0:T(8,128)(2,1)}, bf16[2,176,2048]{2,1,0:T(8,128)(2,1)}, u32[]{:S(2)}, u32[]{:S(2)}) collective-permute-start(bf16[2,176,2048]{2,1,0:T(8,128)(2,1)} %select_bitcast_fusion.6), channel_id=1, source_target_pairs={{0,1},{1,0},{2,3},{3,2},{4,5},{5,4},{6,7},{7,6},{8,9},{9,8},{10,11... | collective-permute-start | bytes 4325384 | tf_op jit(solution)/shard_map/ppermute | solution.py:100
  641.6 70.6 %collective-permute-start.15 = (bf16[2,2,256,1408]{2,3,1,0:T(8,128)(2,1)}, bf16[2,2,256,1408]{2,3,1,0:T(8,128)(2,1)}, u32[]{:S(2)}, u32[]{:S(2)}) collective-permute-start(bf16[2,2,256,1408]{2,3,1,0:T(8,128)(2,1)} %select_bitcast_fusion), channel_id=1, source_target_pairs={{0,1},{1,0},{2,3},{3,2},{4,5},{5,4},{6,7},{7,6},{8,9},{9,8},{10,11... | collective-permute-start | bytes 8650760 | tf_op jit(solution)/shard_map/ppermute | solution.py:100
  652.5 32.3 %collective-permute-start.19 = (bf16[176,2048]{1,0:T(8,128)(2,1)S(1)}, bf16[176,2048]{1,0:T(8,128)(2,1)S(1)}, u32[]{:S(2)}, u32[]{:S(2)}) collective-permute-start(bf16[176,2048]{1,0:T(8,128)(2,1)S(1)} %select_bitcast_fusion.18), channel_id=1, source_target_pairs={{0,4},{4,0},{1,5},{5,1},{2,6},{6,2},{3,7},{7,3},{8,12},{12,8},{9,1... | collective-permute-start | bytes 2162696 | tf_op jit(solution)/shard_map/ppermute | solution.py:100
  686.1 283.8 %all-gather.22.cloned.1.call-start = ((), (), s32[]{:S(2)}) async-start(), calls=%async_computation.15 | async-start | bytes 7208960 | tf_op jit(solution)/shard_map/all_gather | solution.py:273
  717.0 63.4 %collective-permute-start.16 = (bf16[2,256,1408]{1,2,0:T(8,128)(2,1)S(1)}, bf16[2,256,1408]{1,2,0:T(8,128)(2,1)S(1)}, u32[]{:S(2)}, u32[]{:S(2)}) collective-permute-start(bf16[2,256,1408]{1,2,0:T(8,128)(2,1)S(1)} %select_bitcast_fusion.7), channel_id=1, source_target_pairs={{0,4},{4,0},{1,5},{5,1},{2,6},{6,2},{3,7},{7,3},{8,12},{12,8},{9,1... | collective-permute-start | bytes 4325384 | tf_op jit(solution)/shard_map/ppermute | solution.py:100
  781.1 17.3 %collective-permute-start.17 = (bf16[256,1408]{0,1:T(8,128)(2,1)S(1)}, bf16[256,1408]{0,1:T(8,128)(2,1)S(1)}, u32[]{:S(2)}, u32[]{:S(2)}) collective-permute-start(bf16[256,1408]{0,1:T(8,128)(2,1)S(1)} %select_bitcast_fusion.19), channel_id=1, source_target_pairs={{0,2},{2,0},{1,3},{3,1},{4,6},{6,4},{5,7},{7,5},{8,10},{10,8},{9,1... | collective-permute-start | bytes 2162696 | tf_op jit(solution)/shard_map/ppermute | solution.py:76
  800.2 216.5 %all-reduce.4.cloned.1.call-start = ((), (), s32[]{:S(2)}) async-start(), calls=%async_computation.12 | async-start | bytes 2097152 | tf_op jit(solution)/shard_map/psum | solution.py:290
  805.3 8.0 copy-start.12
  812.1 4.2 copy-start.6
  812.1 62.1 %collective-permute-start.13 = (bf16[2,256,2048]{2,1,0:T(8,128)(2,1)}, bf16[2,256,2048]{2,1,0:T(8,128)(2,1)}, u32[]{:S(2)}, u32[]{:S(2)}) collective-permute-start(bf16[2,256,2048]{2,1,0:T(8,128)(2,1)} %select_bitcast_fusion.3), channel_id=1, source_target_pairs={{0,1},{1,0},{2,3},{3,2},{4,5},{5,4},{6,7},{7,6},{8,9},{9,8},{10,11... | collective-permute-start | bytes 6291464 | tf_op jit(solution)/shard_map/ppermute | solution.py:100
  816.3 4.9 copy-start.25
  834.3 39.9 %copy-start.1 = (bf16[2,2,256,2048]{3,2,1,0:T(8,128)(2,1)S(1)}, bf16[2,2,256,2048]{3,2,1,0:T(8,128)(2,1)}, u32[]{:S(2)}) copy-start(bf16[2,2,256,2048]{3,2,1,0:T(8,128)(2,1)} %copy-done) | copy-start | bytes 12582916
  834.4 39.5 %collective-permute-start.10 = (bf16[2,2,256,384]{3,2,1,0:T(8,128)(2,1)S(1)}, bf16[2,2,256,384]{3,2,1,0:T(8,128)(2,1)S(1)}, u32[]{:S(2)}, u32[]{:S(2)}) collective-permute-start(bf16[2,2,256,384]{3,2,1,0:T(8,128)(2,1)S(1)} %select_bitcast_fusion.15), channel_id=1, source_target_pairs={{0,1},{1,0},{2,3},{3,2},{4,5},{5,4},{6,7},{7,6},{8,9},{9,8},{10,11... | collective-permute-start | bytes 2359304 | tf_op jit(solution)/shard_map/ppermute | solution.py:100
  877.2 69.3 %collective-permute-start.14 = (bf16[256,2048]{1,0:T(8,128)(2,1)S(1)}, bf16[256,2048]{1,0:T(8,128)(2,1)S(1)}, u32[]{:S(2)}, u32[]{:S(2)}) collective-permute-start(bf16[256,2048]{1,0:T(8,128)(2,1)S(1)} %select_bitcast_fusion.12), channel_id=1, source_target_pairs={{0,4},{4,0},{1,5},{5,1},{2,6},{6,2},{3,7},{7,3},{8,12},{12,8},{9,1... | collective-permute-start | bytes 3145736 | tf_op jit(solution)/shard_map/ppermute | solution.py:100
  883.3 62.2 %collective-permute-start.11 = (bf16[2,256,384]{2,1,0:T(8,128)(2,1)S(1)}, bf16[2,256,384]{2,1,0:T(8,128)(2,1)S(1)}, u32[]{:S(2)}, u32[]{:S(2)}) collective-permute-start(bf16[2,256,384]{2,1,0:T(8,128)(2,1)S(1)} %select_bitcast_fusion.23), channel_id=1, source_target_pairs={{0,4},{4,0},{1,5},{5,1},{2,6},{6,2},{3,7},{7,3},{8,12},{12,8},{9,1... | collective-permute-start | bytes 1179656 | tf_op jit(solution)/shard_map/ppermute | solution.py:100
  945.6 5.3 collective-permute-start.12
  948.0 4.1 copy-start.22
  948.0 71.5 %all-gather.20.cloned.1.call-start = ((), (), s32[]{:S(2)}) async-start(), calls=%async_computation.14 | async-start | bytes 1966080 | tf_op jit(solution)/shard_map/all_gather | solution.py:273
  951.8 145.0 %reduce-scatter.11.cloned.1.call-start = ((), (), s32[]{:S(2)}) async-start(), calls=%async_computation.11 | async-start | bytes 4718592 | tf_op jit(solution)/shard_map/reduce_scatter | solution.py:66
  956.5 231.3 %reduce-scatter.7.cloned.1.call-start = ((), (), s32[]{:S(2)}) async-start(), calls=%async_computation.7 | async-start | bytes 4718592 | tf_op jit(solution)/shard_map/reduce_scatter | solution.py:66
  1031.7 65.2 %copy-start.31 = (f32[1,2048]{1,0:T(1,128)S(1)}, f32[1,2048]{1,0:T(1,128)}, u32[]{:S(2)}) copy-start(f32[1,2048]{1,0:T(1,128)} %copy-done.30) | copy-start | bytes 24580
  1031.7 65.2 %copy-start.41 = (f32[128]{0:T(128)S(1)}, f32[128]{0:T(128)}, u32[]{:S(2)}) copy-start(f32[128]{0:T(128)} %copy-done.40) | copy-start | bytes 1540
  1033.5 154.3 %copy-start.4 = (bf16[128,2048]{1,0:T(8,128)(2,1)S(1)}, bf16[128,2048]{1,0:T(8,128)(2,1)}, u32[]{:S(2)}) copy-start(bf16[128,2048]{1,0:T(8,128)(2,1)} %reduce-scatter.5.cloned.1.call-done) | copy-start | bytes 1572868
  1033.5 154.3 %copy-start.10 = (bf16[128,2048]{1,0:T(8,128)(2,1)S(1)}, bf16[128,2048]{1,0:T(8,128)(2,1)}, u32[]{:S(2)}) copy-start(bf16[128,2048]{1,0:T(8,128)(2,1)} %param.44) | copy-start | bytes 1572868
  1033.6 154.3 %copy-start.11 = (bf16[128,2048]{1,0:T(8,128)(2,1)S(1)}, bf16[128,2048]{1,0:T(8,128)(2,1)}, u32[]{:S(2)}) copy-start(bf16[128,2048]{1,0:T(8,128)(2,1)} %reduce-scatter.9.cloned.1.call-done) | copy-start | bytes 1572868
  1033.6 154.3 %copy-start.39 = (f32[128]{0:T(128)S(1)}, f32[128]{0:T(128)}, u32[]{:S(2)}) copy-start(f32[128]{0:T(128)} %copy-done.37) | copy-start | bytes 1540
  1033.6 154.3 %copy-start.43 = (f32[128]{0:T(128)S(1)}, f32[128]{0:T(128)}, u32[]{:S(2)}) copy-start(f32[128]{0:T(128)} %get-tuple-element.305) | copy-start | bytes 1540
  1033.6 154.3 %copy-start.45 = (f32[128]{0:T(128)S(1)}, f32[128]{0:T(128)}, u32[]{:S(2)}) copy-start(f32[128]{0:T(128)} %copy-done.44) | copy-start | bytes 1540
  1033.6 154.3 %copy-start.46 = (f32[128]{0:T(128)S(1)}, f32[128]{0:T(128)}, u32[]{:S(2)}) copy-start(f32[128]{0:T(128)} %get-tuple-element.303) | copy-start | bytes 1540
  (21 other events, 30.2 us)
Sparse Core Ops, SparseCore 0:
  30.6 56.5 all-gather.9
  171.0 85.6 reduce-scatter.4
  261.3 45.1 all-gather.11
  307.9 91.1 all-gather.13
  513.7 92.5 reduce-scatter.8
  610.2 29.8 all-gather.15
  686.2 29.7 all-gather.17
  800.3 46.3 all-gather.21
  948.1 36.2 all-reduce.3
  986.4 20.8 all-gather.19
  1009.6 87.2 reduce-scatter.10
  1099.0 88.7 reduce-scatter.6

commit v3 on v2

--- a/solution.py
+++ b/solution.py
@@ -3,11 +3,15 @@
 import jax
 import jax.numpy as jnp
 from jax import lax
+from jax.experimental import pallas as pl
+from jax.experimental.pallas import tpu as pltpu
 from jax.sharding import Mesh, PartitionSpec as P
 
 KV = 4
 HD = 64
 PAIR = 2
+SQUARE_DEVICES = 8
+MESH = pl.DeviceIdType.MESH
 epsilon = 1e-05
 
 TP = ("rep", "zl")
@@ -106,6 +110,512 @@
         pieces = jnp.moveaxis(partial.reshape((PAIR, PAIR) + partial.shape[1:]), 1, 0)
         return halve(halve(pieces, "x"), "zh")
     return lax.psum_scatter(partial, HOLDERS, scatter_dimension=0, tiled=False)
+
+
+def neighbours():
+    r, zl = lax.axis_index("rep"), lax.axis_index("zl")
+    partner, across = r + 1 - 2 * lax.rem(r, 2), lax.rem(r + 2, 4)
+    return {
+        "core": {"rep": partner},
+        "low": {"zl": 1 - zl},
+        "y": {"rep": across},
+        "both": {"rep": across, "zl": 1 - zl},
+        "x": {"x": 1 - lax.axis_index("x")},
+        "high": {"zh": 1 - lax.axis_index("zh")},
+    }
+
+
+def meet(near, names):
+    barrier = pltpu.get_barrier_semaphore()
+    for name in names:
+        pl.semaphore_signal(barrier, 1, device_id=near[name], device_id_type=MESH)
+    pl.semaphore_wait(barrier, len(names))
+
+
+class Wires:
+    def __init__(self, near, send, recv, local):
+        self.near, self.sems, self.local_sems = near, (send, recv), local
+        self.used, self.used_local, self.sent, self.kept = 0, 0, [], []
+
+    def describe(self, source, target, name):
+        at = self.used
+        self.used += 1
+        return pltpu.make_async_remote_copy(
+            src_ref=source,
+            dst_ref=target,
+            send_sem=self.sems[0].at[at],
+            recv_sem=self.sems[1].at[at],
+            device_id=self.near[name],
+            device_id_type=MESH,
+        )
+
+    def push(self, source, target, name):
+        copy = self.describe(source, target, name)
+        copy.start()
+        self.sent.append(copy)
+        return copy
+
+    def keep(self, source, target):
+        copy = pltpu.make_async_copy(source, target, self.local_sems.at[self.used_local])
+        self.used_local += 1
+        copy.start()
+        self.kept.append(copy)
+        return copy
+
+    def finish(self):
+        for copy in self.sent:
+            copy.wait_send()
+        for copy in self.kept:
+            copy.wait()
+
+
+class Spread:
+    def __init__(self, wires, own, whole):
+        self.wires, self.own, self.whole = wires, own, whole
+        self.length = own.shape[0]
+        r, zl = lax.axis_index("rep"), lax.axis_index("zl")
+        self.slots = {
+            "own": r * PAIR + zl,
+            "low": r * PAIR + 1 - zl,
+            "y": lax.rem(r + 2, 4) * PAIR + zl,
+            "both": lax.rem(r + 2, 4) * PAIR + 1 - zl,
+        }
+
+    def part(self, kind, half=None):
+        if half is None:
+            return self.whole.at[pl.ds(self.slots[kind] * self.length, self.length)]
+        size = self.length // 2
+        return self.whole.at[pl.ds(self.slots[kind] * self.length + half * size, size)]
+
+    def start(self, keep=True):
+        push, size = self.wires.push, self.length // 2
+        halves = [self.own.at[pl.ds(half * size, size)] for half in range(2)]
+        self.low = [push(halves[h], self.part("own", h), "low") for h in (0, 1)]
+        self.y = [push(halves[h], self.part("own", h), "y") for h in (1, 0)][::-1]
+        self.core = push(self.own, self.part("own"), "core")
+        if keep:
+            self.wires.keep(self.own, self.part("own"))
+
+    def pass_on(self):
+        push = self.wires.push
+        self.low[0].wait_recv()
+        self.first = push(self.part("low", 0), self.part("low", 0), "y")
+        self.y[1].wait_recv()
+        self.second = push(self.part("y", 1), self.part("y", 1), "low")
+        self.low[1].wait_recv()
+        self.core_low = push(self.part("low"), self.part("low"), "core")
+        self.y[0].wait_recv()
+        self.core_y = push(self.part("y"), self.part("y"), "core")
+
+    def last(self):
+        self.first.wait_recv()
+        self.second.wait_recv()
+        self.core_both = self.wires.push(self.part("both"), self.part("both"), "core")
+
+    def end(self):
+        for copy in (self.core, self.core_low, self.core_y, self.core_both):
+            copy.wait_recv()
+
+
+SPREAD_COPIES = 10
+SQUARE = ("core", "low", "y", "both")
+
+
+class Gather:
+    def __init__(self, near, scratch):
+        self.near = near
+        self.mine, self.out_core, self.in_core, self.out_far, self.in_far, self.sems = scratch
+
+    def core_copy(self, kind):
+        return pltpu.make_async_remote_copy(
+            src_ref=self.out_core.at[kind],
+            dst_ref=self.in_core.at[kind],
+            send_sem=self.sems.at[0, kind],
+            recv_sem=self.sems.at[1, kind],
+            device_id=self.near["core"],
+            device_id_type=MESH,
+        )
+
+    def far_copy(self, kind):
+        r, zl = lax.axis_index("rep"), lax.axis_index("zl")
+        target = {"rep": lax.rem(r + 2 * (kind // 2), 4), "zl": lax.rem(zl + lax.rem(kind, 2), 2)}
+        return pltpu.make_async_remote_copy(
+            src_ref=self.out_far.at[kind],
+            dst_ref=self.in_far.at[kind],
+            send_sem=self.sems.at[2, kind],
+            recv_sem=self.sems.at[3, kind],
+            device_id=target,
+            device_id_type=MESH,
+        )
+
+    def slot(self, step):
+        r, zl = lax.axis_index("rep"), lax.axis_index("zl")
+        kind = step // 2
+        rep = lax.rem(r + 2 * (kind // 2), 4)
+        other = rep + 1 - 2 * lax.rem(rep, 2)
+        rep = jnp.where(lax.rem(step, 2) == 0, other, rep)
+        return rep * PAIR + lax.rem(zl + lax.rem(kind, 2), 2)
+
+    def put(self, step, partial):
+        kind = step // 2
+        width = self.mine.shape[1]
+        chunk = min(width, 512)
+
+        @pl.when(lax.rem(step, 2) == 0)
+        def _():
+            for at in range(0, width, chunk):
+                columns = slice(at, at + chunk)
+                self.out_core[kind, :, columns] = partial(columns).astype(jnp.bfloat16)
+            self.core_copy(kind).start()
+
+        @pl.when(lax.rem(step, 2) == 1)
+        def _():
+            for at in range(0, width, chunk):
+                columns = slice(at, at + chunk)
+                self.mine[:, columns] = partial(columns)
+            self.core_copy(kind).wait_recv()
+            total = self.mine[...] + self.in_core[kind].astype(jnp.float32)
+
+            @pl.when(kind == 0)
+            def _():
+                self.mine_total(total)
+
+            @pl.when(kind > 0)
+            def _():
+                self.out_far[kind] = total.astype(jnp.bfloat16)
+                self.far_copy(kind).start()
+
+    def mine_total(self, total):
+        self.out_far[0] = total.astype(jnp.bfloat16)
+
+    def total(self):
+        result = self.out_far[0].astype(jnp.float32)
+        for kind in range(1, 4):
+            self.far_copy(kind).wait_recv()
+            result = result + self.in_far[kind].astype(jnp.float32)
+        return result
+
+    def finish(self):
+        for kind in range(4):
+            self.core_copy(kind).wait_send()
+        for kind in range(1, 4):
+            self.far_copy(kind).wait_send()
+
+
+def gather_scratch(length, width):
+    return [
+        pltpu.VMEM((length, width), jnp.float32),
+        pltpu.VMEM((4, length, width), jnp.bfloat16),
+        pltpu.VMEM((4, length, width), jnp.bfloat16),
+        pltpu.VMEM((4, length, width), jnp.bfloat16),
+        pltpu.VMEM((4, length, width), jnp.bfloat16),
+        pltpu.SemaphoreType.DMA((4, 4)),
+    ]
+
+
+def turn(values, cos_table, sin_table):
+    wide = values.shape[1]
+    lane = lax.broadcasted_iota(jnp.int32, values.shape, 1)
+    other = jnp.where(
+        lax.rem(lane, HD) < HD // 2,
+        pltpu.roll(values, wide - HD // 2, 1),
+        pltpu.roll(values, HD // 2, 1),
+    )
+    return values * cos_table + other * sin_table
+
+
+def softmax_rows(query, key, causal, scale):
+    scores = contract_last(query, key) * scale
+    log_total = jnp.log(jnp.sum(jnp.where(causal, jnp.exp(scores), 0.0), axis=-1, keepdims=True))
+    return jnp.where(causal, jnp.exp(scores - log_total), 0.0)
+
+
+def causal_mask(length):
+    rows = lax.broadcasted_iota(jnp.int32, (length, length), 0)
+    return rows >= lax.broadcasted_iota(jnp.int32, (length, length), 1)
+
+
+def forward_kernel(
+    x_ref, gain_ref, attn_pack, mlp_pack, down_piece, out_piece, cot_ref, cos_ref, sin_ref,
+    attn_w, mlp_w, down_w, out_w, gains, hidden, cot_all, qkv, attended, mixed, hidden_two,
+    gain_slots, own_hidden, own_two, send, recv, local, *scratch,
+):
+    near = neighbours()
+    r, zl = lax.axis_index("rep"), lax.axis_index("zl")
+    zh, x = lax.axis_index("zh"), lax.axis_index("x")
+    length, width = x_ref.shape
+    rows, wide = attn_pack.shape[1:]
+    heads_wide = wide - 2 * HD
+    heads = heads_wide // HD
+    deep = down_piece.shape[0]
+    wires = Wires(near, send, recv, local)
+
+    def shard(high, low, side):
+        return (high * PAIR + low) * PAIR + side
+
+    def slot(ref, high, low, side):
+        return ref.at[pl.ds(shard(high, low, side) * rows, rows)]
+
+    def deep_slot(high, side):
+        return down_w.at[pl.ds((high * PAIR + side) * deep, deep)]
+
+    meet(near, SQUARE + ("x", "high"))
+
+    gain_own = gain_slots.at[(x * PAIR + zh) * PAIR + zl]
+    gain_low = wires.push(gain_ref, gain_own, "low")
+    attn_low = wires.push(attn_pack.at[1 - zl], slot(attn_w, zh, zl, x), "low")
+    attn_own_high = wires.push(attn_pack.at[zl], slot(attn_w, zh, zl, x), "high")
+    attn_own_x = wires.push(attn_pack.at[zl], slot(attn_w, zh, zl, x), "x")
+    gain_slots[(x * PAIR + zh) * PAIR + zl] = gain_ref[...]
+    wires.keep(attn_pack.at[zl], slot(attn_w, zh, zl, x))
+    origin_high, origin_x = r // PAIR, lax.rem(r, PAIR)
+    on_side, on_high = x == origin_x, zh == origin_high
+    out_high = wires.describe(out_piece, out_w, "high")
+    out_x = wires.describe(out_piece, out_w, "x")
+    out_x_later = pltpu.make_async_remote_copy(
+        src_ref=out_w,
+        dst_ref=out_w,
+        send_sem=wires.sems[0].at[wires.used - 1],
+        recv_sem=wires.sems[1].at[wires.used - 1],
+        device_id=near["x"],
+        device_id_type=MESH,
+    )
+    out_keep = pltpu.make_async_copy(out_piece, out_w, local.at[local.shape[0] - 1])
+
+    @pl.when(on_side & on_high)
+    def _():
+        out_high.start()
+        out_x.start()
+        out_keep.start()
+
+    x_float = x_ref[...].astype(jnp.float32)
+    rms_one = lax.rsqrt(jnp.mean(x_float * x_float, axis=-1, keepdims=True) + epsilon)
+
+    gain_low.wait_recv()
+    pair = gain_slots.at[pl.ds((x * PAIR + zh) * PAIR, PAIR)]
+    gain_high = wires.push(pair, pair, "high")
+    attn_low.wait_recv()
+    attn_low_high = wires.push(slot(attn_w, zh, 1 - zl, x), slot(attn_w, zh, 1 - zl, x), "high")
+    attn_low_x = wires.push(slot(attn_w, zh, 1 - zl, x), slot(attn_w, zh, 1 - zl, x), "x")
+    gain_high.wait_recv()
+    quad = gain_slots.at[pl.ds(x * PAIR * PAIR, PAIR * PAIR)]
+    gain_x = wires.push(quad, quad, "x")
+    gain_x.wait_recv()
+    for high in range(PAIR):
+        for low in range(PAIR):
+            for side in range(PAIR):
+                at = shard(high, low, side) * rows
+                gains[:, at : at + rows] = gain_slots[(side * PAIR + high) * PAIR + low]
+
+    own_hidden[...] = (x_float * rms_one * gains[0:1, :]).astype(jnp.bfloat16)
+    spread = Spread(wires, own_hidden, hidden)
+    spread.start(keep=False)
+    hidden[pl.ds(spread.slots["own"] * length, length), :] = own_hidden[...]
+
+    attn_own_high.wait_recv()
+    attn_high_x = wires.push(slot(attn_w, 1 - zh, zl, x), slot(attn_w, 1 - zh, zl, x), "x")
+    attn_low_high.wait_recv()
+    attn_both_x = wires.push(slot(attn_w, 1 - zh, 1 - zl, x), slot(attn_w, 1 - zh, 1 - zl, x), "x")
+
+    @pl.when(on_side & jnp.logical_not(on_high))
+    def _():
+        out_high.wait_recv()
+        out_x_later.start()
+
+    for copy in (attn_own_x, attn_low_x, attn_high_x, attn_both_x):
+        copy.wait_recv()
+
+    @pl.when(jnp.logical_not(on_side))
+    def _():
+        out_x.wait_recv()
+
+    @pl.when(on_side & on_high)
+    def _():
+        out_keep.wait()
+
+    wires.kept.pop(0).wait()
+
+    mlp_own_high = wires.push(mlp_pack.at[zl], slot(mlp_w, zh, zl, x), "high")
+    mlp_own_x = wires.push(mlp_pack.at[zl], slot(mlp_w, zh, zl, x), "x")
+    down_high = wires.push(down_piece, deep_slot(zh, x), "high")
+    down_x = wires.push(down_piece, deep_slot(zh, x), "x")
+    wires.keep(mlp_pack.at[zl], slot(mlp_w, zh, zl, x))
+    wires.keep(down_piece, deep_slot(zh, x))
+    mlp_low = wires.push(mlp_pack.at[1 - zl], slot(mlp_w, zh, zl, x), "low")
+
+    gather = Gather(near, scratch)
+    causal = causal_mask(length)
+    scale = HD ** (-0.5)
+
+    def sequence(step, _):
+        at = pl.multiple_of(gather.slot(step) * length, length)
+        raw = matmul(hidden[pl.ds(at, length), :], attn_w[...])
+        turned = turn(raw, cos_ref[...], sin_ref[...]).astype(jnp.bfloat16)
+        qkv[pl.ds(at, length), :] = turned
+        key, value = turned[:, heads_wide : heads_wide + HD], turned[:, heads_wide + HD :]
+        outs = []
+        for head in range(heads):
+            query = turned[:, head * HD : (head + 1) * HD]
+            weights = softmax_rows(query, key, causal, scale)
+            outs.append(matmul(weights.astype(jnp.bfloat16), value))
+        block = jnp.concatenate(outs, axis=1).astype(jnp.bfloat16)
+        attended[pl.ds(at, length), :] = block
+        gather.put(step, lambda columns: matmul(block, out_w[:, columns]))
+        return 0
+
+    spread.core.wait_recv()
+    lax.fori_loop(0, 2, sequence, 0)
+    spread.pass_on()
+    spread.core_low.wait_recv()
+    lax.fori_loop(2, 4, sequence, 0)
+    mlp_low.wait_recv()
+    mlp_low_high = wires.push(slot(mlp_w, zh, 1 - zl, x), slot(mlp_w, zh, 1 - zl, x), "high")
+    mlp_low_x = wires.push(slot(mlp_w, zh, 1 - zl, x), slot(mlp_w, zh, 1 - zl, x), "x")
+    spread.last()
+    spread.core_y.wait_recv()
+    spread.core_both.wait_recv()
+    cot_spread = Spread(wires, cot_ref, cot_all)
+    cot_spread.start()
+    lax.fori_loop(4, 8, sequence, 0)
+    mixed[...] = x_ref[...].astype(jnp.float32) + gather.total()
+    mixed_sum = mixed[...]
+    rms_two = lax.rsqrt(jnp.mean(mixed_sum * mixed_sum, axis=-1, keepdims=True) + epsilon)
+    own_two[...] = (mixed_sum * rms_two * gains[1:2, :]).astype(jnp.bfloat16)
+    two_spread = Spread(wires, own_two, hidden_two)
+    two_spread.start()
+    cot_spread.pass_on()
+    mlp_own_high.wait_recv()
+    mlp_high_x = wires.push(slot(mlp_w, 1 - zh, zl, x), slot(mlp_w, 1 - zh, zl, x), "x")
+    cot_spread.last()
+    two_spread.pass_on()
+    two_spread.last()
+    down_high.wait_recv()
+    down_both_x = wires.push(deep_slot(1 - zh, x), deep_slot(1 - zh, x), "x")
+    mlp_low_high.wait_recv()
+    mlp_both_x = wires.push(slot(mlp_w, 1 - zh, 1 - zl, x), slot(mlp_w, 1 - zh, 1 - zl, x), "x")
+    for copy in (mlp_own_x, mlp_low_x, mlp_high_x, mlp_both_x, down_x, down_both_x):
+        copy.wait_recv()
+    cot_spread.end()
+    two_spread.end()
+    gather.finish()
+
+    @pl.when(on_side)
+    def _():
+        out_x.wait_send()
+
+    @pl.when(on_side & on_high)
+    def _():
+        out_high.wait_send()
+
+    wires.finish()
+
+
+FORWARD_COPIES = 60
+
+
+def forward(x_rows, gain_rows, attn_pack, mlp_pack, down_piece, out_piece, cotangent, tables):
+    length, width = x_rows.shape
+    group = SQUARE_DEVICES
+    rows, wide = attn_pack.shape[1:]
+    heads_wide = wide - 2 * HD
+    deep = down_piece.shape[0]
+    bf16, f32 = jnp.bfloat16, jnp.float32
+    shapes = [
+        ((width, wide), bf16, True),
+        ((width, mlp_pack.shape[2]), bf16, False),
+        ((PAIR * PAIR * deep, width), bf16, False),
+        ((heads_wide, width), bf16, True),
+        ((8, width), f32, True),
+        ((group * length, width), bf16, True),
+        ((group * length, width), bf16, False),
+        ((group * length, wide), bf16, True),
+        ((group * length, heads_wide), bf16, True),
+        ((length, width), f32, True),
+        ((group * length, width), bf16, False),
+    ]
+    vmem = pl.BlockSpec(memory_space=pltpu.VMEM)
+    far = pl.BlockSpec(memory_space=pl.ANY)
+    return pl.pallas_call(
+        forward_kernel,
+        out_shape=[jax.ShapeDtypeStruct(shape, kind) for shape, kind, _ in shapes],
+        in_specs=[vmem] * 9,
+        out_specs=[vmem if near else far for _, _, near in shapes],
+        scratch_shapes=[
+            pltpu.VMEM((8, 8, rows), f32),
+            pltpu.VMEM((length, width), bf16),
+            pltpu.VMEM((length, width), bf16),
+            pltpu.SemaphoreType.DMA((FORWARD_COPIES,)),
+            pltpu.SemaphoreType.DMA((FORWARD_COPIES,)),
+            pltpu.SemaphoreType.DMA((8,)),
+        ]
+        + gather_scratch(length, width),
+        compiler_params=pltpu.CompilerParams(
+            collective_id=0, has_side_effects=True, vmem_limit_bytes=60 * 2**20
+        ),
+        name="forward",
+    )(x_rows, gain_rows, attn_pack, mlp_pack, down_piece, out_piece, cotangent, *tables)
+
+
+def spread_kernel(own, whole, send, recv, local):
+    near = neighbours()
+    meet(near, SQUARE)
+    wires = Wires(near, send, recv, local)
+    spread = Spread(wires, own, whole)
+    spread.start()
+    spread.pass_on()
+    spread.last()
+    spread.end()
+    wires.finish()
+
+
+def spread_rows(rows, call):
+    length, width = rows.shape
+    return pl.pallas_call(
+        spread_kernel,
+        out_shape=jax.ShapeDtypeStruct((SQUARE_DEVICES * length, width), rows.dtype),
+        in_specs=[pl.BlockSpec(memory_space=pltpu.VMEM)],
+        out_specs=pl.BlockSpec(memory_space=pl.ANY),
+        scratch_shapes=[
+            pltpu.SemaphoreType.DMA((SPREAD_COPIES,)),
+            pltpu.SemaphoreType.DMA((SPREAD_COPIES,)),
+            pltpu.SemaphoreType.DMA((1,)),
+        ],
+        compiler_params=pltpu.CompilerParams(collective_id=call, has_side_effects=True),
+        name="spread",
+    )(rows)
+
+
+def gather_kernel(partial, result, *scratch):
+    near = neighbours()
+    meet(near, SQUARE)
+    gather = Gather(near, scratch)
+    length = result.shape[0]
+
+    def block(step, _):
+        at = pl.multiple_of(gather.slot(step) * length, length)
+        gather.put(step, lambda columns: partial[pl.ds(at, length), columns].astype(jnp.float32))
+        return 0
+
+    for first in (6, 2, 4, 0):
+        lax.fori_loop(first, first + 2, block, 0)
+    result[...] = gather.total()
+    gather.finish()
+
+
+def gather_rows(partial, call):
+    length, width = partial.shape[0] // SQUARE_DEVICES, partial.shape[1]
+    vmem = pl.BlockSpec(memory_space=pltpu.VMEM)
+    return pl.pallas_call(
+        gather_kernel,
+        out_shape=jax.ShapeDtypeStruct((length, width), jnp.float32),
+        in_specs=[vmem],
+        out_specs=vmem,
+        scratch_shapes=gather_scratch(length, width),
+        compiler_params=pltpu.CompilerParams(
+            collective_id=call, has_side_effects=True, vmem_limit_bytes=40 * 2**20
+        ),
+        name="gather",
+    )(partial)
 
 
 def per_device(
@@ -329,6 +839,222 @@
     )
 
 
+def per_device_square(
+    block_input,
+    cotangent,
+    attn_gain,
+    query_weight,
+    key_weight,
+    value_weight,
+    out_weight,
+    mlp_gain,
+    gate_weight,
+    up_weight,
+    down_weight,
+):
+    length, width = block_input.shape
+    reps, xs = lax.axis_size("rep"), lax.axis_size("x")
+    high = lax.axis_size("zh")
+    holders = high * xs
+    group = reps * PAIR
+    r, zl, x = lax.axis_index("rep"), lax.axis_index("zl"), lax.axis_index("x")
+    shard = (lax.axis_index("zh") * PAIR + zl) * xs + x
+    rows = query_weight.shape[0]
+    heads_wide = query_weight.shape[1] // group
+    per_rep = holders // reps
+    hidden_piece = down_weight.shape[0] // reps
+    hidden_wide = holders * hidden_piece
+    heads = heads_wide // HD
+    scale_factor = HD ** (-0.5)
+
+    def own_rep(values, axis):
+        return lax.dynamic_index_in_dim(values, r, axis, keepdims=False)
+
+    def by_holder(values, axis):
+        shape = values.shape
+        cut = values.reshape(shape[:axis] + (high, PAIR, xs, -1) + shape[axis + 1 :])
+        cut = jnp.moveaxis(cut, axis + 1, 0)
+        return cut.reshape((PAIR,) + shape[:axis] + (holders, -1) + shape[axis + 1 :])
+
+    def query_columns(weight):
+        pieces = by_holder(weight, 1).reshape(PAIR, rows, reps, heads_wide)
+        return own_rep(pieces, 2)
+
+    def hidden_columns(weight):
+        pieces = by_holder(weight, 1).reshape(PAIR, rows, holders, reps, hidden_piece)
+        return own_rep(pieces, 3).reshape(PAIR, rows, hidden_wide)
+
+    key_heads = [
+        (((r * per_rep // xs) * PAIR + low) * xs * heads_wide // (per_rep * HD)) * KV
+        // (query_weight.shape[1] // HD)
+        for low in range(PAIR)
+    ]
+
+    def key_columns(weight):
+        pieces = weight.reshape(rows, KV, HD)
+        return jnp.stack(
+            [lax.dynamic_index_in_dim(pieces, k, 1, keepdims=False) for k in key_heads]
+        )
+
+    attn_pack = jnp.concatenate(
+        [query_columns(query_weight), key_columns(key_weight), key_columns(value_weight)], axis=2
+    )
+    mlp_pack = jnp.concatenate([hidden_columns(gate_weight), hidden_columns(up_weight)], axis=2)
+
+    cos_table, sin_table = rotary_tables(length, HD)
+    sign = jnp.where(jnp.arange(HD) < HD // 2, -1.0, 1.0)
+    turned = heads + 1
+    cos_wide = jnp.concatenate([jnp.tile(cos_table, (1, turned)), jnp.ones_like(cos_table)], axis=1)
+    sin_wide = jnp.concatenate(
+        [jnp.tile(sin_table * sign, (1, turned)), jnp.zeros_like(cos_table)], axis=1
+    )
+    gain_rows = jnp.zeros((8, rows), jnp.float32)
+    gain_rows = gain_rows.at[0].set(attn_gain.astype(jnp.float32))
+    gain_rows = gain_rows.at[1].set(mlp_gain.astype(jnp.float32))
+    (
+        attn_w, mlp_w, down_w, out_w, gains, hidden_one, cot_all, qkv, attended, mixed_sum, hidden_two,
+    ) = forward(
+        block_input,
+        gain_rows,
+        attn_pack,
+        mlp_pack,
+        own_rep(down_weight.reshape(reps, hidden_piece, width), 0),
+        out_weight,
+        cotangent,
+        (cos_wide, sin_wide),
+    )
+    gain_one, gain_two = gains[0], gains[1]
+
+    x_float = block_input.astype(jnp.float32)
+    rms_one = lax.rsqrt(jnp.mean(x_float * x_float, axis=-1, keepdims=True) + epsilon)
+    normed_one = x_float * rms_one
+
+    def rotary_back(grads):
+        return (
+            grads * cos_table[:, None, :] + rotate_back(grads * sin_table[:, None, :])
+        ).astype(jnp.bfloat16)
+
+    qkv = qkv.reshape(group, length, -1)
+    query_rot = qkv[..., :heads_wide].reshape(group, length, heads, HD)
+    key_rot = qkv[..., heads_wide : heads_wide + HD]
+    value_rows = qkv[..., heads_wide + HD :]
+    causal = jnp.arange(length)[:, None] >= jnp.arange(length)[None, :]
+
+    def product_of(spec, left, right):
+        return jnp.einsum(spec, left, right, preferred_element_type=jnp.float32)
+
+    scores = product_of("bigd,bjd->bgij", query_rot, key_rot) * scale_factor
+    log_total = jnp.log(jnp.sum(jnp.where(causal, jnp.exp(scores), 0.0), axis=-1))
+    weights = jnp.where(causal, jnp.exp(scores - log_total[..., None]), 0.0)
+    weights_bf = weights.astype(jnp.bfloat16)
+
+    rms_two = lax.rsqrt(jnp.mean(mixed_sum * mixed_sum, axis=-1, keepdims=True) + epsilon)
+    normed_two = mixed_sum * rms_two
+    gate_up = matmul(hidden_two, mlp_w)
+    gate_raw, up_raw = gate_up[:, :hidden_wide], gate_up[:, hidden_wide:]
+    sigmoid = jax.nn.sigmoid(gate_raw)
+    activated = gate_raw * sigmoid
+    product = (activated * up_raw).astype(jnp.bfloat16)
+    grad_product = contract_last(cot_all, down_w)
+    grad_gate = grad_product * up_raw * sigmoid * (1.0 + gate_raw * (1.0 - sigmoid))
+    grad_up = grad_product * activated
+    grad_both = jnp.concatenate([grad_gate, grad_up], axis=1).astype(jnp.bfloat16)
+    grad_hidden_two = gather_rows(contract_last(grad_both, mlp_w).astype(jnp.bfloat16), 1)
+    block_output = (mixed_sum + gather_rows(matmul(product, down_w).astype(jnp.bfloat16), 2)).astype(jnp.bfloat16)
+    down_local = contract_first(product, cot_all).astype(jnp.bfloat16)
+    mlp_local = contract_first(hidden_two, grad_both).astype(jnp.bfloat16)
+
+    grad_mixed = cotangent.astype(jnp.float32) + norm_back(
+        grad_hidden_two * gain_two[None, :], mixed_sum, rms_two
+    )
+
+    grad_mixed_bf = spread_rows(grad_mixed.astype(jnp.bfloat16), 3)
+    grad_attended = contract_last(grad_mixed_bf, out_w).astype(jnp.bfloat16)
+    out_local = contract_first(attended, grad_mixed_bf).astype(jnp.bfloat16)
+    grad_attended = grad_attended.reshape(group, length, heads, HD)
+    grad_weights = product_of("bigd,bjd->bgij", grad_attended, value_rows)
+    row_total = jnp.sum(weights * grad_weights, axis=-1, keepdims=True)
+    grad_scores = (weights * (grad_weights - row_total) * scale_factor).astype(jnp.bfloat16)
+    grad_query = rotary_back(product_of("bgij,bjd->bigd", grad_scores, key_rot))
+    grad_key = rotary_back(product_of("bgij,bigd->bjd", grad_scores, query_rot)[:, :, None])
+    grad_value = product_of("bgij,bigd->bjd", weights_bf, grad_attended).astype(jnp.bfloat16)
+    grad_attn = jnp.concatenate(
+        [
+            grad_query.reshape(group * length, heads_wide),
+            grad_key.reshape(group * length, HD),
+            grad_value.reshape(group * length, HD),
+        ],
+        axis=1,
+    )
+    grad_hidden_one = gather_rows(contract_last(grad_attn, attn_w).astype(jnp.bfloat16), 4)
+    attn_local = contract_first(hidden_one, grad_attn).astype(jnp.bfloat16)
+    input_grad = grad_mixed + norm_back(
+        grad_hidden_one * gain_one[None, :], x_float, rms_one
+    )
+
+    def to_owner(partial):
+        pieces = partial.reshape(high, PAIR, xs, rows, -1)
+        pieces = jnp.swapaxes(pieces, 1, 2).reshape(holders, PAIR, rows, -1)
+        pieces = swap(scatter_holders(pieces), "zl")
+        return lax.all_gather(pieces, "rep", axis=0).astype(jnp.float32)
+
+    def from_holder(values):
+        cut = values.reshape(PAIR, rows, high, xs, -1)
+        return cut.transpose(1, 2, 0, 3, 4).reshape(rows, -1)
+
+    down_grad = scatter_holders(down_local.reshape(holders, hidden_piece, width))
+    down_grad = lax.all_gather(down_grad, "rep", axis=0, tiled=True).astype(jnp.float32)
+    mlp_grad = to_owner(mlp_local).reshape(reps, PAIR, rows, 2, holders, hidden_piece)
+    mlp_grad = mlp_grad.transpose(3, 1, 2, 4, 0, 5)
+    gate_grad, up_grad = from_holder(mlp_grad[0]), from_holder(mlp_grad[1])
+    out_padded = jnp.where(
+        (jnp.arange(reps) == r)[:, None, None],
+        out_local.reshape(1, per_rep * rows, width),
+        jnp.zeros((), jnp.bfloat16),
+    )
+    out_padded = scatter_holders(out_padded.reshape(holders, rows, width))
+    out_grad = lax.psum(out_padded, "rep").astype(jnp.float32)
+    attn_grad = to_owner(attn_local)
+    query_grad = attn_grad[..., :heads_wide].transpose(1, 2, 0, 3)
+    query_grad = from_holder(query_grad.reshape(PAIR, rows, holders, -1))
+    key_value = attn_grad[..., heads_wide:]
+
+    def key_back(values):
+        total = jnp.zeros((KV, rows, HD), jnp.float32)
+        for rep in range(reps):
+            for low in range(PAIR):
+                head = (rep * per_rep // xs) * PAIR + low
+                head = head * xs * heads_wide // (per_rep * HD)
+                head = head * KV // (query_weight.shape[1] // HD)
+                total = total.at[head].add(values[rep, low])
+        return total.transpose(1, 0, 2).reshape(rows, -1)
+
+    key_grad, value_grad = key_back(key_value[..., :HD]), key_back(key_value[..., HD:])
+    gain_grads = lax.psum(
+        jnp.stack(
+            [
+                jnp.sum(grad_hidden_one * normed_one, axis=0),
+                jnp.sum(grad_hidden_two * normed_two, axis=0),
+            ]
+        ),
+        ("rep", "zh", "zl", "x"),
+    )
+    gain_grads = lax.dynamic_slice_in_dim(gain_grads, shard * rows, rows, axis=1)
+    return (
+        block_output,
+        input_grad,
+        query_grad,
+        key_grad,
+        value_grad,
+        out_grad,
+        gate_grad,
+        up_grad,
+        down_grad,
+        gain_grads[0],
+        gain_grads[1],
+    )
+
+
 def solution(mesh):
     reps, shards = mesh.shape["rep"], mesh.shape["shard"]
     xs = 1
@@ -339,6 +1065,7 @@
     tokens, matrix, vector = P(names, None), P(names[1:], None), P(names[1:])
     in_specs = (tokens, tokens, vector) + (matrix,) * 4 + (vector,) + (matrix,) * 3
     out_specs = (tokens, tokens) + (matrix,) * 7 + (vector,) * 2
+    square = reps == 4 and shards // (PAIR * xs) == PAIR and xs == PAIR
     return jax.shard_map(
-        per_device, mesh=cube, in_specs=in_specs, out_specs=out_specs, check_vma=False
-    )
+        per_device_square if square else per_device, mesh=cube, in_specs=in_specs, out_specs=out_specs, check_vma=False
+    )

time: 1210 us -> 896 us (0.74)
  waiting for transfers between devices: 818 us -> 214 us
  Pallas kernels: 0 us -> 384 us
  matrix products: 90.6 us -> 63.6 us
  other arithmetic: 85.4 us -> 61.5 us
  blocking collectives: 59.6 us -> 38.7 us
  starting transfers between devices: 26.2 us -> 6.9 us
    pallas_call x0 -> x5, Pallas kernels: none -> 384 us  [the longest x1 262 us: forward(): pl.pallas_call(forward_kernel, out_shape=[jax.ShapeDtypeStruct(shape, kin...]
    reduce_scatter x4 -> x0, waiting for transfers between devices: 282 us -> none  [scatter_tokens(): lax.psum_scatter(partial.astype(jnp.bfloat16), TP, scatter_dimension=0, t...]
    ppermute x8 -> x0, waiting for transfers between devices: 239 us -> none  [exchange(): came = lax.ppermute(piece, axis, SWAP)]
    ppermute x4 -> x2, waiting for transfers between devices: 70.4 us -> 16.6 us  [swap(): came = lax.ppermute(jnp.where(first, pieces[1], pieces[0]), axis, SWAP)]
    ppermute x8, waiting for transfers between devices: 226 us -> 197 us  [halve(): came = lax.ppermute(jnp.where(first, pieces[1], pieces[0]), axis, SWAP)]
    all_gather x1 -> x0, blocking collectives: 17.9 us -> none  [per_device(): lax.all_gather(jnp.stack([attn_gain, mlp_gain]), ('zh', 'zl', 'x'), axis=...]
    another operation x20 -> x2, other arithmetic: 17.3 us -> 0.67 us  [the longest x14 14.1 us: exchange(): jnp.stack([jnp.where(first, piece, came), jnp.where(first, came, piece)])]
    dot_general x4 -> x2, matrix products: 27.8 us -> 14.7 us  [matmul(): return jnp.dot(left, right, preferred_element_type=jnp.float32)]
  transfers between devices with their start and end apart: 32 -> 14, of which waited for: 20 -> 6; matrix products, arithmetic and copies ran while one was open for 18% -> 9% of each run, Pallas kernels for 0% -> 5%
where the time goes in v3:
time: 896 us; the launch traced here: 889 us
  Pallas kernels  384 us (43%)
  waiting for transfers between devices  214 us (24%)
  local copies, waits for them, and re-layouts  106 us (12%)
  matrix products  63.6 us (7%)
  other arithmetic  61.5 us (7%)
  blocking collectives  38.7 us (4%)
  between operations  15 us (2%)
    pallas_call x1, Pallas kernels, forward(): pl.pallas_call(forward_kernel, out_shape=[jax.ShapeDtypeStruct(shape, kin...  262 us
    ppermute x8, waiting for transfers between devices, halve(): came = lax.ppermute(jnp.where(first, pieces[1], pieces[0]), axis, SWAP)  197 us
    pallas_call x3, Pallas kernels, gather_rows(): pl.pallas_call(gather_kernel, out_shape=jax.ShapeDtypeStruct((length, wid...  98.5 us
    psum x1, blocking collectives, per_device_square(): lax.psum(jnp.stack([jnp.sum(grad_hidden_one * normed_one, axis=0), jnp.su...  38.7 us
    unnamed x81, local copies, waits for them, and re-layouts  34.6 us
    pallas_call x1, Pallas kernels, spread_rows(): pl.pallas_call(spread_kernel, out_shape=jax.ShapeDtypeStruct((SQUARE_DEVI...  23.3 us
    dot_general x4, matrix products, contract_first(): lax.dot_general(left, right, (((0,), (0,)), ((), ())), preferred_element_...  18.6 us
    dot_general x4, matrix products, contract_last(): lax.dot_general(left, right, (((1,), (1,)), ((), ())), preferred_element_...  18.4 us
  transfers between devices with their start and end apart: 14, of which 6 were waited for; matrix products, arithmetic and copies ran while one was open for 9% of the time, Pallas kernels for 5%

profile of v3, /device:TPU:1, one launch (start us, length us, event | category | flops | bytes accessed | tf_op | source)
XLA Modules:
  0.0 889.2 jit_solution(8345760825282880688)
XLA Ops:
  11.4 2.6 reshape.790
  14.0 2.4 copy.97
  16.4 4.5 copy.106
  21.0 3.6 copy.107
  24.5 4.5 copy.104
  29.1 2.0 copy.105
  32.0 2.3 constant_dynamic-slice_fusion.1
  34.4 2.3 copy.109
  36.7 2.3 copy.108
  41.6 2.9 pad_maximum_fusion.3.mlp_pack
  46.7 261.9 %forward.1 = (bf16[2048,384]{1,0:T(8,128)(2,1)}, bf16[2048,1408]{1,0:T(8,128)(2,1)}, bf16[704,2048]{1,0:T(8,128)(2,1)}, bf16[256,2048]{1,0:T(8,128)(2,1)}, f32[8...) custom-call(bf16[128,2048]{1,0:T(8,128)(2,1)} %x_ref.1, ...), custom_call_target="tpu_custom_call" | custom-call | tf_op jit(solution)/shard_map/forward/pallas_call | solution.py:538
  308.7 11.1 %fusion.86 = f32[1024,1408]{1,0:T(8,128)S(1)} fusion(bf16[1024,2048]{1,0:T(8,128)(2,1)} %get-tuple-element.239, bf16[2048,1408]{1,0:T(8,128)(2,1)} %get-tuple-element.240), kind=kOutput, calls=%fused_computation.198 | convolution fusion | flops 5905580032 | bytes 15728640 | tf_op jit(solution)/shard_map/dot_general | solution.py:50
  319.8 4.2 multiply_convert_fusion.1
  325.2 6.9 convolution_convert_fusion.2.partial
  332.1 28.8 %gather.4 = f32[128,2048]{1,0:T(8,128)S(1)} custom-call(bf16[1024,2048]{1,0:T(8,128)(2,1)S(1)} %convolution_convert_fusion.2.partial), custom_call_target="tpu_custom_call" | custom-call | tf_op jit(solution)/shard_map/gather/pallas_call | solution.py:608
  362.4 3.6 convolution_convert_fusion.3.partial
  366.1 28.8 %gather.3 = f32[128,2048]{1,0:T(8,128)S(1)} custom-call(bf16[1024,2048]{1,0:T(8,128)(2,1)S(1)} %convolution_convert_fusion.3.partial), custom_call_target="tpu_custom_call" | custom-call | tf_op jit(solution)/shard_map/gather/pallas_call | solution.py:608
  395.8 2.0 copy.115
  397.8 2.8 fusion.40
  400.6 2.9 fusion.81
  403.5 23.3 %spread.1 = bf16[1024,2048]{1,0:T(8,128)(2,1)} custom-call(bf16[128,2048]{1,0:T(8,128)(2,1)} %get-tuple-element.275.own), custom_call_target="tpu_custom_call" | custom-call | tf_op jit(solution)/shard_map/spread/pallas_call | solution.py:573
  426.9 3.5 convolution_convert_fusion.7
  431.3 1.4 fusion.38
  432.8 3.7 fusion.8
  438.3 2.9 convolution_bitcast_fusion.2
  441.2 4.3 broadcast_multiply_fusion
  446.5 4.9 convolution_convert_fusion.5
  456.2 1.5 select_bitcast_fusion.1
  457.8 1.6 copy-done.3
  461.1 3.6 convolution_convert_fusion.4
  468.4 8.9 convolution_convert_fusion
  477.3 3.3 copy.161
  480.6 2.2 fusion.18
  482.9 1.5 collective-permute-start.1
  484.4 32.4 %collective-permute-done.3 = bf16[2,256,2048]{2,1,0:T(8,128)(2,1)} collective-permute-done((bf16[2,256,2048]{2,1,0:T(8,128)(2,1)}, bf16[2,256,2048]{2,1,0:T(8,128)(2,1)}, u32[]{:S(2)}, u32[]{:S(2)}) %collective-permute-start.3) | collective-permute-done | bytes 2097184 | tf_op jit(solution)/shard_map/ppermute | solution.py:104
  516.8 2.9 fusion.3
  519.8 1.5 collective-permute-start.4
  521.3 1.9 select_bitcast_fusion
  525.0 42.6 %collective-permute-done.4 = bf16[256,2048]{1,0:T(8,128)(2,1)S(1)} collective-permute-done((bf16[256,2048]{1,0:T(8,128)(2,1)S(1)}, bf16[256,2048]{1,0:T(8,128)(2,1)S(1)}, u32[]{:S(2)}, u32[]{:S(2)}) %collective-permute-start.4) | collective-permute-done | bytes 1048608 | tf_op jit(solution)/shard_map/ppermute | solution.py:104
  567.7 1.5 fusion.9
  570.8 2.2 fusion.5
  573.2 34.1 %collective-permute-done.9 = bf16[176,2048]{1,0:T(8,128)(2,1)S(1)} collective-permute-done((bf16[176,2048]{1,0:T(8,128)(2,1)S(1)}, bf16[176,2048]{1,0:T(8,128)(2,1)S(1)}, u32[]{:S(2)}, u32[]{:S(2)}) %collective-permute-start.9) | collective-permute-done | bytes 720928 | tf_op jit(solution)/shard_map/ppermute | solution.py:104
  609.0 23.6 %collective-permute-done.5 = bf16[2,2,256,1408]{3,2,1,0:T(8,128)(2,1)} collective-permute-done((bf16[2,2,256,1408]{3,2,1,0:T(8,128)(2,1)}, bf16[2,2,256,1408]{3,2,1,0:T(8,128)(2,1)}, u32[]{:S(2)}, u32[]{:S(2)}) %collective-permute-start.5) | collective-permute-done | bytes 2883616 | tf_op jit(solution)/shard_map/ppermute | solution.py:104
  632.5 4.8 fusion.2
  637.6 64.7 %collective-permute-done.6 = bf16[2,256,1408]{2,1,0:T(8,128)(2,1)S(1)} collective-permute-done((bf16[2,256,1408]{2,1,0:T(8,128)(2,1)S(1)}, bf16[2,256,1408]{2,1,0:T(8,128)(2,1)S(1)}, u32[]{:S(2)}, u32[]{:S(2)}) %collective-permute-start.6) | collective-permute-done | bytes 1441824 | tf_op jit(solution)/shard_map/ppermute | solution.py:104
  703.0 16.6 %collective-permute-done.7 = bf16[256,1408]{1,0:T(8,128)(2,1)S(1)} collective-permute-done((bf16[256,1408]{1,0:T(8,128)(2,1)S(1)}, bf16[256,1408]{1,0:T(8,128)(2,1)S(1)}, u32[]{:S(2)}, u32[]{:S(2)}) %collective-permute-start.7) | collective-permute-done | bytes 720928 | tf_op jit(solution)/shard_map/ppermute | solution.py:80
  721.1 3.8 convolution_convert_fusion.1.partial
  724.9 40.8 %gather.5 = f32[128,2048]{1,0:T(8,128)S(1)} custom-call(bf16[1024,2048]{1,0:T(8,128)(2,1)S(1)} %convolution_convert_fusion.1.partial), custom_call_target="tpu_custom_call" | custom-call | tf_op jit(solution)/shard_map/gather/pallas_call | solution.py:608
  766.4 38.7 %psum.15 = f32[2,2048]{1,0:T(2,128)S(1)} all-reduce(f32[2,2048]{1,0:T(2,128)S(1)} %pad_maximum_fusion.8), channel_id=1, replica_groups=mesh['rep'=4,'zh'=2,'zl'=2,'x'=2] {'rep','zh','zl','x'}, use_global_device_ids=true, to_apply=%region_9.10 | all-reduce | flops 4096 | bytes 32768 | tf_op jit(solution)/shard_map/psum | solution.py:1033
  805.7 1.4 fusion.25
  807.1 2.8 convert_element_type.197
  809.9 3.1 copy.127
  813.0 3.0 slice.647
  816.0 2.9 copy.128
  819.0 2.7 reshape.807
  830.6 5.1 convert_element_type.216
  835.7 8.2 copy.130
  843.9 8.5 convert_bitcast_fusion
  852.4 7.7 fusion.82
  860.5 3.1 copy.132
  863.6 6.2 copy.138
  869.8 3.2 copy.133
  873.0 3.1 copy.134
  876.1 6.4 copy.139
  (177 shorter events, 45.4 us)
Async XLA Ops:
  7.2 31.7 %copy-start = (bf16[704,2048]{1,0:T(8,128)(2,1)S(1)}, bf16[704,2048]{1,0:T(8,128)(2,1)}, u32[]{:S(2)}) copy-start(bf16[704,2048]{1,0:T(8,128)(2,1)} %param.57) | copy-start | bytes 8650756
  7.2 799.9 %all-reduce.7.cloned.1.call-start = ((), (), s32[]{:S(2)}) async-start(), calls=%async_computation | async-start | bytes 2097152 | tf_op jit(solution)/shard_map/psum | solution.py:1016
  40.6 0.6 copy-start.16
  41.5 5.2 copy-start.21
  308.6 11.1 %copy-start.23 = (bf16[1024,2048]{1,0:T(8,128)(2,1)S(1)}, bf16[1024,2048]{1,0:T(8,128)(2,1)}, u32[]{:S(2)}) copy-start(bf16[1024,2048]{1,0:T(8,128)(2,1)} %get-tuple-element.242) | copy-start | bytes 12582916
  308.6 11.1 %copy-start.25 = (bf16[704,2048]{1,0:T(8,128)(2,1)S(1)}, bf16[704,2048]{1,0:T(8,128)(2,1)}, u32[]{:S(2)}) copy-start(bf16[704,2048]{1,0:T(8,128)(2,1)} %get-tuple-element.241) | copy-start | bytes 8650756
  308.7 16.5 %slice-start = ((s8[5767168]{0:T(1024)(128)(4,1)}), s8[4194304]{0:T(1024)(128)(4,1)S(1)}, s32[]{:S(2)}) async-start(s8[5767168]{0:T(1024)(128)(4,1)} %bitcast.384), calls=%async_computation.4 | async-start | bytes 8388608
  319.8 5.4 slice-start.1
  324.0 1.1 copy-start.32
  324.0 8.1 copy-start.30
  324.0 38.4 %copy-start.28 = (bf16[1024,704]{1,0:T(8,128)(2,1)}, bf16[1024,704]{1,0:T(8,128)(2,1)S(1)}, u32[]{:S(2)}) copy-start(bf16[1024,704]{1,0:T(8,128)(2,1)S(1)} %get-tuple-element.281) | copy-start | bytes 4325380
  332.1 28.9 %copy-start.7 = (f32[128,2048]{1,0:T(8,128)S(1)}, f32[128,2048]{1,0:T(8,128)}, u32[]{:S(2)}) copy-start(f32[128,2048]{1,0:T(8,128)} %get-tuple-element.238) | copy-start | bytes 3145732
  366.0 28.9 %copy-start.13 = (bf16[1024,384]{1,0:T(8,128)(2,1)S(1)}, bf16[1024,384]{1,0:T(8,128)(2,1)}, u32[]{:S(2)}) copy-start(bf16[1024,384]{1,0:T(8,128)(2,1)} %get-tuple-element.244) | copy-start | bytes 2359300
  394.9 5.7 copy-start.14
  403.5 23.3 %copy-start.26 = (bf16[256,2048]{1,0:T(8,128)(2,1)S(1)}, bf16[256,2048]{1,0:T(8,128)(2,1)}, u32[]{:S(2)}) copy-start(bf16[256,2048]{1,0:T(8,128)(2,1)} %get-tuple-element.245) | copy-start | bytes 3145732
  432.8 5.6 copy-start.11
  432.8 5.6 copy-start.15
  436.5 1.3 copy-start.12
  441.2 4.4 copy-start.17
  445.6 0.8 copy-start.20
  446.5 4.9 copy-start.18
  451.4 3.0 copy-start.10
  451.4 3.1 copy-start.27
  451.6 4.2 copy-start.5
  452.6 28.0 %collective-permute-start = (bf16[2,2,256,384]{3,2,1,0:T(8,128)(2,1)}, bf16[2,2,256,384]{3,2,1,0:T(8,128)(2,1)}, u32[]{:S(2)}, u32[]{:S(2)}) collective-permute-start(bf16[2,2,256,384]{3,2,1,0:T(8,128)(2,1)} %select_bitcast_fusion.5), channel_id=1, source_target_pairs={{0,1},{1,0},{2,3},{3,2},{4,5},{5,4},{6,7},{7,6},{8,9},{9,8},{10,11... | collective-permute-start | bytes 2359304 | tf_op jit(solution)/shard_map/ppermute | solution.py:104
  456.2 3.1 copy-start.3
  456.2 4.4 copy-start.24
  456.2 4.9 copy-start.29
  459.3 57.5 %collective-permute-start.3 = (bf16[2,256,2048]{2,1,0:T(8,128)(2,1)}, bf16[2,256,2048]{2,1,0:T(8,128)(2,1)}, u32[]{:S(2)}, u32[]{:S(2)}) collective-permute-start(bf16[2,256,2048]{2,1,0:T(8,128)(2,1)} %select_bitcast_fusion.1), channel_id=1, source_target_pairs={{0,1},{1,0},{2,3},{3,2},{4,5},{5,4},{6,7},{7,6},{8,9},{9,8},{10,11... | collective-permute-start | bytes 6291464 | tf_op jit(solution)/shard_map/ppermute | solution.py:104
  464.7 2.1 copy-start.31
  464.7 2.4 copy-start.33
  464.9 3.5 copy-start.22
  466.2 104.6 %collective-permute-start.8 = (bf16[2,176,2048]{2,1,0:T(8,128)(2,1)}, bf16[2,176,2048]{2,1,0:T(8,128)(2,1)}, u32[]{:S(2)}, u32[]{:S(2)}) collective-permute-start(bf16[2,176,2048]{2,1,0:T(8,128)(2,1)} %select_bitcast_fusion.2), channel_id=1, source_target_pairs={{0,1},{1,0},{2,3},{3,2},{4,5},{5,4},{6,7},{7,6},{8,9},{9,8},{10,11... | collective-permute-start | bytes 4325384 | tf_op jit(solution)/shard_map/ppermute | solution.py:104
  477.3 3.4 copy-start.6
  480.6 40.7 %copy-start.2 = (bf16[2,2,2,256,1408]{4,3,1,0,2:T(8,128)(2,1)}, bf16[2,2,2,256,1408]{4,3,1,0,2:T(8,128)(2,1)S(1)}, u32[]{:S(2)}) copy-start(bf16[2,2,2,256,1408]{4,3,1,0,2:T(8,128)(2,1)S(1)} %copy.161) | copy-start | bytes 17301508
  480.6 36.2 %copy-start.4 = (bf16[2,2,256,2048]{3,2,1,0:T(8,128)(2,1)S(1)}, bf16[2,2,256,2048]{3,2,1,0:T(8,128)(2,1)}, u32[]{:S(2)}) copy-start(bf16[2,2,256,2048]{3,2,1,0:T(8,128)(2,1)} %copy-done.3) | copy-start | bytes 12582916
  482.9 40.3 %collective-permute-start.1 = (bf16[2,256,384]{2,1,0:T(8,128)(2,1)S(1)}, bf16[2,256,384]{2,1,0:T(8,128)(2,1)S(1)}, u32[]{:S(2)}, u32[]{:S(2)}) collective-permute-start(bf16[2,256,384]{2,1,0:T(8,128)(2,1)S(1)} %select_bitcast_fusion.8), channel_id=1, source_target_pairs={{0,4},{4,0},{1,5},{5,1},{2,6},{6,2},{3,7},{7,3},{8,12},{12,8},{9,1... | collective-permute-start | bytes 1179656 | tf_op jit(solution)/shard_map/ppermute | solution.py:104
  519.8 47.9 %collective-permute-start.4 = (bf16[256,2048]{1,0:T(8,128)(2,1)S(1)}, bf16[256,2048]{1,0:T(8,128)(2,1)S(1)}, u32[]{:S(2)}, u32[]{:S(2)}) collective-permute-start(bf16[256,2048]{1,0:T(8,128)(2,1)S(1)} %select_bitcast_fusion.4), channel_id=1, source_target_pairs={{0,4},{4,0},{1,5},{5,1},{2,6},{6,2},{3,7},{7,3},{8,12},{12,8},{9,1... | collective-permute-start | bytes 3145736 | tf_op jit(solution)/shard_map/ppermute | solution.py:104
  524.1 45.8 %collective-permute-start.2 = (bf16[256,384]{1,0:T(8,128)(2,1)}, bf16[256,384]{1,0:T(8,128)(2,1)S(1)}, u32[]{:S(2)}, u32[]{:S(2)}) collective-permute-start(bf16[256,384]{1,0:T(8,128)(2,1)} %select_bitcast_fusion.9), channel_id=1, source_target_pairs={{0,2},{2,0},{1,3},{3,1},{4,6},{6,4},{5,7},{7,5},{8,10},{10,8},{9,1... | collective-permute-start | bytes 589832 | tf_op jit(solution)/shard_map/ppermute | solution.py:80
  569.2 240.7 %all-gather.8.cloned.1.call-start = ((), (), s32[]{:S(2)}) async-start(), calls=%async_computation.2 | async-start | bytes 1966080 | tf_op jit(solution)/shard_map/all_gather | solution.py:999
  569.3 63.3 %collective-permute-start.5 = (bf16[2,2,256,1408]{3,2,1,0:T(8,128)(2,1)}, bf16[2,2,256,1408]{3,2,1,0:T(8,128)(2,1)}, u32[]{:S(2)}, u32[]{:S(2)}) collective-permute-start(bf16[2,2,256,1408]{3,2,1,0:T(8,128)(2,1)} %select_bitcast_fusion), channel_id=1, source_target_pairs={{0,1},{1,0},{2,3},{3,2},{4,5},{5,4},{6,7},{7,6},{8,9},{9,8},{10,11... | collective-permute-start | bytes 8650760 | tf_op jit(solution)/shard_map/ppermute | solution.py:104
  570.7 259.9 %all-gather.6.cloned.1.call-start = ((), (), s32[]{:S(2)}) async-start(), calls=%async_computation.1 | async-start | bytes 3604480 | tf_op jit(solution)/shard_map/all_gather | solution.py:1006
  573.1 34.2 %collective-permute-start.9 = (bf16[176,2048]{1,0:T(8,128)(2,1)S(1)}, bf16[176,2048]{1,0:T(8,128)(2,1)S(1)}, u32[]{:S(2)}, u32[]{:S(2)}) collective-permute-start(bf16[176,2048]{1,0:T(8,128)(2,1)S(1)} %select_bitcast_fusion.6), channel_id=1, source_target_pairs={{0,4},{4,0},{1,5},{5,1},{2,6},{6,2},{3,7},{7,3},{8,12},{12,8},{9,1... | collective-permute-start | bytes 2162696 | tf_op jit(solution)/shard_map/ppermute | solution.py:104
  608.5 227.2 %all-gather.10.cloned.1.call-start = ((), (), s32[]{:S(2)}) async-start(), calls=%async_computation.3 | async-start | bytes 7208960 | tf_op jit(solution)/shard_map/all_gather | solution.py:999
  637.5 64.8 %collective-permute-start.6 = (bf16[2,256,1408]{2,1,0:T(8,128)(2,1)S(1)}, bf16[2,256,1408]{2,1,0:T(8,128)(2,1)S(1)}, u32[]{:S(2)}, u32[]{:S(2)}) collective-permute-start(bf16[2,256,1408]{2,1,0:T(8,128)(2,1)S(1)} %select_bitcast_fusion.3), channel_id=1, source_target_pairs={{0,4},{4,0},{1,5},{5,1},{2,6},{6,2},{3,7},{7,3},{8,12},{12,8},{9,1... | collective-permute-start | bytes 4325384 | tf_op jit(solution)/shard_map/ppermute | solution.py:104
  702.9 16.7 %collective-permute-start.7 = (bf16[256,1408]{1,0:T(8,128)(2,1)S(1)}, bf16[256,1408]{1,0:T(8,128)(2,1)S(1)}, u32[]{:S(2)}, u32[]{:S(2)}) collective-permute-start(bf16[256,1408]{1,0:T(8,128)(2,1)S(1)} %select_bitcast_fusion.7), channel_id=1, source_target_pairs={{0,2},{2,0},{1,3},{3,1},{4,6},{6,4},{5,7},{7,5},{8,10},{10,8},{9,1... | collective-permute-start | bytes 2162696 | tf_op jit(solution)/shard_map/ppermute | solution.py:80
  719.8 1.3 copy-start.19
  724.9 40.9 %copy-start.8 = (bf16[128,2048]{1,0:T(8,128)(2,1)S(1)}, bf16[128,2048]{1,0:T(8,128)(2,1)}, u32[]{:S(2)}) copy-start(bf16[128,2048]{1,0:T(8,128)(2,1)} %x_ref.1) | copy-start | bytes 1572868
  724.9 80.8 %copy-start.9 = (f32[128,2048]{1,0:T(8,128)S(1)}, f32[128,2048]{1,0:T(8,128)}, u32[]{:S(2)}) copy-start(f32[128,2048]{1,0:T(8,128)} %get-tuple-element.276) | copy-start | bytes 3145732
  876.1 6.4 copy-start.1
Sparse Core Ops, SparseCore 0:
  569.3 34.8 all-reduce.6
  606.4 20.9 all-gather.7
  629.5 27.0 all-gather.5
  721.2 65.9 all-gather.9

commit v4 on v3

--- a/solution.py
+++ b/solution.py
@@ -222,13 +222,18 @@
 
 
 class Gather:
-    def __init__(self, near, scratch):
-        self.near = near
+    def __init__(self, near, scratch, source=None):
+        self.near, self.source = near, source
         self.mine, self.out_core, self.in_core, self.out_far, self.in_far, self.sems = scratch
 
     def core_copy(self, kind):
+        outgoing = self.out_core.at[kind]
+        if self.source is not None:
+            length = self.mine.shape[0]
+            at = pl.multiple_of(self.slot(2 * kind) * length, length)
+            outgoing = self.source.at[pl.ds(at, length)]
         return pltpu.make_async_remote_copy(
-            src_ref=self.out_core.at[kind],
+            src_ref=outgoing,
             dst_ref=self.in_core.at[kind],
             send_sem=self.sems.at[0, kind],
             recv_sem=self.sems.at[1, kind],
@@ -263,7 +268,7 @@
 
         @pl.when(lax.rem(step, 2) == 0)
         def _():
-            for at in range(0, width, chunk):
+            for at in range(0, width, chunk) if self.source is None else ():
                 columns = slice(at, at + chunk)
                 self.out_core[kind, :, columns] = partial(columns).astype(jnp.bfloat16)
             self.core_copy(kind).start()
@@ -588,7 +593,7 @@
 def gather_kernel(partial, result, *scratch):
     near = neighbours()
     meet(near, SQUARE)
-    gather = Gather(near, scratch)
+    gather = Gather(near, scratch, partial)
     length = result.shape[0]
 
     def block(step, _):
@@ -616,6 +621,357 @@
         ),
         name="gather",
     )(partial)
+
+
+def backward_kernel(
+    partial, mlp_local, down_local, hidden, attn_w, out_w, qkv, attended, mixed, cot_ref, x_ref,
+    gains, cos_ref, sin_ref,
+    mlp_out, down_out, attn_out, out_out, input_grad, gain_grads,
+    mlp_x, down_x, attn_x, out_x, mlp_high, down_high, attn_high, out_high, gain_in,
+    own_mixed, grad_mixed, grad_attn, attn_local, out_local, send, recv, local,
+    mine, out_core, in_core, out_far, in_far, sems_two, sems_one,
+):
+    near = neighbours()
+    r, zl = lax.axis_index("rep"), lax.axis_index("zl")
+    zh, x = lax.axis_index("zh"), lax.axis_index("x")
+    length, width = x_ref.shape
+    wide = attn_w.shape[1]
+    rows = mlp_x.shape[1]
+    heads_wide = wide - 2 * HD
+    heads = heads_wide // HD
+    deep = down_x.shape[1]
+    wires = Wires(near, send, recv, local)
+    push = wires.push
+    float32, bf16 = jnp.float32, jnp.bfloat16
+
+    def slot(ref, high, low, side):
+        return ref.at[pl.ds(pl.multiple_of(((high * PAIR + low) * PAIR + side) * rows, 16), rows)]
+
+    def deep_slot(high, side):
+        return down_local.at[pl.ds(pl.multiple_of((high * PAIR + side) * deep, 16), deep)]
+
+    def add_into(target, *others):
+        total = target[...].astype(float32)
+        for other in others:
+            total = total + other[...].astype(float32)
+        target[...] = total.astype(bf16)
+
+    meet(near, SQUARE + ("x", "high"))
+
+    mlp_x_copies, down_x_copies = {}, {}
+    for at, high in ((0, 1 - zh), (1, zh)):
+        for lower, low in ((0, 1 - zl), (1, zl)):
+            mlp_x_copies[at, lower] = push(
+                slot(mlp_local, high, low, 1 - x), mlp_x.at[2 * at + lower], "x"
+            )
+        down_x_copies[at] = push(deep_slot(high, 1 - x), down_x.at[at], "x")
+
+    def to_high(lower, low):
+        mlp_x_copies[0, lower].wait_recv()
+        add_into(mlp_x.at[lower], slot(mlp_local, 1 - zh, low, x))
+        return push(mlp_x.at[lower], mlp_high.at[lower], "high")
+
+    gather = Gather(near, (mine, out_core, in_core, out_far, in_far, sems_two), partial)
+
+    def block(step, _):
+        at = pl.multiple_of(gather.slot(step) * length, length)
+        gather.put(step, lambda columns: partial[pl.ds(at, length), columns].astype(float32))
+        return 0
+
+    for first in (6, 2, 4, 0):
+        lax.fori_loop(first, first + 2, block, 0)
+    grad_hidden = gather.total()
+    mixed_sum = mixed[...]
+    rms_two = lax.rsqrt(jnp.mean(mixed_sum * mixed_sum, axis=-1, keepdims=True) + epsilon)
+    gain_grads[1:2, :] = jnp.sum(grad_hidden * (mixed_sum * rms_two), axis=0, keepdims=True)
+    grad = cot_ref[...].astype(float32) + norm_back(
+        grad_hidden * gains[1:2, :], mixed_sum, rms_two
+    )
+    input_grad[...] = grad
+    own_mixed[...] = grad.astype(bf16)
+    spread = Spread(wires, own_mixed, grad_mixed)
+    spread.start(keep=False)
+    grad_mixed[pl.ds(pl.multiple_of(spread.slots["own"] * length, length), length), :] = own_mixed[...]
+    gather.finish()
+    mlp_high_copies = [to_high(0, 1 - zl)]
+
+    gather = Gather(near, (mine, out_core, in_core, out_far, in_far, sems_one))
+    causal = causal_mask(length)
+    scale = HD ** (-0.5)
+
+    def sequence(step, _):
+        at = pl.multiple_of(gather.slot(step) * length, length)
+        here = pl.ds(at, length)
+        grad_out = contract_last(grad_mixed[here, :], out_w[...]).astype(bf16)
+        turned = qkv[here, :]
+        key, value = turned[:, heads_wide : heads_wide + HD], turned[:, heads_wide + HD :]
+        grads = []
+        grad_key = jnp.zeros((length, HD), float32)
+        grad_value = jnp.zeros((length, HD), float32)
+        for head in range(heads):
+            own = slice(head * HD, (head + 1) * HD)
+            query, upper = turned[:, own], grad_out[:, own]
+            weights = softmax_rows(query, key, causal, scale)
+            grad_weights = contract_last(upper, value)
+            row_total = jnp.sum(weights * grad_weights, axis=-1, keepdims=True)
+            grad_scores = (weights * (grad_weights - row_total) * scale).astype(bf16)
+            grads.append(matmul(grad_scores, key))
+            grad_key = grad_key + contract_first(grad_scores, query)
+            grad_value = grad_value + contract_first(weights.astype(bf16), upper)
+        grads = jnp.concatenate(grads + [grad_key, grad_value], axis=1)
+        grads = turn(grads, cos_ref[...], -sin_ref[...]).astype(bf16)
+        grad_attn[here, :] = grads
+        gather.put(step, lambda columns: contract_last(grads, attn_w[columns, :]))
+        return 0
+
+    spread.core.wait_recv()
+    lax.fori_loop(0, 2, sequence, 0)
+    spread.pass_on()
+    mlp_high_copies.append(to_high(1, zl))
+    spread.core_low.wait_recv()
+    lax.fori_loop(2, 4, sequence, 0)
+    spread.last()
+    down_x_copies[0].wait_recv()
+    add_into(down_x.at[0], deep_slot(1 - zh, x))
+    down_high_copy = push(down_x.at[0], down_high, "high")
+    spread.core_y.wait_recv()
+    spread.core_both.wait_recv()
+    lax.fori_loop(4, 8, sequence, 0)
+
+    def own_columns(at, _):
+        here = pl.ds(pl.multiple_of(at * rows, rows), rows)
+        attn_local[here, :] = contract_first(hidden[:, here], grad_attn[...]).astype(bf16)
+        return 0
+
+    lax.fori_loop(0, width // rows, own_columns, 0)
+    attn_x_copies = {}
+    for at, high in ((0, 1 - zh), (1, zh)):
+        for lower, low in ((0, 1 - zl), (1, zl)):
+            attn_x_copies[at, lower] = push(
+                slot(attn_local, high, low, 1 - x), attn_x.at[2 * at + lower], "x"
+            )
+
+    def out_columns(at, _):
+        here = pl.ds(pl.multiple_of(at * 512, 512), 512)
+        out_local[:, here] = contract_first(attended[...], grad_mixed[:, here]).astype(bf16)
+        return 0
+
+    lax.fori_loop(0, width // 512, out_columns, 0)
+    on_side, on_high = x == lax.rem(r, PAIR), zh == r // PAIR
+    out_x_copy = wires.describe(out_local, out_x, "x")
+    out_high_copy = wires.describe(out_local, out_high, "high")
+
+    @pl.when(jnp.logical_not(on_side))
+    def _():
+        out_x_copy.start()
+
+    def to_group(out, piece_rows, column, forward):
+        here = out.at[pl.ds(pl.multiple_of(column * piece_rows, 16), piece_rows)]
+        return push(here, here, "y"), push(here, here, "core")
+
+    column_own, column_low = r * PAIR + zl, r * PAIR + 1 - zl
+    across = lax.rem(r + 2, 4)
+
+    def entry(out, column, size):
+        return out.at[pl.ds(pl.multiple_of(column * size, 16), size)]
+
+    def finish_first(x_copy, in_x, part, high_copy, in_high, out):
+        x_copy.wait_recv()
+        high_copy.wait_recv()
+        add_into(in_x, part, in_high)
+        return push(in_x, entry(out, column_own, rows), "low")
+
+    def finish_second(x_copy, in_x, part, high_copy, in_high, out, column, size):
+        x_copy.wait_recv()
+        high_copy.wait_recv()
+        add_into(in_x, part, in_high)
+        target = entry(out, column, size)
+        wires.keep(in_x, target)
+        return push(in_x, target, "y"), push(in_x, target, "core")
+
+    mlp_low = finish_first(
+        mlp_x_copies[1, 0], mlp_x.at[2], slot(mlp_local, zh, 1 - zl, x),
+        mlp_high_copies[0], mlp_high.at[0], mlp_out,
+    )
+
+    grad_hidden = gather.total()
+    x_float = x_ref[...].astype(float32)
+    rms_one = lax.rsqrt(jnp.mean(x_float * x_float, axis=-1, keepdims=True) + epsilon)
+    gain_grads[0:1, :] = jnp.sum(grad_hidden * (x_float * rms_one), axis=0, keepdims=True)
+    input_grad[...] = input_grad[...] + norm_back(grad_hidden * gains[0:1, :], x_float, rms_one)
+    gain_grads[2:8, :] = jnp.zeros((6, width), float32)
+
+    attn_high_copies = []
+    for lower, low in ((0, 1 - zl), (1, zl)):
+        attn_x_copies[0, lower].wait_recv()
+        add_into(attn_x.at[lower], slot(attn_local, 1 - zh, low, x))
+        attn_high_copies.append(push(attn_x.at[lower], attn_high.at[lower], "high"))
+
+    @pl.when(on_side)
+    def _():
+        out_x_copy.wait_recv()
+        add_into(out_local, out_x)
+
+        @pl.when(jnp.logical_not(on_high))
+        def _():
+            out_high_copy.start()
+
+    mlp_second = finish_second(
+        mlp_x_copies[1, 1], mlp_x.at[3], slot(mlp_local, zh, zl, x),
+        mlp_high_copies[1], mlp_high.at[1], mlp_out, column_own, rows,
+    )
+    for at, name in enumerate(("x", "high", "low", "y", "core")):
+        copy = push(gain_grads, gain_in.at[at], name)
+        copy.wait()
+        wires.sent.pop()
+        gain_grads[...] = gain_grads[...] + gain_in[at]
+    mlp_low.wait_recv()
+    mlp_third = to_group(mlp_out, rows, column_low, None)
+    down_second = finish_second(
+        down_x_copies[1], down_x.at[1], deep_slot(zh, x),
+        down_high_copy, down_high, down_out, r, deep,
+    )
+    mlp_second[0].wait_recv()
+    here = entry(mlp_out, across * PAIR + zl, rows)
+    last = [push(here, here, "core")]
+    mlp_third[0].wait_recv()
+    here = entry(mlp_out, across * PAIR + 1 - zl, rows)
+    last.append(push(here, here, "core"))
+    attn_low = finish_first(
+        attn_x_copies[1, 0], attn_x.at[2], slot(attn_local, zh, 1 - zl, x),
+        attn_high_copies[0], attn_high.at[0], attn_out,
+    )
+    attn_second = finish_second(
+        attn_x_copies[1, 1], attn_x.at[3], slot(attn_local, zh, zl, x),
+        attn_high_copies[1], attn_high.at[1], attn_out, column_own, rows,
+    )
+
+    holder = zh * PAIR + x
+    role = lax.rem(r - holder + 4, 4)
+    is_core = r == holder + 1 - 2 * lax.rem(holder, 2)
+    is_y = role == 2
+    out_core_copy = wires.describe(out_local, out_out, "core")
+    out_y_copy = wires.describe(out_local, out_out, "y")
+    out_y_later = pltpu.make_async_remote_copy(
+        src_ref=out_out,
+        dst_ref=out_out,
+        send_sem=send.at[wires.used - 1],
+        recv_sem=recv.at[wires.used - 1],
+        device_id=near["y"],
+        device_id_type=MESH,
+    )
+    out_keep = pltpu.make_async_copy(out_local, out_out, local.at[local.shape[0] - 1])
+
+    @pl.when(role == 0)
+    def _():
+        out_high_copy.wait_recv()
+        add_into(out_local, out_high)
+        out_core_copy.start()
+        out_y_copy.start()
+        out_keep.start()
+
+    attn_low.wait_recv()
+    attn_third = to_group(attn_out, rows, column_low, None)
+    down_second[0].wait_recv()
+    here = entry(down_out, across, deep)
+    last.append(push(here, here, "core"))
+    attn_second[0].wait_recv()
+    here = entry(attn_out, across * PAIR + zl, rows)
+    last.append(push(here, here, "core"))
+
+    @pl.when(is_core)
+    def _():
+        out_core_copy.wait_recv()
+        out_y_later.start()
+
+    attn_third[0].wait_recv()
+    here = entry(attn_out, across * PAIR + 1 - zl, rows)
+    last.append(push(here, here, "core"))
+
+    @pl.when((role != 0) & jnp.logical_not(is_core))
+    def _():
+        out_y_copy.wait_recv()
+
+    for copy in (mlp_second[1], mlp_third[1], down_second[1], attn_second[1], attn_third[1], *last):
+        copy.wait_recv()
+
+    @pl.when(role == 0)
+    def _():
+        out_core_copy.wait_send()
+        out_y_copy.wait_send()
+        out_keep.wait()
+
+    @pl.when(is_core)
+    def _():
+        out_y_later.wait_send()
+
+    @pl.when(jnp.logical_not(on_side))
+    def _():
+        out_x_copy.wait_send()
+
+    @pl.when(on_side & jnp.logical_not(on_high))
+    def _():
+        out_high_copy.wait_send()
+
+    gather.finish()
+    wires.finish()
+
+
+BACKWARD_COPIES = 64
+
+
+def backward(partial, mlp_local, down_local, saved, x_rows, cotangent, tables):
+    hidden, attn_w, out_w, qkv, attended, mixed, gains = saved
+    length, width = x_rows.shape
+    rows = width // SQUARE_DEVICES
+    wide, mlp_wide = attn_w.shape[1], mlp_local.shape[1]
+    heads_wide = wide - 2 * HD
+    deep = down_local.shape[0] // (PAIR * PAIR)
+    bf16, f32 = jnp.bfloat16, jnp.float32
+    shapes = [
+        ((width, mlp_wide), bf16, False),
+        ((PAIR * PAIR * deep, width), bf16, False),
+        ((width, wide), bf16, False),
+        ((heads_wide, width), bf16, False),
+        ((length, width), f32, True),
+        ((8, width), f32, True),
+    ]
+    vmem = pl.BlockSpec(memory_space=pltpu.VMEM)
+    far = pl.BlockSpec(memory_space=pl.ANY)
+    return pl.pallas_call(
+        backward_kernel,
+        out_shape=[jax.ShapeDtypeStruct(shape, kind) for shape, kind, _ in shapes],
+        in_specs=[vmem] * 14,
+        out_specs=[vmem if near else far for _, _, near in shapes],
+        scratch_shapes=[
+            pltpu.VMEM((4, rows, mlp_wide), bf16),
+            pltpu.VMEM((2, deep, width), bf16),
+            pltpu.VMEM((4, rows, wide), bf16),
+            pltpu.VMEM((heads_wide, width), bf16),
+            pltpu.VMEM((2, rows, mlp_wide), bf16),
+            pltpu.VMEM((deep, width), bf16),
+            pltpu.VMEM((2, rows, wide), bf16),
+            pltpu.VMEM((heads_wide, width), bf16),
+            pltpu.VMEM((5, 8, width), f32),
+            pltpu.VMEM((length, width), bf16),
+            pltpu.VMEM((SQUARE_DEVICES * length, width), bf16),
+            pltpu.VMEM((SQUARE_DEVICES * length, wide), bf16),
+            pltpu.VMEM((width, wide), bf16),
+            pltpu.VMEM((heads_wide, width), bf16),
+            pltpu.SemaphoreType.DMA((BACKWARD_COPIES,)),
+            pltpu.SemaphoreType.DMA((BACKWARD_COPIES,)),
+            pltpu.SemaphoreType.DMA((8,)),
+        ]
+        + gather_scratch(length, width)
+        + [pltpu.SemaphoreType.DMA((4, 4))],
+        compiler_params=pltpu.CompilerParams(
+            collective_id=5, has_side_effects=True, vmem_limit_bytes=63 * 2**20
+        ),
+        name="backward",
+    )(
+        partial, mlp_local, down_local, hidden, attn_w, out_w, qkv, attended, mixed, cotangent,
+        x_rows, gains, *tables,
+    )
 
 
 def per_device(
@@ -923,33 +1279,6 @@
         cotangent,
         (cos_wide, sin_wide),
     )
-    gain_one, gain_two = gains[0], gains[1]
-
-    x_float = block_input.astype(jnp.float32)
-    rms_one = lax.rsqrt(jnp.mean(x_float * x_float, axis=-1, keepdims=True) + epsilon)
-    normed_one = x_float * rms_one
-
-    def rotary_back(grads):
-        return (
-            grads * cos_table[:, None, :] + rotate_back(grads * sin_table[:, None, :])
-        ).astype(jnp.bfloat16)
-
-    qkv = qkv.reshape(group, length, -1)
-    query_rot = qkv[..., :heads_wide].reshape(group, length, heads, HD)
-    key_rot = qkv[..., heads_wide : heads_wide + HD]
-    value_rows = qkv[..., heads_wide + HD :]
-    causal = jnp.arange(length)[:, None] >= jnp.arange(length)[None, :]
-
-    def product_of(spec, left, right):
-        return jnp.einsum(spec, left, right, preferred_element_type=jnp.float32)
-
-    scores = product_of("bigd,bjd->bgij", query_rot, key_rot) * scale_factor
-    log_total = jnp.log(jnp.sum(jnp.where(causal, jnp.exp(scores), 0.0), axis=-1))
-    weights = jnp.where(causal, jnp.exp(scores - log_total[..., None]), 0.0)
-    weights_bf = weights.astype(jnp.bfloat16)
-
-    rms_two = lax.rsqrt(jnp.mean(mixed_sum * mixed_sum, axis=-1, keepdims=True) + epsilon)
-    normed_two = mixed_sum * rms_two
     gate_up = matmul(hidden_two, mlp_w)
     gate_raw, up_raw = gate_up[:, :hidden_wide], gate_up[:, hidden_wide:]
     sigmoid = jax.nn.sigmoid(gate_raw)
@@ -959,62 +1288,31 @@
     grad_gate = grad_product * up_raw * sigmoid * (1.0 + gate_raw * (1.0 - sigmoid))
     grad_up = grad_product * activated
     grad_both = jnp.concatenate([grad_gate, grad_up], axis=1).astype(jnp.bfloat16)
-    grad_hidden_two = gather_rows(contract_last(grad_both, mlp_w).astype(jnp.bfloat16), 1)
+    hidden_partial = contract_last(grad_both, mlp_w).astype(jnp.bfloat16)
     block_output = (mixed_sum + gather_rows(matmul(product, down_w).astype(jnp.bfloat16), 2)).astype(jnp.bfloat16)
     down_local = contract_first(product, cot_all).astype(jnp.bfloat16)
     mlp_local = contract_first(hidden_two, grad_both).astype(jnp.bfloat16)
 
-    grad_mixed = cotangent.astype(jnp.float32) + norm_back(
-        grad_hidden_two * gain_two[None, :], mixed_sum, rms_two
-    )
-
-    grad_mixed_bf = spread_rows(grad_mixed.astype(jnp.bfloat16), 3)
-    grad_attended = contract_last(grad_mixed_bf, out_w).astype(jnp.bfloat16)
-    out_local = contract_first(attended, grad_mixed_bf).astype(jnp.bfloat16)
-    grad_attended = grad_attended.reshape(group, length, heads, HD)
-    grad_weights = product_of("bigd,bjd->bgij", grad_attended, value_rows)
-    row_total = jnp.sum(weights * grad_weights, axis=-1, keepdims=True)
-    grad_scores = (weights * (grad_weights - row_total) * scale_factor).astype(jnp.bfloat16)
-    grad_query = rotary_back(product_of("bgij,bjd->bigd", grad_scores, key_rot))
-    grad_key = rotary_back(product_of("bgij,bigd->bjd", grad_scores, query_rot)[:, :, None])
-    grad_value = product_of("bgij,bigd->bjd", weights_bf, grad_attended).astype(jnp.bfloat16)
-    grad_attn = jnp.concatenate(
-        [
-            grad_query.reshape(group * length, heads_wide),
-            grad_key.reshape(group * length, HD),
-            grad_value.reshape(group * length, HD),
-        ],
-        axis=1,
-    )
-    grad_hidden_one = gather_rows(contract_last(grad_attn, attn_w).astype(jnp.bfloat16), 4)
-    attn_local = contract_first(hidden_one, grad_attn).astype(jnp.bfloat16)
-    input_grad = grad_mixed + norm_back(
-        grad_hidden_one * gain_one[None, :], x_float, rms_one
-    )
-
-    def to_owner(partial):
-        pieces = partial.reshape(high, PAIR, xs, rows, -1)
-        pieces = jnp.swapaxes(pieces, 1, 2).reshape(holders, PAIR, rows, -1)
-        pieces = swap(scatter_holders(pieces), "zl")
-        return lax.all_gather(pieces, "rep", axis=0).astype(jnp.float32)
+    mlp_grad, down_grad, attn_grad, out_grad, input_grad, gain_grads = backward(
+        hidden_partial,
+        mlp_local,
+        down_local,
+        (hidden_one, attn_w, out_w, qkv, attended, mixed_sum, gains),
+        block_input,
+        cotangent,
+        (cos_wide, sin_wide),
+    )
 
     def from_holder(values):
         cut = values.reshape(PAIR, rows, high, xs, -1)
         return cut.transpose(1, 2, 0, 3, 4).reshape(rows, -1)
 
-    down_grad = scatter_holders(down_local.reshape(holders, hidden_piece, width))
-    down_grad = lax.all_gather(down_grad, "rep", axis=0, tiled=True).astype(jnp.float32)
-    mlp_grad = to_owner(mlp_local).reshape(reps, PAIR, rows, 2, holders, hidden_piece)
+    down_grad = down_grad.astype(jnp.float32)
+    out_grad = out_grad.astype(jnp.float32)
+    mlp_grad = mlp_grad.astype(jnp.float32).reshape(reps, PAIR, rows, 2, holders, hidden_piece)
     mlp_grad = mlp_grad.transpose(3, 1, 2, 4, 0, 5)
     gate_grad, up_grad = from_holder(mlp_grad[0]), from_holder(mlp_grad[1])
-    out_padded = jnp.where(
-        (jnp.arange(reps) == r)[:, None, None],
-        out_local.reshape(1, per_rep * rows, width),
-        jnp.zeros((), jnp.bfloat16),
-    )
-    out_padded = scatter_holders(out_padded.reshape(holders, rows, width))
-    out_grad = lax.psum(out_padded, "rep").astype(jnp.float32)
-    attn_grad = to_owner(attn_local)
+    attn_grad = attn_grad.astype(jnp.float32).reshape(reps, PAIR, rows, -1)
     query_grad = attn_grad[..., :heads_wide].transpose(1, 2, 0, 3)
     query_grad = from_holder(query_grad.reshape(PAIR, rows, holders, -1))
     key_value = attn_grad[..., heads_wide:]
@@ -1030,15 +1328,6 @@
         return total.transpose(1, 0, 2).reshape(rows, -1)
 
     key_grad, value_grad = key_back(key_value[..., :HD]), key_back(key_value[..., HD:])
-    gain_grads = lax.psum(
-        jnp.stack(
-            [
-                jnp.sum(grad_hidden_one * normed_one, axis=0),
-                jnp.sum(grad_hidden_two * normed_two, axis=0),
-            ]
-        ),
-        ("rep", "zh", "zl", "x"),
-    )
     gain_grads = lax.dynamic_slice_in_dim(gain_grads, shard * rows, rows, axis=1)
     return (
         block_output,

time: 896 us -> 691 us (0.77)
  waiting for transfers between devices: 214 us -> 0 us
  Pallas kernels: 384 us -> 537 us
  other arithmetic: 61.5 us -> 9.23 us
  blocking collectives: 38.7 us -> 0 us
  matrix products: 63.6 us -> 40.7 us
  between operations: 15 us -> 1.57 us
  local copies, waits for them, and re-layouts: 106 us -> 96 us
    pallas_call x1, Pallas kernels: 23.3 us -> 246 us  [backward(): pl.pallas_call(backward_kernel, out_shape=[jax.ShapeDtypeStruct(shape, ki...]
    ppermute x10 -> x0, waiting for transfers between devices: 214 us -> none  [the longest x8 197 us: halve(): came = lax.ppermute(jnp.where(first, pieces[1], pieces[0]), axis, SWAP)]
    pallas_call x3 -> x1, Pallas kernels: 98.5 us -> 28.8 us  [gather_rows(): pl.pallas_call(gather_kernel, out_shape=jax.ShapeDtypeStruct((length, wid...]
    psum x1 -> x0, blocking collectives: 38.7 us -> none  [per_device_square(): lax.psum(jnp.stack([jnp.sum(grad_hidden_one * normed_one, axis=0), jnp.su...]
    transpose x0 -> x2, local copies, waits for them, and re-layouts: none -> 24.8 us  [per_device_square(): mlp_grad = mlp_grad.transpose(3, 1, 2, 4, 0, 5)]
    convert_element_type x12 -> x3, other arithmetic: 26.5 us -> 5.77 us  [the longest x1 3.3 us: per_device_square(): down_grad = down_grad.astype(jnp.float32)]
    dot_general x5 -> x0, matrix products: 11.9 us -> none  [product_of(): return jnp.einsum(spec, left, right, preferred_element_type=jnp.float32)]
    unnamed x81 -> x45, local copies, waits for them, and re-layouts: 34.6 us -> 27 us
  transfers between devices with their start and end apart: 14 -> 0, of which waited for: 6 -> 0; matrix products, arithmetic and copies ran while one was open for 9% -> 0% of each run, Pallas kernels for 5% -> 0%
where the time goes in v4:
time: 691 us; the launch traced here: 684 us
  Pallas kernels  537 us (78%)
  local copies, waits for them, and re-layouts  96 us (14%)
  matrix products  40.7 us (6%)
  other arithmetic  9.23 us (1%)
    pallas_call x1, Pallas kernels, forward(): pl.pallas_call(forward_kernel, out_shape=[jax.ShapeDtypeStruct(shape, kin...  262 us
    pallas_call x1, Pallas kernels, backward(): pl.pallas_call(backward_kernel, out_shape=[jax.ShapeDtypeStruct(shape, ki...  246 us
    pallas_call x1, Pallas kernels, gather_rows(): pl.pallas_call(gather_kernel, out_shape=jax.ShapeDtypeStruct((length, wid...  28.8 us
    unnamed x45, local copies, waits for them, and re-layouts  27 us
    transpose x2, local copies, waits for them, and re-layouts, per_device_square(): mlp_grad = mlp_grad.transpose(3, 1, 2, 4, 0, 5)  24.8 us
    slice x3, local copies, waits for them, and re-layouts, per_device_square(): gate_grad, up_grad = (from_holder(mlp_grad[0]), from_holder(mlp_grad[1]))  16.3 us
    dot_general x2, matrix products, matmul(): return jnp.dot(left, right, preferred_element_type=jnp.float32)  14.8 us

profile of v4, /device:TPU:1, one launch (start us, length us, event | category | flops | bytes accessed | tf_op | source)
XLA Modules:
  0.0 684.1 jit_solution(506735849167685942)
XLA Ops:
  0.6 0.7 reshape.654
  1.3 0.7 convert.18
  2.0 1.0 copy.36
  3.1 1.0 copy.33
  4.2 0.1 copy.38
  4.3 0.1 copy.37
  4.4 0.1 copy.35
  4.5 0.1 copy.34
  4.6 1.8 reshape.656
  6.5 0.2 copy.32
  6.7 0.9 maximum_maximum_fusion.attn_pack
  7.6 3.1 copy.41
  10.7 1.8 copy.42
  12.5 3.1 copy.39
  15.6 0.2 copy.40
  15.8 1.2 constant_dynamic-slice_fusion.1
  17.1 0.3 copy.44
  17.3 0.3 copy.43
  17.6 1.5 pad_maximum_fusion.3.mlp_pack
  19.1 2.0 dynamic-slice_bitcast_fusion.down_piece
  21.2 0.1 fusion.13
  21.4 0.1 copy.45
  21.6 0.7 concatenate.65.cos_ref
  22.3 0.1 copy.46
  22.4 0.7 concatenate.67.sin_ref
  23.1 261.9 %forward.1 = (bf16[2048,384]{1,0:T(8,128)(2,1)}, bf16[2048,1408]{1,0:T(8,128)(2,1)}, bf16[704,2048]{1,0:T(8,128)(2,1)}, bf16[256,2048]{1,0:T(8,128)(2,1)}, f32[8...) custom-call(bf16[128,2048]{1,0:T(8,128)(2,1)} %x_ref.3, ...), custom_call_target="tpu_custom_call" | custom-call | tf_op jit(solution)/shard_map/forward/pallas_call | solution.py:543
  285.1 11.1 %fusion.20 = f32[1024,1408]{1,0:T(8,128)S(1)} fusion(bf16[1024,2048]{1,0:T(8,128)(2,1)} %get-tuple-element.245, bf16[2048,1408]{1,0:T(8,128)(2,1)} %get-tuple-element.246), kind=kOutput, calls=%fused_computation.62 | convolution fusion | flops 5905580032 | bytes 15728640 | tf_op jit(solution)/shard_map/dot_general | solution.py:50
  296.2 4.3 multiply_convert_fusion.1
  300.5 3.6 convolution_convert_fusion.2.partial
  304.2 28.8 %gather.1 = f32[128,2048]{1,0:T(8,128)S(1)} custom-call(bf16[1024,2048]{1,0:T(8,128)(2,1)S(1)} %convolution_convert_fusion.2.partial), custom_call_target="tpu_custom_call" | custom-call | tf_op jit(solution)/shard_map/gather/pallas_call | solution.py:613
  333.0 0.9 add_convert_fusion
  333.9 8.3 %convolution_convert_fusion.1.partial = bf16[1024,2048]{1,0:T(8,128)(2,1)} fusion(bf16[2048,1408]{1,0:T(8,128)(2,1)S(1)} %bitcast.127, bf16[1024,704]{1,0:T(8,128)(2,1)S(1)} %get-tuple-element.275, bf16[1024,704]{1,0:T(8,128)(2,1)S(1)} %get-tuple-element.274), kind=kOutput, calls=%fused_computation.1 | convolution fusion | flops 5913444352 | bytes 12845056 | tf_op jit(solution)/shard_map/dot_general | solution.py:54
  342.1 9.0 %convolution_convert_fusion.mlp_local = bf16[2048,1408]{1,0:T(8,128)(2,1)} fusion(bf16[1024,2048]{1,0:T(8,128)(2,1)S(1)} %copy-done.6, bf16[1024,704]{1,0:T(8,128)(2,1)S(1)} %get-tuple-element.275, bf16[1024,704]{1,0:T(8,128)(2,1)S(1)} %get-tuple-element.274), kind=kOutput, calls=%fused_computation | convolution fusion | flops 5914230784 | bytes 12845056 | tf_op jit(solution)/shard_map/dot_general | solution.py:60
  351.1 4.5 convolution_convert_fusion.3.down_local
  355.6 245.8 %backward.1 = (bf16[2048,1408]{1,0:T(8,128)(2,1)}, bf16[704,2048]{1,0:T(8,128)(2,1)}, bf16[2048,384]{1,0:T(8,128)(2,1)}, bf16[256,2048]{1,0:T(8,128)(2,1)}, f32[128,2048]{1,0:T(8,128)}, /*index=5*/f32[8,2048]{1,0:T(8,128)}) custom-call(bf16[1024,2048]{1,0:T(8,128)(2,1)} %convolution_convert_fusion.1.partial, ...), custom_call_target="tpu_custom_call" | custom-call | tf_op jit(solution)/shard_map/backward/pallas_call | solution.py:941
  601.4 1.4 slice.498
  602.8 2.9 copy.93
  605.8 4.2 reshape.668
  610.0 0.9 fusion.18
  610.9 1.0 copy.76
  611.9 0.1 copy.77
  612.2 0.1 copy.79
  612.3 0.1 copy.80
  612.4 0.1 copy.81
  612.5 0.1 copy.82
  612.6 0.1 copy.83
  612.7 0.8 copy.71
  613.8 0.1 copy.86
  613.9 0.1 copy.87
  614.0 0.1 copy.88
  614.4 0.8 copy.72
  615.2 1.6 convert_element_type.35
  616.8 9.1 %copy.66 = f32[2048,1408]{0,1:T(8,128)} copy(bf16[2048,1408]{1,0:T(8,128)(2,1)} %get-tuple-element.258) | data formatting | bytes 17301504 | tf_op jit(solution)/shard_map/transpose | solution.py:1313
  625.9 15.7 %reshape.689 = f32[4,2,256,2,4,176]{2,1,0,5,4,3:T(2,128)} reshape(f32[2048,1408]{0,1:T(8,128)} %copy.66) | data formatting | bytes 23068672 | tf_op jit(solution)/shard_map/transpose | solution.py:1313
  641.6 9.9 %fusion.17 = (f32[1,2,256,4,4,176]{2,1,4,5,3,0:T(2,128)}, f32[1,2,256,4,4,176]{2,1,4,5,3,0:T(2,128)S(1)}) fusion(f32[2,2,256,4,4,176]{2,1,4,5,3,0:T(2,128)} %bitcast.93), kind=kLoop, calls=%fused_computation.59 | loop fusion | bytes 23068672 | tf_op jit(solution)/shard_map/slice | solution.py:1314
  651.5 1.9 copy.67
  653.4 3.2 copy.68
  656.6 6.2 copy.73
  662.8 4.5 copy.69
  667.3 3.2 copy.70
  670.5 6.4 copy.74
  676.8 3.3 convert_element_type.36
  680.1 1.4 fusion.19
  681.5 2.3 copy.110
  (52 shorter events, 0.9 us)
Async XLA Ops:
  2.0 5.6 copy-start.4
  285.0 11.2 %copy-start.5 = (bf16[1024,2048]{1,0:T(8,128)(2,1)S(1)}, bf16[1024,2048]{1,0:T(8,128)(2,1)}, u32[]{:S(2)}) copy-start(bf16[1024,2048]{1,0:T(8,128)(2,1)} %get-tuple-element.248) | copy-start | bytes 12582916
  285.0 11.2 %copy-start.7 = (bf16[704,2048]{1,0:T(8,128)(2,1)S(1)}, bf16[704,2048]{1,0:T(8,128)(2,1)}, u32[]{:S(2)}) copy-start(bf16[704,2048]{1,0:T(8,128)(2,1)} %get-tuple-element.247) | copy-start | bytes 8650756
  285.1 48.8 %slice-start = ((s8[5767168]{0:T(1024)(128)(4,1)}), s8[4194304]{0:T(1024)(128)(4,1)S(1)}, s32[]{:S(2)}) async-start(s8[5767168]{0:T(1024)(128)(4,1)} %bitcast.126), calls=%async_computation | async-start | bytes 8388608
  296.2 37.7 %slice-start.1 = ((s8[5767168]{0:T(1024)(128)(4,1)}), s8[1572864]{0:T(1024)(128)(4,1)S(1)}, s32[]{:S(2)}) async-start(s8[5767168]{0:T(1024)(128)(4,1)} %bitcast.126), calls=%async_computation.1 | async-start | bytes 3145728
  304.1 28.8 %copy-start.1 = (f32[128,2048]{1,0:T(8,128)S(1)}, f32[128,2048]{1,0:T(8,128)}, u32[]{:S(2)}) copy-start(f32[128,2048]{1,0:T(8,128)} %get-tuple-element.244.mixed) | copy-start | bytes 3145732
  333.9 8.3 %copy-start.6 = (bf16[1024,2048]{1,0:T(8,128)(2,1)S(1)}, bf16[1024,2048]{1,0:T(8,128)(2,1)}, u32[]{:S(2)}) copy-start(bf16[1024,2048]{1,0:T(8,128)(2,1)} %get-tuple-element.245) | copy-start | bytes 12582916
  605.8 4.2 copy-start
  612.2 3.1 copy-start.3
  670.5 6.4 copy-start.2

commit v5 on v4

--- a/solution.py
+++ b/solution.py
@@ -2,6 +2,7 @@
 
 import jax
 import jax.numpy as jnp
+import numpy as np
 from jax import lax
 from jax.experimental import pallas as pl
 from jax.experimental.pallas import tpu as pltpu
@@ -114,15 +115,29 @@
 
 def neighbours():
     r, zl = lax.axis_index("rep"), lax.axis_index("zl")
+    zh, x = lax.axis_index("zh"), lax.axis_index("x")
     partner, across = r + 1 - 2 * lax.rem(r, 2), lax.rem(r + 2, 4)
-    return {
+    near = {
         "core": {"rep": partner},
         "low": {"zl": 1 - zl},
         "y": {"rep": across},
-        "both": {"rep": across, "zl": 1 - zl},
-        "x": {"x": 1 - lax.axis_index("x")},
-        "high": {"zh": 1 - lax.axis_index("zh")},
+        "x": {"x": 1 - x},
+        "high": {"zh": 1 - zh},
     }
+    for at, (high, low, side) in enumerate(((0, 1, 1), (1, 0, 1), (1, 1, 0), (1, 1, 1))):
+        flip = {}
+        if high:
+            flip["zh"] = 1 - zh
+        if low:
+            flip["zl"] = 1 - zl
+        if side:
+            flip["x"] = 1 - x
+        near[f"peer{at}"] = flip
+    return near
+
+
+PEERS = ("low", "x", "high", "peer0", "peer1", "peer2", "peer3")
+SQUARE = ("core", "low", "y")
 
 
 def meet(near, names):
@@ -136,6 +151,11 @@
     def __init__(self, near, send, recv, local):
         self.near, self.sems, self.local_sems = near, (send, recv), local
         self.used, self.used_local, self.sent, self.kept = 0, 0, [], []
+
+    def done(self, *copies):
+        for copy in copies:
+            copy.wait()
+        self.kept = [kept for kept in self.kept if all(kept is not copy for copy in copies)]
 
     def describe(self, source, target, name):
         at = self.used
@@ -174,42 +194,38 @@
         self.wires, self.own, self.whole = wires, own, whole
         self.length = own.shape[0]
         r, zl = lax.axis_index("rep"), lax.axis_index("zl")
+        across = lax.rem(r + 2, 4)
         self.slots = {
             "own": r * PAIR + zl,
             "low": r * PAIR + 1 - zl,
-            "y": lax.rem(r + 2, 4) * PAIR + zl,
-            "both": lax.rem(r + 2, 4) * PAIR + 1 - zl,
+            "y": across * PAIR + zl,
+            "both": across * PAIR + 1 - zl,
         }
 
-    def part(self, kind, half=None):
-        if half is None:
-            return self.whole.at[pl.ds(self.slots[kind] * self.length, self.length)]
-        size = self.length // 2
-        return self.whole.at[pl.ds(self.slots[kind] * self.length + half * size, size)]
+    def part(self, kind):
+        start = pl.multiple_of(self.slots[kind] * self.length, 16)
+        return self.whole.at[pl.ds(start, self.length)]
 
     def start(self, keep=True):
-        push, size = self.wires.push, self.length // 2
-        halves = [self.own.at[pl.ds(half * size, size)] for half in range(2)]
-        self.low = [push(halves[h], self.part("own", h), "low") for h in (0, 1)]
-        self.y = [push(halves[h], self.part("own", h), "y") for h in (1, 0)][::-1]
+        push = self.wires.push
+        self.low = push(self.own, self.part("own"), "low")
+        self.y = push(self.own, self.part("own"), "y")
         self.core = push(self.own, self.part("own"), "core")
         if keep:
             self.wires.keep(self.own, self.part("own"))
 
-    def pass_on(self):
+    def pass_low(self):
         push = self.wires.push
-        self.low[0].wait_recv()
-        self.first = push(self.part("low", 0), self.part("low", 0), "y")
-        self.y[1].wait_recv()
-        self.second = push(self.part("y", 1), self.part("y", 1), "low")
-        self.low[1].wait_recv()
+        self.low.wait_recv()
+        self.both = push(self.part("low"), self.part("low"), "y")
         self.core_low = push(self.part("low"), self.part("low"), "core")
-        self.y[0].wait_recv()
-        self.core_y = push(self.part("y"), self.part("y"), "core")
-
-    def last(self):
-        self.first.wait_recv()
-        self.second.wait_recv()
+
+    def pass_y(self):
+        self.y.wait_recv()
+        self.core_y = self.wires.push(self.part("y"), self.part("y"), "core")
+
+    def pass_both(self):
+        self.both.wait_recv()
         self.core_both = self.wires.push(self.part("both"), self.part("both"), "core")
 
     def end(self):
@@ -217,8 +233,8 @@
             copy.wait_recv()
 
 
-SPREAD_COPIES = 10
-SQUARE = ("core", "low", "y", "both")
+SPREAD_COPIES = 7
+BOTH, ACROSS, OWN, LOW = 3, 2, 0, 1
 
 
 class Gather:
@@ -229,9 +245,7 @@
     def core_copy(self, kind):
         outgoing = self.out_core.at[kind]
         if self.source is not None:
-            length = self.mine.shape[0]
-            at = pl.multiple_of(self.slot(2 * kind) * length, length)
-            outgoing = self.source.at[pl.ds(at, length)]
+            outgoing = self.source.at[pl.ds(self.start_of(kind, True), self.mine.shape[0])]
         return pltpu.make_async_remote_copy(
             src_ref=outgoing,
             dst_ref=self.in_core.at[kind],
@@ -242,63 +256,64 @@
         )
 
     def far_copy(self, kind):
-        r, zl = lax.axis_index("rep"), lax.axis_index("zl")
-        target = {"rep": lax.rem(r + 2 * (kind // 2), 4), "zl": lax.rem(zl + lax.rem(kind, 2), 2)}
         return pltpu.make_async_remote_copy(
             src_ref=self.out_far.at[kind],
             dst_ref=self.in_far.at[kind],
             send_sem=self.sems.at[2, kind],
             recv_sem=self.sems.at[3, kind],
-            device_id=target,
+            device_id=self.near["low" if kind == LOW else "y"],
             device_id_type=MESH,
         )
 
-    def slot(self, step):
+    def start_of(self, kind, other):
         r, zl = lax.axis_index("rep"), lax.axis_index("zl")
-        kind = step // 2
         rep = lax.rem(r + 2 * (kind // 2), 4)
-        other = rep + 1 - 2 * lax.rem(rep, 2)
-        rep = jnp.where(lax.rem(step, 2) == 0, other, rep)
-        return rep * PAIR + lax.rem(zl + lax.rem(kind, 2), 2)
-
-    def put(self, step, partial):
-        kind = step // 2
-        width = self.mine.shape[1]
+        if other:
+            rep = rep + 1 - 2 * lax.rem(rep, 2)
+        slot = rep * PAIR + lax.rem(zl + kind % 2, 2)
+        return pl.multiple_of(slot * self.mine.shape[0], 16)
+
+    def run(self, partial):
+        length, width = self.mine.shape
         chunk = min(width, 512)
-
-        @pl.when(lax.rem(step, 2) == 0)
-        def _():
-            for at in range(0, width, chunk) if self.source is None else ():
-                columns = slice(at, at + chunk)
-                self.out_core[kind, :, columns] = partial(columns).astype(jnp.bfloat16)
+        order = (BOTH, ACROSS, OWN, LOW)
+
+        def send_core(kind):
+            if self.source is None:
+                start = self.start_of(kind, True)
+                for at in range(0, width, chunk):
+                    columns = slice(at, at + chunk)
+                    self.out_core[kind, :, columns] = partial(start, columns).astype(jnp.bfloat16)
             self.core_copy(kind).start()
 
-        @pl.when(lax.rem(step, 2) == 1)
-        def _():
+        def send_far(kind):
+            start = self.start_of(kind, False)
+            self.core_copy(kind).wait_recv()
+            if kind == LOW:
+                self.far_copy(BOTH).wait_recv()
             for at in range(0, width, chunk):
                 columns = slice(at, at + chunk)
-                self.mine[:, columns] = partial(columns)
-            self.core_copy(kind).wait_recv()
-            total = self.mine[...] + self.in_core[kind].astype(jnp.float32)
-
-            @pl.when(kind == 0)
-            def _():
-                self.mine_total(total)
-
-            @pl.when(kind > 0)
-            def _():
-                self.out_far[kind] = total.astype(jnp.bfloat16)
+                total = partial(start, columns) + self.in_core[kind, :, columns].astype(jnp.float32)
+                if kind == LOW:
+                    total = total + self.in_far[BOTH, :, columns].astype(jnp.float32)
+                if kind == OWN:
+                    self.mine[:, columns] = total
+                else:
+                    self.out_far[kind, :, columns] = total.astype(jnp.bfloat16)
+            if kind != OWN:
                 self.far_copy(kind).start()
 
-    def mine_total(self, total):
-        self.out_far[0] = total.astype(jnp.bfloat16)
+        send_core(order[0])
+        for before, kind in zip(order, order[1:]):
+            send_core(kind)
+            send_far(before)
+        send_far(order[-1])
 
     def total(self):
-        result = self.out_far[0].astype(jnp.float32)
-        for kind in range(1, 4):
-            self.far_copy(kind).wait_recv()
-            result = result + self.in_far[kind].astype(jnp.float32)
-        return result
+        self.far_copy(ACROSS).wait_recv()
+        self.far_copy(LOW).wait_recv()
+        result = self.mine[...] + self.in_far[ACROSS].astype(jnp.float32)
+        return result + self.in_far[LOW].astype(jnp.float32)
 
     def finish(self):
         for kind in range(4):
@@ -340,10 +355,25 @@
     return rows >= lax.broadcasted_iota(jnp.int32, (length, length), 1)
 
 
+def sequence_order(step):
+    r, zl = lax.axis_index("rep"), lax.axis_index("zl")
+    kind = step // 2
+    rep = lax.rem(r + 2 * (kind // 2), 4)
+    other = rep + 1 - 2 * lax.rem(rep, 2)
+    rep = jnp.where(lax.rem(step, 2) == 0, rep, other)
+    return rep * PAIR + lax.rem(zl + lax.rem(kind, 2), 2)
+
+
+def shard_of(high, low, side):
+    return (high * PAIR + low) * PAIR + side
+
+
 def forward_kernel(
-    x_ref, gain_ref, attn_pack, mlp_pack, down_piece, out_piece, cot_ref, cos_ref, sin_ref,
+    x_ref, gain_ref, query_w, key_w, value_w, cos_ref, sin_ref,
+    gate_far, up_far, down_far, out_piece, cot_far,
     attn_w, mlp_w, down_w, out_w, gains, hidden, cot_all, qkv, attended, mixed, hidden_two,
-    gain_slots, own_hidden, own_two, send, recv, local, *scratch,
+    gain_slots, own_hidden, own_two, attn_pack, mlp_pack, gate_near, up_near,
+    send, recv, local, *scratch,
 ):
     near = neighbours()
     r, zl = lax.axis_index("rep"), lax.axis_index("zl")
@@ -352,36 +382,64 @@
     rows, wide = attn_pack.shape[1:]
     heads_wide = wide - 2 * HD
     heads = heads_wide // HD
-    deep = down_piece.shape[0]
+    reps = lax.axis_size("rep")
+    hidden_piece = down_far.shape[0] // reps
+    deep = hidden_piece
     wires = Wires(near, send, recv, local)
-
-    def shard(high, low, side):
-        return (high * PAIR + low) * PAIR + side
+    push = wires.push
 
     def slot(ref, high, low, side):
-        return ref.at[pl.ds(shard(high, low, side) * rows, rows)]
+        return ref.at[pl.ds(pl.multiple_of(shard_of(high, low, side) * rows, 16), rows)]
 
     def deep_slot(high, side):
-        return down_w.at[pl.ds((high * PAIR + side) * deep, deep)]
-
-    meet(near, SQUARE + ("x", "high"))
-
-    gain_own = gain_slots.at[(x * PAIR + zh) * PAIR + zl]
-    gain_low = wires.push(gain_ref, gain_own, "low")
-    attn_low = wires.push(attn_pack.at[1 - zl], slot(attn_w, zh, zl, x), "low")
-    attn_own_high = wires.push(attn_pack.at[zl], slot(attn_w, zh, zl, x), "high")
-    attn_own_x = wires.push(attn_pack.at[zl], slot(attn_w, zh, zl, x), "x")
-    gain_slots[(x * PAIR + zh) * PAIR + zl] = gain_ref[...]
-    wires.keep(attn_pack.at[zl], slot(attn_w, zh, zl, x))
-    origin_high, origin_x = r // PAIR, lax.rem(r, PAIR)
-    on_side, on_high = x == origin_x, zh == origin_high
+        return down_w.at[pl.ds(pl.multiple_of((high * PAIR + side) * deep, 16), deep)]
+
+    gate_in = wires.keep(gate_far, gate_near)
+    up_in = wires.keep(up_far, up_near)
+    cot_spread = Spread(wires, cot_far, cot_all)
+    wires.keep(cot_far, cot_spread.part("own"))
+    down_piece = down_far.at[pl.ds(pl.multiple_of(r * deep, 16), deep)]
+    wires.keep(down_piece, deep_slot(zh, x))
+    for low in range(PAIR):
+        at = pl.multiple_of(shard_of(r // PAIR, low, lax.rem(r, PAIR)) * heads_wide, 128)
+        attn_pack[low, :, :heads_wide] = query_w[:, pl.ds(at, heads_wide)]
+        pair = pl.ds(pl.multiple_of((r // PAIR) * (PAIR * HD), 128), PAIR * HD)
+        own = slice(low * HD, (low + 1) * HD)
+        attn_pack[low, :, heads_wide : heads_wide + HD] = key_w[:, pair][:, own]
+        attn_pack[low, :, heads_wide + HD :] = value_w[:, pair][:, own]
+    meet(near, ("core", "y") + PEERS)
+
+    own_shard = shard_of(zh, zl, x)
+    gain_copies = [push(gain_ref, gain_slots.at[own_shard], name) for name in PEERS]
+    gain_slots[own_shard] = gain_ref[...]
+    attn_low = push(attn_pack.at[1 - zl], slot(attn_w, zh, zl, x), "low")
+    attn_own_high = push(attn_pack.at[zl], slot(attn_w, zh, zl, x), "high")
+    attn_own_x = push(attn_pack.at[zl], slot(attn_w, zh, zl, x), "x")
+    attn_keep = wires.keep(attn_pack.at[zl], slot(attn_w, zh, zl, x))
+
+    x_float = x_ref[...].astype(jnp.float32)
+    rms_one = lax.rsqrt(jnp.mean(x_float * x_float, axis=-1, keepdims=True) + epsilon)
+    for copy in gain_copies:
+        copy.wait_recv()
+    for at in range(SQUARE_DEVICES):
+        gains[:, at * rows : (at + 1) * rows] = gain_slots[at]
+    own_hidden[...] = (x_float * rms_one * gains[0:1, :]).astype(jnp.bfloat16)
+    spread = Spread(wires, own_hidden, hidden)
+    spread.start(keep=False)
+    hidden[pl.ds(pl.multiple_of(spread.slots["own"] * length, 16), length), :] = own_hidden[...]
+
+    attn_low.wait_recv()
+    attn_low_high = push(slot(attn_w, zh, 1 - zl, x), slot(attn_w, zh, 1 - zl, x), "high")
+    attn_low_x = push(slot(attn_w, zh, 1 - zl, x), slot(attn_w, zh, 1 - zl, x), "x")
+
+    on_side, on_high = x == lax.rem(r, PAIR), zh == r // PAIR
     out_high = wires.describe(out_piece, out_w, "high")
     out_x = wires.describe(out_piece, out_w, "x")
     out_x_later = pltpu.make_async_remote_copy(
         src_ref=out_w,
         dst_ref=out_w,
-        send_sem=wires.sems[0].at[wires.used - 1],
-        recv_sem=wires.sems[1].at[wires.used - 1],
+        send_sem=send.at[wires.used - 1],
+        recv_sem=recv.at[wires.used - 1],
         device_id=near["x"],
         device_id_type=MESH,
     )
@@ -393,67 +451,49 @@
         out_x.start()
         out_keep.start()
 
-    x_float = x_ref[...].astype(jnp.float32)
-    rms_one = lax.rsqrt(jnp.mean(x_float * x_float, axis=-1, keepdims=True) + epsilon)
-
-    gain_low.wait_recv()
-    pair = gain_slots.at[pl.ds((x * PAIR + zh) * PAIR, PAIR)]
-    gain_high = wires.push(pair, pair, "high")
-    attn_low.wait_recv()
-    attn_low_high = wires.push(slot(attn_w, zh, 1 - zl, x), slot(attn_w, zh, 1 - zl, x), "high")
-    attn_low_x = wires.push(slot(attn_w, zh, 1 - zl, x), slot(attn_w, zh, 1 - zl, x), "x")
-    gain_high.wait_recv()
-    quad = gain_slots.at[pl.ds(x * PAIR * PAIR, PAIR * PAIR)]
-    gain_x = wires.push(quad, quad, "x")
-    gain_x.wait_recv()
-    for high in range(PAIR):
-        for low in range(PAIR):
-            for side in range(PAIR):
-                at = shard(high, low, side) * rows
-                gains[:, at : at + rows] = gain_slots[(side * PAIR + high) * PAIR + low]
-
-    own_hidden[...] = (x_float * rms_one * gains[0:1, :]).astype(jnp.bfloat16)
-    spread = Spread(wires, own_hidden, hidden)
-    spread.start(keep=False)
-    hidden[pl.ds(spread.slots["own"] * length, length), :] = own_hidden[...]
-
     attn_own_high.wait_recv()
-    attn_high_x = wires.push(slot(attn_w, 1 - zh, zl, x), slot(attn_w, 1 - zh, zl, x), "x")
+    attn_high_x = push(slot(attn_w, 1 - zh, zl, x), slot(attn_w, 1 - zh, zl, x), "x")
+
+    wires.done(gate_in, up_in)
+    hidden_wide = mlp_pack.shape[2] // 2
+    for rep in range(reps):
+
+        @pl.when(r == rep)
+        def _(rep=rep):
+            def pack(step, _):
+                here = pl.ds(pl.multiple_of(step * 32, 32), 32)
+                for low in range(PAIR):
+                    for base, source in ((0, gate_near), (hidden_wide, up_near)):
+                        parts = []
+                        for high in range(PAIR):
+                            for side in range(PAIR):
+                                at = (shard_of(high, low, side) * reps + rep) * hidden_piece
+                                parts.append(source[here, at : at + hidden_piece])
+                        mlp_pack[low, here, base : base + hidden_wide] = jnp.concatenate(
+                            parts, axis=1
+                        )
+                return 0
+
+            lax.fori_loop(0, rows // 32, pack, 0)
+
     attn_low_high.wait_recv()
-    attn_both_x = wires.push(slot(attn_w, 1 - zh, 1 - zl, x), slot(attn_w, 1 - zh, 1 - zl, x), "x")
-
-    @pl.when(on_side & jnp.logical_not(on_high))
-    def _():
-        out_high.wait_recv()
-        out_x_later.start()
-
+    attn_both_x = push(slot(attn_w, 1 - zh, 1 - zl, x), slot(attn_w, 1 - zh, 1 - zl, x), "x")
+
+    mlp_own_high = push(mlp_pack.at[zl], slot(mlp_w, zh, zl, x), "high")
+    mlp_low = push(mlp_pack.at[1 - zl], slot(mlp_w, zh, zl, x), "low")
     for copy in (attn_own_x, attn_low_x, attn_high_x, attn_both_x):
         copy.wait_recv()
-
-    @pl.when(jnp.logical_not(on_side))
-    def _():
-        out_x.wait_recv()
-
-    @pl.when(on_side & on_high)
-    def _():
-        out_keep.wait()
-
-    wires.kept.pop(0).wait()
-
-    mlp_own_high = wires.push(mlp_pack.at[zl], slot(mlp_w, zh, zl, x), "high")
-    mlp_own_x = wires.push(mlp_pack.at[zl], slot(mlp_w, zh, zl, x), "x")
-    down_high = wires.push(down_piece, deep_slot(zh, x), "high")
-    down_x = wires.push(down_piece, deep_slot(zh, x), "x")
+    mlp_own_x = push(mlp_pack.at[zl], slot(mlp_w, zh, zl, x), "x")
+    down_x = push(down_piece, deep_slot(zh, x), "x")
     wires.keep(mlp_pack.at[zl], slot(mlp_w, zh, zl, x))
-    wires.keep(down_piece, deep_slot(zh, x))
-    mlp_low = wires.push(mlp_pack.at[1 - zl], slot(mlp_w, zh, zl, x), "low")
+    wires.done(attn_keep)
 
     gather = Gather(near, scratch)
     causal = causal_mask(length)
     scale = HD ** (-0.5)
 
     def sequence(step, _):
-        at = pl.multiple_of(gather.slot(step) * length, length)
+        at = pl.multiple_of(sequence_order(step) * length, length)
         raw = matmul(hidden[pl.ds(at, length), :], attn_w[...])
         turned = turn(raw, cos_ref[...], sin_ref[...]).astype(jnp.bfloat16)
         qkv[pl.ds(at, length), :] = turned
@@ -463,45 +503,66 @@
             query = turned[:, head * HD : (head + 1) * HD]
             weights = softmax_rows(query, key, causal, scale)
             outs.append(matmul(weights.astype(jnp.bfloat16), value))
-        block = jnp.concatenate(outs, axis=1).astype(jnp.bfloat16)
-        attended[pl.ds(at, length), :] = block
-        gather.put(step, lambda columns: matmul(block, out_w[:, columns]))
+        attended[pl.ds(at, length), :] = jnp.concatenate(outs, axis=1).astype(jnp.bfloat16)
         return 0
 
+    spread.pass_low()
+    spread.pass_y()
     spread.core.wait_recv()
     lax.fori_loop(0, 2, sequence, 0)
-    spread.pass_on()
     spread.core_low.wait_recv()
     lax.fori_loop(2, 4, sequence, 0)
+    down_high = push(down_piece, deep_slot(zh, x), "high")
+    spread.pass_both()
+    spread.core_y.wait_recv()
+    lax.fori_loop(4, 6, sequence, 0)
+
+    @pl.when(on_side & jnp.logical_not(on_high))
+    def _():
+        out_high.wait_recv()
+        out_x_later.start()
+
+    spread.core_both.wait_recv()
+    lax.fori_loop(6, 8, sequence, 0)
+
+    @pl.when(jnp.logical_not(on_side))
+    def _():
+        out_x.wait_recv()
+
+    @pl.when(on_side & on_high)
+    def _():
+        out_keep.wait()
+
+    gather.run(
+        lambda start, columns: matmul(attended[pl.ds(start, length), :], out_w[:, columns])
+    )
+    mlp_own_high.wait_recv()
+    mlp_high_x = push(slot(mlp_w, 1 - zh, zl, x), slot(mlp_w, 1 - zh, zl, x), "x")
     mlp_low.wait_recv()
-    mlp_low_high = wires.push(slot(mlp_w, zh, 1 - zl, x), slot(mlp_w, zh, 1 - zl, x), "high")
-    mlp_low_x = wires.push(slot(mlp_w, zh, 1 - zl, x), slot(mlp_w, zh, 1 - zl, x), "x")
-    spread.last()
-    spread.core_y.wait_recv()
-    spread.core_both.wait_recv()
-    cot_spread = Spread(wires, cot_ref, cot_all)
-    cot_spread.start()
-    lax.fori_loop(4, 8, sequence, 0)
+    mlp_low_high = push(slot(mlp_w, zh, 1 - zl, x), slot(mlp_w, zh, 1 - zl, x), "high")
+    mlp_low_x = push(slot(mlp_w, zh, 1 - zl, x), slot(mlp_w, zh, 1 - zl, x), "x")
+
     mixed[...] = x_ref[...].astype(jnp.float32) + gather.total()
     mixed_sum = mixed[...]
     rms_two = lax.rsqrt(jnp.mean(mixed_sum * mixed_sum, axis=-1, keepdims=True) + epsilon)
     own_two[...] = (mixed_sum * rms_two * gains[1:2, :]).astype(jnp.bfloat16)
     two_spread = Spread(wires, own_two, hidden_two)
     two_spread.start()
-    cot_spread.pass_on()
-    mlp_own_high.wait_recv()
-    mlp_high_x = wires.push(slot(mlp_w, 1 - zh, zl, x), slot(mlp_w, 1 - zh, zl, x), "x")
-    cot_spread.last()
-    two_spread.pass_on()
-    two_spread.last()
+    cot_spread.start(keep=False)
     down_high.wait_recv()
-    down_both_x = wires.push(deep_slot(1 - zh, x), deep_slot(1 - zh, x), "x")
+    down_both_x = push(deep_slot(1 - zh, x), deep_slot(1 - zh, x), "x")
+    two_spread.pass_low()
+    two_spread.pass_y()
+    two_spread.pass_both()
+    cot_spread.pass_low()
+    cot_spread.pass_y()
+    cot_spread.pass_both()
     mlp_low_high.wait_recv()
-    mlp_both_x = wires.push(slot(mlp_w, 1 - zh, 1 - zl, x), slot(mlp_w, 1 - zh, 1 - zl, x), "x")
-    for copy in (mlp_own_x, mlp_low_x, mlp_high_x, mlp_both_x, down_x, down_both_x):
+    mlp_both_x = push(slot(mlp_w, 1 - zh, 1 - zl, x), slot(mlp_w, 1 - zh, 1 - zl, x), "x")
+    two_spread.end()
+    cot_spread.end()
+    for copy in (mlp_own_x, mlp_low_x, mlp_high_x, down_x, down_both_x, mlp_both_x):
         copy.wait_recv()
-    cot_spread.end()
-    two_spread.end()
     gather.finish()
 
     @pl.when(on_side)
@@ -515,19 +576,21 @@
     wires.finish()
 
 
-FORWARD_COPIES = 60
-
-
-def forward(x_rows, gain_rows, attn_pack, mlp_pack, down_piece, out_piece, cotangent, tables):
+FORWARD_COPIES = 64
+
+
+def forward(x_rows, gain_rows, attention, mlp, out_piece, cotangent, tables):
     length, width = x_rows.shape
     group = SQUARE_DEVICES
-    rows, wide = attn_pack.shape[1:]
-    heads_wide = wide - 2 * HD
-    deep = down_piece.shape[0]
+    rows = attention[0].shape[0]
+    heads_wide = width // group
+    wide = heads_wide + 2 * HD
+    deep = mlp[2].shape[0] // 4
+    mlp_wide = 2 * PAIR * PAIR * deep
     bf16, f32 = jnp.bfloat16, jnp.float32
     shapes = [
         ((width, wide), bf16, True),
-        ((width, mlp_pack.shape[2]), bf16, False),
+        ((width, mlp_wide), bf16, False),
         ((PAIR * PAIR * deep, width), bf16, False),
         ((heads_wide, width), bf16, True),
         ((8, width), f32, True),
@@ -543,51 +606,26 @@
     return pl.pallas_call(
         forward_kernel,
         out_shape=[jax.ShapeDtypeStruct(shape, kind) for shape, kind, _ in shapes],
-        in_specs=[vmem] * 9,
+        in_specs=[vmem] * 7 + [far] * 5,
         out_specs=[vmem if near else far for _, _, near in shapes],
         scratch_shapes=[
-            pltpu.VMEM((8, 8, rows), f32),
+            pltpu.VMEM((group, 8, rows), f32),
             pltpu.VMEM((length, width), bf16),
             pltpu.VMEM((length, width), bf16),
+            pltpu.VMEM((PAIR, rows, wide), bf16),
+            pltpu.VMEM((PAIR, rows, mlp_wide), bf16),
+            pltpu.VMEM(mlp[0].shape, bf16),
+            pltpu.VMEM(mlp[1].shape, bf16),
             pltpu.SemaphoreType.DMA((FORWARD_COPIES,)),
             pltpu.SemaphoreType.DMA((FORWARD_COPIES,)),
-            pltpu.SemaphoreType.DMA((8,)),
+            pltpu.SemaphoreType.DMA((10,)),
         ]
         + gather_scratch(length, width),
         compiler_params=pltpu.CompilerParams(
             collective_id=0, has_side_effects=True, vmem_limit_bytes=60 * 2**20
         ),
         name="forward",
-    )(x_rows, gain_rows, attn_pack, mlp_pack, down_piece, out_piece, cotangent, *tables)
-
-
-def spread_kernel(own, whole, send, recv, local):
-    near = neighbours()
-    meet(near, SQUARE)
-    wires = Wires(near, send, recv, local)
-    spread = Spread(wires, own, whole)
-    spread.start()
-    spread.pass_on()
-    spread.last()
-    spread.end()
-    wires.finish()
-
-
-def spread_rows(rows, call):
-    length, width = rows.shape
-    return pl.pallas_call(
-        spread_kernel,
-        out_shape=jax.ShapeDtypeStruct((SQUARE_DEVICES * length, width), rows.dtype),
-        in_specs=[pl.BlockSpec(memory_space=pltpu.VMEM)],
-        out_specs=pl.BlockSpec(memory_space=pl.ANY),
-        scratch_shapes=[
-            pltpu.SemaphoreType.DMA((SPREAD_COPIES,)),
-            pltpu.SemaphoreType.DMA((SPREAD_COPIES,)),
-            pltpu.SemaphoreType.DMA((1,)),
-        ],
-        compiler_params=pltpu.CompilerParams(collective_id=call, has_side_effects=True),
-        name="spread",
-    )(rows)
+    )(x_rows, gain_rows, *attention, *tables, *mlp, out_piece, cotangent)
 
 
 def gather_kernel(partial, result, *scratch):
@@ -595,14 +633,7 @@
     meet(near, SQUARE)
     gather = Gather(near, scratch, partial)
     length = result.shape[0]
-
-    def block(step, _):
-        at = pl.multiple_of(gather.slot(step) * length, length)
-        gather.put(step, lambda columns: partial[pl.ds(at, length), columns].astype(jnp.float32))
-        return 0
-
-    for first in (6, 2, 4, 0):
-        lax.fori_loop(first, first + 2, block, 0)
+    gather.run(lambda start, columns: partial[pl.ds(start, length), columns].astype(jnp.float32))
     result[...] = gather.total()
     gather.finish()
 
@@ -673,13 +704,7 @@
 
     gather = Gather(near, (mine, out_core, in_core, out_far, in_far, sems_two), partial)
 
-    def block(step, _):
-        at = pl.multiple_of(gather.slot(step) * length, length)
-        gather.put(step, lambda columns: partial[pl.ds(at, length), columns].astype(float32))
-        return 0
-
-    for first in (6, 2, 4, 0):
-        lax.fori_loop(first, first + 2, block, 0)
+    gather.run(lambda start, columns: partial[pl.ds(start, length), columns].astype(float32))
     grad_hidden = gather.total()
     mixed_sum = mixed[...]
     rms_two = lax.rsqrt(jnp.mean(mixed_sum * mixed_sum, axis=-1, keepdims=True) + epsilon)
@@ -700,7 +725,7 @@
     scale = HD ** (-0.5)
 
     def sequence(step, _):
-        at = pl.multiple_of(gather.slot(step) * length, length)
+        at = pl.multiple_of(sequence_order(step) * length, length)
         here = pl.ds(at, length)
         grad_out = contract_last(grad_mixed[here, :], out_w[...]).astype(bf16)
         turned = qkv[here, :]
@@ -721,22 +746,28 @@
         grads = jnp.concatenate(grads + [grad_key, grad_value], axis=1)
         grads = turn(grads, cos_ref[...], -sin_ref[...]).astype(bf16)
         grad_attn[here, :] = grads
-        gather.put(step, lambda columns: contract_last(grads, attn_w[columns, :]))
         return 0
 
+    spread.pass_low()
+    spread.pass_y()
     spread.core.wait_recv()
     lax.fori_loop(0, 2, sequence, 0)
-    spread.pass_on()
     mlp_high_copies.append(to_high(1, zl))
     spread.core_low.wait_recv()
     lax.fori_loop(2, 4, sequence, 0)
-    spread.last()
+    spread.pass_both()
+    spread.core_y.wait_recv()
+    lax.fori_loop(4, 6, sequence, 0)
     down_x_copies[0].wait_recv()
     add_into(down_x.at[0], deep_slot(1 - zh, x))
     down_high_copy = push(down_x.at[0], down_high, "high")
-    spread.core_y.wait_recv()
     spread.core_both.wait_recv()
-    lax.fori_loop(4, 8, sequence, 0)
+    lax.fori_loop(6, 8, sequence, 0)
+    gather.run(
+        lambda start, columns: contract_last(
+            grad_attn[pl.ds(start, length), :], attn_w[columns, :]
+        )
+    )
 
     def own_columns(at, _):
         here = pl.ds(pl.multiple_of(at * rows, rows), rows)
@@ -801,6 +832,19 @@
     input_grad[...] = input_grad[...] + norm_back(grad_hidden * gains[0:1, :], x_float, rms_one)
     gain_grads[2:8, :] = jnp.zeros((6, width), float32)
 
+    directions = ("core", "y", "low", "x", "high")
+    steps = []
+
+    def total_step(at):
+        if steps:
+            steps[-1].wait()
+            wires.sent = [copy for copy in wires.sent if copy is not steps[-1]]
+            gain_grads[...] = gain_grads[...] + gain_in[at - 1]
+        if at < len(directions):
+            steps.append(push(gain_grads, gain_in.at[at], directions[at]))
+
+    total_step(0)
+
     attn_high_copies = []
     for lower, low in ((0, 1 - zl), (1, zl)):
         attn_x_copies[0, lower].wait_recv()
@@ -820,20 +864,19 @@
         mlp_x_copies[1, 1], mlp_x.at[3], slot(mlp_local, zh, zl, x),
         mlp_high_copies[1], mlp_high.at[1], mlp_out, column_own, rows,
     )
-    for at, name in enumerate(("x", "high", "low", "y", "core")):
-        copy = push(gain_grads, gain_in.at[at], name)
-        copy.wait()
-        wires.sent.pop()
-        gain_grads[...] = gain_grads[...] + gain_in[at]
+    total_step(1)
     mlp_low.wait_recv()
     mlp_third = to_group(mlp_out, rows, column_low, None)
+    total_step(2)
     down_second = finish_second(
         down_x_copies[1], down_x.at[1], deep_slot(zh, x),
         down_high_copy, down_high, down_out, r, deep,
     )
+    total_step(3)
     mlp_second[0].wait_recv()
     here = entry(mlp_out, across * PAIR + zl, rows)
     last = [push(here, here, "core")]
+    total_step(4)
     mlp_third[0].wait_recv()
     here = entry(mlp_out, across * PAIR + 1 - zl, rows)
     last.append(push(here, here, "core"))
@@ -870,6 +913,7 @@
         out_y_copy.start()
         out_keep.start()
 
+    total_step(5)
     attn_low.wait_recv()
     attn_third = to_group(attn_out, rows, column_low, None)
     down_second[0].wait_recv()
@@ -974,6 +1018,81 @@
     )
 
 
+def arrange_kernel(mlp, attn, down, out, gate_grad, up_grad, query_grad, key_grad, value_grad, down_grad, out_grad):
+    float32 = jnp.float32
+    down_grad[...] = down[...].astype(float32)
+    out_grad[...] = out[...].astype(float32)
+    columns, _, mlp_wide = mlp.shape
+    reps = columns // PAIR
+    heads_wide = attn.shape[2] - 2 * HD
+    piece = mlp_wide // (2 * PAIR * PAIR)
+    for high in range(PAIR):
+        for low in range(PAIR):
+            for side in range(PAIR):
+                shard, holder = shard_of(high, low, side), high * PAIR + side
+                for base, target in ((0, gate_grad), (mlp_wide // 2, up_grad)):
+                    at = base + holder * piece
+                    parts = [mlp[rep * PAIR + low, :, at : at + piece] for rep in range(reps)]
+                    joined = jnp.concatenate(parts, axis=1).astype(float32)
+                    target[:, shard * reps * piece : (shard + 1) * reps * piece] = joined
+                query_grad[:, shard * heads_wide : (shard + 1) * heads_wide] = attn[
+                    holder * PAIR + low, :, :heads_wide
+                ].astype(float32)
+    for at, target in ((heads_wide, key_grad), (heads_wide + HD, value_grad)):
+        heads = []
+        for high in range(PAIR):
+            for low in range(PAIR):
+                first, second = high * PAIR * PAIR + low, (high * PAIR + 1) * PAIR + low
+                heads.append(
+                    attn[first, :, at : at + HD].astype(float32)
+                    + attn[second, :, at : at + HD].astype(float32)
+                )
+        target[...] = jnp.concatenate(heads, axis=1)
+
+
+def arrange(mlp, attn, down, out):
+    columns, rows, _ = mlp.shape
+    steps = 8
+    block = rows // steps
+    width = out.shape[1]
+    reps = columns // PAIR
+    f32 = jnp.float32
+
+    def split(rows_in, wide):
+        return pl.BlockSpec((rows_in // steps, wide), lambda i: (i, 0))
+
+    def deep(values):
+        return pl.BlockSpec((columns, block, values.shape[2]), lambda i: (0, i, 0))
+
+    mlp_columns = mlp.shape[2] // 2 * columns
+    shapes = [
+        (rows, mlp_columns), (rows, mlp_columns), (rows, width), (rows, KV * HD), (rows, KV * HD),
+        (down.shape[0], width), (out.shape[0], width),
+    ]
+    return pl.pallas_call(
+        arrange_kernel,
+        grid=(steps,),
+        out_shape=[jax.ShapeDtypeStruct(shape, f32) for shape in shapes],
+        in_specs=[deep(mlp), deep(attn), split(down.shape[0], width), split(out.shape[0], width)],
+        out_specs=[split(*shape) for shape in shapes],
+        compiler_params=pltpu.CompilerParams(vmem_limit_bytes=40 * 2**20),
+        name="arrange",
+    )(mlp, attn, down, out)
+
+
+def rotary_numbers(length, wide):
+    positions = np.arange(length, dtype=np.float32)[:, None]
+    spacing = np.arange(HD // 2, dtype=np.float32) * np.float32(-2.0 * math.log(10000.0) / HD)
+    angles = positions * np.exp(spacing)[None, :]
+    cos_half, sin_half = np.cos(angles), np.sin(angles)
+    turned = wide // HD - 1
+    cos_one = np.concatenate([cos_half, cos_half], axis=1)
+    sin_one = np.concatenate([-sin_half, sin_half], axis=1)
+    cos_wide = np.concatenate([cos_one] * turned + [np.ones_like(cos_one)], axis=1)
+    sin_wide = np.concatenate([sin_one] * turned + [np.zeros_like(sin_one)], axis=1)
+    return jnp.asarray(cos_wide, jnp.float32), jnp.asarray(sin_wide, jnp.float32)
+
+
 def per_device(
     block_input,
     cotangent,
@@ -1209,76 +1328,26 @@
     down_weight,
 ):
     length, width = block_input.shape
-    reps, xs = lax.axis_size("rep"), lax.axis_size("x")
-    high = lax.axis_size("zh")
-    holders = high * xs
-    group = reps * PAIR
-    r, zl, x = lax.axis_index("rep"), lax.axis_index("zl"), lax.axis_index("x")
-    shard = (lax.axis_index("zh") * PAIR + zl) * xs + x
     rows = query_weight.shape[0]
-    heads_wide = query_weight.shape[1] // group
-    per_rep = holders // reps
-    hidden_piece = down_weight.shape[0] // reps
-    hidden_wide = holders * hidden_piece
-    heads = heads_wide // HD
-    scale_factor = HD ** (-0.5)
-
-    def own_rep(values, axis):
-        return lax.dynamic_index_in_dim(values, r, axis, keepdims=False)
-
-    def by_holder(values, axis):
-        shape = values.shape
-        cut = values.reshape(shape[:axis] + (high, PAIR, xs, -1) + shape[axis + 1 :])
-        cut = jnp.moveaxis(cut, axis + 1, 0)
-        return cut.reshape((PAIR,) + shape[:axis] + (holders, -1) + shape[axis + 1 :])
-
-    def query_columns(weight):
-        pieces = by_holder(weight, 1).reshape(PAIR, rows, reps, heads_wide)
-        return own_rep(pieces, 2)
-
-    def hidden_columns(weight):
-        pieces = by_holder(weight, 1).reshape(PAIR, rows, holders, reps, hidden_piece)
-        return own_rep(pieces, 3).reshape(PAIR, rows, hidden_wide)
-
-    key_heads = [
-        (((r * per_rep // xs) * PAIR + low) * xs * heads_wide // (per_rep * HD)) * KV
-        // (query_weight.shape[1] // HD)
-        for low in range(PAIR)
-    ]
-
-    def key_columns(weight):
-        pieces = weight.reshape(rows, KV, HD)
-        return jnp.stack(
-            [lax.dynamic_index_in_dim(pieces, k, 1, keepdims=False) for k in key_heads]
-        )
-
-    attn_pack = jnp.concatenate(
-        [query_columns(query_weight), key_columns(key_weight), key_columns(value_weight)], axis=2
-    )
-    mlp_pack = jnp.concatenate([hidden_columns(gate_weight), hidden_columns(up_weight)], axis=2)
-
-    cos_table, sin_table = rotary_tables(length, HD)
-    sign = jnp.where(jnp.arange(HD) < HD // 2, -1.0, 1.0)
-    turned = heads + 1
-    cos_wide = jnp.concatenate([jnp.tile(cos_table, (1, turned)), jnp.ones_like(cos_table)], axis=1)
-    sin_wide = jnp.concatenate(
-        [jnp.tile(sin_table * sign, (1, turned)), jnp.zeros_like(cos_table)], axis=1
-    )
-    gain_rows = jnp.zeros((8, rows), jnp.float32)
-    gain_rows = gain_rows.at[0].set(attn_gain.astype(jnp.float32))
-    gain_rows = gain_rows.at[1].set(mlp_gain.astype(jnp.float32))
+    zl, x = lax.axis_index("zl"), lax.axis_index("x")
+    shard = shard_of(lax.axis_index("zh"), zl, x)
+    tables = rotary_numbers(length, width // SQUARE_DEVICES + 2 * HD)
+    gain_rows = jnp.concatenate(
+        [jnp.stack([attn_gain, mlp_gain]).astype(jnp.float32), jnp.zeros((6, rows), jnp.float32)]
+    )
     (
         attn_w, mlp_w, down_w, out_w, gains, hidden_one, cot_all, qkv, attended, mixed_sum, hidden_two,
     ) = forward(
         block_input,
         gain_rows,
-        attn_pack,
-        mlp_pack,
-        own_rep(down_weight.reshape(reps, hidden_piece, width), 0),
+        (query_weight, key_weight, value_weight),
+        (gate_weight, up_weight, down_weight),
         out_weight,
         cotangent,
-        (cos_wide, sin_wide),
-    )
+        tables,
+    )
+
+    hidden_wide = down_w.shape[0]
     gate_up = matmul(hidden_two, mlp_w)
     gate_raw, up_raw = gate_up[:, :hidden_wide], gate_up[:, hidden_wide:]
     sigmoid = jax.nn.sigmoid(gate_raw)
@@ -1289,7 +1358,8 @@
     grad_up = grad_product * activated
     grad_both = jnp.concatenate([grad_gate, grad_up], axis=1).astype(jnp.bfloat16)
     hidden_partial = contract_last(grad_both, mlp_w).astype(jnp.bfloat16)
-    block_output = (mixed_sum + gather_rows(matmul(product, down_w).astype(jnp.bfloat16), 2)).astype(jnp.bfloat16)
+    down_sum = gather_rows(matmul(product, down_w).astype(jnp.bfloat16), 2)
+    block_output = (mixed_sum + down_sum).astype(jnp.bfloat16)
     down_local = contract_first(product, cot_all).astype(jnp.bfloat16)
     mlp_local = contract_first(hidden_two, grad_both).astype(jnp.bfloat16)
 
@@ -1300,34 +1370,14 @@
         (hidden_one, attn_w, out_w, qkv, attended, mixed_sum, gains),
         block_input,
         cotangent,
-        (cos_wide, sin_wide),
-    )
-
-    def from_holder(values):
-        cut = values.reshape(PAIR, rows, high, xs, -1)
-        return cut.transpose(1, 2, 0, 3, 4).reshape(rows, -1)
-
-    down_grad = down_grad.astype(jnp.float32)
-    out_grad = out_grad.astype(jnp.float32)
-    mlp_grad = mlp_grad.astype(jnp.float32).reshape(reps, PAIR, rows, 2, holders, hidden_piece)
-    mlp_grad = mlp_grad.transpose(3, 1, 2, 4, 0, 5)
-    gate_grad, up_grad = from_holder(mlp_grad[0]), from_holder(mlp_grad[1])
-    attn_grad = attn_grad.astype(jnp.float32).reshape(reps, PAIR, rows, -1)
-    query_grad = attn_grad[..., :heads_wide].transpose(1, 2, 0, 3)
-    query_grad = from_holder(query_grad.reshape(PAIR, rows, holders, -1))
-    key_value = attn_grad[..., heads_wide:]
-
-    def key_back(values):
-        total = jnp.zeros((KV, rows, HD), jnp.float32)
-        for rep in range(reps):
-            for low in range(PAIR):
-                head = (rep * per_rep // xs) * PAIR + low
-                head = head * xs * heads_wide // (per_rep * HD)
-                head = head * KV // (query_weight.shape[1] // HD)
-                total = total.at[head].add(values[rep, low])
-        return total.transpose(1, 0, 2).reshape(rows, -1)
-
-    key_grad, value_grad = key_back(key_value[..., :HD]), key_back(key_value[..., HD:])
+        tables,
+    )
+    gate_grad, up_grad, query_grad, key_grad, value_grad, down_grad, out_grad = arrange(
+        mlp_grad.reshape(SQUARE_DEVICES, rows, -1),
+        attn_grad.reshape(SQUARE_DEVICES, rows, -1),
+        down_grad,
+        out_grad,
+    )
     gain_grads = lax.dynamic_slice_in_dim(gain_grads, shard * rows, rows, axis=1)
     return (
         block_output,

time: 691 us -> 519 us (0.75)
  local copies, waits for them, and re-layouts: 96 us -> 10.8 us
  Pallas kernels: 537 us -> 457 us
  other arithmetic: 9.23 us -> 1.52 us
    pallas_call x1, Pallas kernels: 262 us -> 192 us  [forward(): pl.pallas_call(forward_kernel, out_shape=[jax.ShapeDtypeStruct(shape, kin...]
    transpose x7 -> x0, local copies, waits for them, and re-layouts: 33.3 us -> none  [the longest x2 24.8 us: per_device_square(): mlp_grad = mlp_grad.transpose(3, 1, 2, 4, 0, 5)]
    pallas_call x1, Pallas kernels: 246 us -> 225 us  [backward(): pl.pallas_call(backward_kernel, out_shape=[jax.ShapeDtypeStruct(shape, ki...]
    unnamed x45 -> x23, local copies, waits for them, and re-layouts: 27 us -> 8.07 us
    slice x5 -> x0, local copies, waits for them, and re-layouts: 18.6 us -> none  [the longest x3 16.3 us: per_device_square(): gate_grad, up_grad = (from_holder(mlp_grad[0]), from_holder(mlp_grad[1]))]
    pallas_call x0 -> x1, Pallas kernels: none -> 10.7 us  [arrange(): pl.pallas_call(arrange_kernel, grid=(steps,), out_shape=[jax.ShapeDtypeSt...]
    reshape x5 -> x0, local copies, waits for them, and re-layouts: 9.54 us -> none  [the longest x1 4.23 us: from_holder(): return cut.transpose(1, 2, 0, 3, 4).reshape(rows, -1)]
where the time goes in v5:
time: 519 us; the launch traced here: 511 us
  Pallas kernels  457 us (88%)
  matrix products  40.2 us (8%)
  local copies, waits for them, and re-layouts  10.8 us (2%)
    pallas_call x1, Pallas kernels, backward(): pl.pallas_call(backward_kernel, out_shape=[jax.ShapeDtypeStruct(shape, ki...  225 us
    pallas_call x1, Pallas kernels, forward(): pl.pallas_call(forward_kernel, out_shape=[jax.ShapeDtypeStruct(shape, kin...  192 us
    pallas_call x1, Pallas kernels, gather_rows(): pl.pallas_call(gather_kernel, out_shape=jax.ShapeDtypeStruct((length, wid...  30 us
    dot_general x2, matrix products, matmul(): return jnp.dot(left, right, preferred_element_type=jnp.float32)  14.4 us
    dot_general x2, matrix products, contract_first(): lax.dot_general(left, right, (((0,), (0,)), ((), ())), preferred_element_...  13.4 us
    dot_general x2, matrix products, contract_last(): lax.dot_general(left, right, (((1,), (1,)), ((), ())), preferred_element_...  12.4 us
    pallas_call x1, Pallas kernels, arrange(): pl.pallas_call(arrange_kernel, grid=(steps,), out_shape=[jax.ShapeDtypeSt...  10.7 us

profile of v5, /device:TPU:1, one launch (start us, length us, event | category | flops | bytes accessed | tf_op | source)
XLA Modules:
  0.0 511.2 jit_solution(12228766445814040764)
XLA Ops:
  0.6 0.7 stack.10
  1.3 0.7 stack.9
  2.0 0.6 fusion.4.gain_ref
  2.6 191.7 %forward.1 = (bf16[2048,384]{1,0:T(8,128)(2,1)}, bf16[2048,1408]{1,0:T(8,128)(2,1)}, bf16[704,2048]{1,0:T(8,128)(2,1)}, bf16[256,2048]{1,0:T(8,128)(2,1)}, f32[8...) custom-call(bf16[128,2048]{1,0:T(8,128)(2,1)} %x_ref.3, ...), custom_call_target="tpu_custom_call" | custom-call | tf_op jit(solution)/shard_map/forward/pallas_call | solution.py:606
  194.2 0.0 copy-start.6
  194.2 0.0 copy-start.8
  194.2 0.0 slice-start
  194.3 10.7 %fusion.8 = f32[1024,1408]{1,0:T(8,128)S(1)} fusion(bf16[1024,2048]{1,0:T(8,128)(2,1)} %get-tuple-element.36, bf16[2048,1408]{1,0:T(8,128)(2,1)} %get-tuple-element.37), kind=kOutput, calls=%fused_computation.20 | convolution fusion | flops 5905580032 | bytes 15728640 | tf_op jit(solution)/shard_map/dot_general | solution.py:51
  205.0 0.0 copy-done.6
  205.0 0.0 copy-done.8
  205.0 0.0 slice-start.1
  205.0 4.2 multiply_convert_fusion.1
  209.2 3.6 convolution_convert_fusion.2.partial
  212.9 0.0 copy-start.4
  212.9 30.0 %gather.1 = f32[128,2048]{1,0:T(8,128)S(1)} custom-call(bf16[1024,2048]{1,0:T(8,128)(2,1)S(1)} %convolution_convert_fusion.2.partial), custom_call_target="tpu_custom_call" | custom-call | tf_op jit(solution)/shard_map/gather/pallas_call | solution.py:644
  242.9 0.0 copy-done.4
  242.9 0.9 add_convert_fusion
  243.8 0.0 slice-done
  243.8 0.0 slice-done.1
  243.8 0.0 copy-start.7
  243.8 8.3 %convolution_convert_fusion.1.partial = bf16[1024,2048]{1,0:T(8,128)(2,1)} fusion(bf16[2048,1408]{1,0:T(8,128)(2,1)S(1)} %bitcast.19, bf16[1024,704]{1,0:T(8,128)(2,1)S(1)} %get-tuple-element.60, bf16[1024,704]{1,0:T(8,128)(2,1)S(1)} %get-tuple-element.59), kind=kOutput, calls=%fused_computation.1 | convolution fusion | flops 5913444352 | bytes 12845056 | tf_op jit(solution)/shard_map/dot_general | solution.py:55
  252.1 0.0 copy-done.7
  252.1 8.7 %convolution_convert_fusion.mlp_local = bf16[2048,1408]{1,0:T(8,128)(2,1)} fusion(bf16[1024,2048]{1,0:T(8,128)(2,1)S(1)} %copy-done.7, bf16[1024,704]{1,0:T(8,128)(2,1)S(1)} %get-tuple-element.60, bf16[1024,704]{1,0:T(8,128)(2,1)S(1)} %get-tuple-element.59), kind=kOutput, calls=%fused_computation | convolution fusion | flops 5914230784 | bytes 12845056 | tf_op jit(solution)/shard_map/dot_general | solution.py:61
  260.8 4.7 convolution_convert_fusion.3.down_local
  265.5 225.0 %backward.1 = (bf16[2048,1408]{1,0:T(8,128)(2,1)}, bf16[704,2048]{1,0:T(8,128)(2,1)}, bf16[2048,384]{1,0:T(8,128)(2,1)}, bf16[256,2048]{1,0:T(8,128)(2,1)}, f32[128,2048]{1,0:T(8,128)}, /*index=5*/f32[8,2048]{1,0:T(8,128)}) custom-call(bf16[1024,2048]{1,0:T(8,128)(2,1)} %convolution_convert_fusion.1.partial, ...), custom_call_target="tpu_custom_call" | custom-call | tf_op jit(solution)/shard_map/backward/pallas_call | solution.py:985
  490.5 0.0 copy-start
  490.5 2.6 copy-done
  493.1 0.0 copy-start.1
  493.1 1.8 copy-done.1
  495.0 0.0 copy-start.2
  495.0 1.4 copy-done.2
  496.4 0.0 copy-start.3
  496.4 1.2 copy-done.3
  497.6 0.0 copy-start.5
  497.6 10.7 %arrange.1 = (f32[256,5632]{1,0:T(8,128)}, f32[256,5632]{1,0:T(8,128)}, f32[256,2048]{1,0:T(8,128)}, f32[256,256]{1,0:T(8,128)}, f32[256,256]{1,0:T(8,128)}, /*index=5*/f32[704,2048]{1,0:T(8,128)}, f32[256,2048]{1,0:T(8,128)}) custom-call(bf16[8,256,1408]{2,1,0:T(8,128)(2,1)S(1)} %bitcast.14, bf16[8,256,384]{2,1,0:T(8,128)(2,1)S(1)} %bitcast.15, ...), custom_call_target="tpu_custom_call" | custom-call | tf_op jit(solution)/shard_map/arrange/pallas_call | solution.py:1072
  508.3 1.4 fusion.7
  509.7 0.0 copy-done.5
  509.7 1.0 copy.28
  (1 shorter events, 0.0 us)
Async XLA Ops:
  194.2 10.8 %copy-start.6 = (bf16[1024,2048]{1,0:T(8,128)(2,1)S(1)}, bf16[1024,2048]{1,0:T(8,128)(2,1)}, u32[]{:S(2)}) copy-start(bf16[1024,2048]{1,0:T(8,128)(2,1)} %get-tuple-element.39) | copy-start | bytes 12582916
  194.2 10.8 %copy-start.8 = (bf16[704,2048]{1,0:T(8,128)(2,1)S(1)}, bf16[704,2048]{1,0:T(8,128)(2,1)}, u32[]{:S(2)}) copy-start(bf16[704,2048]{1,0:T(8,128)(2,1)} %get-tuple-element.38) | copy-start | bytes 8650756
  194.2 49.6 %slice-start = ((s8[5767168]{0:T(1024)(128)(4,1)}), s8[4194304]{0:T(1024)(128)(4,1)S(1)}, s32[]{:S(2)}) async-start(s8[5767168]{0:T(1024)(128)(4,1)} %bitcast.18), calls=%async_computation | async-start | bytes 8388608
  205.0 38.8 %slice-start.1 = ((s8[5767168]{0:T(1024)(128)(4,1)}), s8[1572864]{0:T(1024)(128)(4,1)S(1)}, s32[]{:S(2)}) async-start(s8[5767168]{0:T(1024)(128)(4,1)} %bitcast.18), calls=%async_computation.1 | async-start | bytes 3145728
  212.9 30.0 %copy-start.4 = (f32[128,2048]{1,0:T(8,128)S(1)}, f32[128,2048]{1,0:T(8,128)}, u32[]{:S(2)}) copy-start(f32[128,2048]{1,0:T(8,128)} %get-tuple-element.35.mixed) | copy-start | bytes 3145732
  243.8 8.3 %copy-start.7 = (bf16[1024,2048]{1,0:T(8,128)(2,1)S(1)}, bf16[1024,2048]{1,0:T(8,128)(2,1)}, u32[]{:S(2)}) copy-start(bf16[1024,2048]{1,0:T(8,128)(2,1)} %get-tuple-element.36) | copy-start | bytes 12582916
  490.5 2.6 copy-start
  493.1 1.8 copy-start.1
  495.0 1.4 copy-start.2
  496.4 1.2 copy-start.3
  497.6 12.2 %copy-start.5 = (f32[128,2048]{1,0:T(8,128)S(1)}, f32[128,2048]{1,0:T(8,128)}, u32[]{:S(2)}) copy-start(f32[128,2048]{1,0:T(8,128)} %get-tuple-element.76) | copy-start | bytes 3145732
